TPU v7x, 32 devices: a whole 2x2x4 slice. The times are simulated.
32 devices in a mesh: srv: 16 (over z, y, x), grp: 2 (over core).
Axes of the slice: x: 2, y: 2, z: 4, core: 2. Of those that a mesh axis runs over, the one named last changes fastest.
Arguments:
- basis_modes: float32 [64, 64, 3072], P(None, ('srv', 'grp')), may hold values from -10 to 10
- weights: float32 [64], replicated, may hold values from 0.5 to 4
- snapshots: float32 [16, 64, 3072], P(None, 'srv', 'grp'), may hold values from -10 to 10
Outputs:
- new_modes: float32 [80, 64, 3072], P(None, ('srv', 'grp'))
- factor: float32 [80, 80], replicated
All inputs are finite; a program needn't handle non-finite values.
Results may differ from a plain program's by a relative error of at most 0.00009.
Values sent between devices are 32-bit elements; how exact they have to be, the bound alone decides.
No kernel may reach another device: no remote copies, remote signals or barrier semaphores. Data moves between devices by JAX's collectives and lax.ppermute only.
A program may use at most 64 MiB of HBM per device.

v0:
```python
import jax
import jax.numpy as jnp
from jax import lax
from jax.sharding import PartitionSpec as P

MODES = 64
SNAPS = 16


def merged_factor(local_gram):
    return jnp.linalg.cholesky(lax.psum(local_gram, ("srv", "grp")))


def per_device(basis_modes, weights, snapshots):
    width = MODES + SNAPS
    total_cells = (
        basis_modes.shape[1] * basis_modes.shape[2] * lax.axis_size("srv") * lax.axis_size("grp")
    )
    scaled = basis_modes * weights[:, None, None]
    arrived = lax.all_to_all(snapshots, "grp", split_axis=1, concat_axis=2, tiled=True)
    panel = jnp.concatenate([scaled, arrived], axis=0).reshape(width, -1)
    local_gram = (
        jnp.dot(panel, panel.T, precision=lax.Precision.HIGHEST, preferred_element_type=jnp.float32)
        / total_cells
    )
    factor = merged_factor(local_gram)
    inverse = lax.linalg.triangular_solve(
        factor, jnp.eye(width, dtype=jnp.float32), left_side=True, lower=True
    )
    result = jnp.dot(
        inverse, panel, precision=lax.Precision.HIGHEST, preferred_element_type=jnp.float32
    )
    result = result.reshape(width, basis_modes.shape[1], basis_modes.shape[2])
    return (result, factor)


def solution(mesh):
    in_specs = (P(None, ("srv", "grp"), None), P(), P(None, "srv", "grp"))
    out_specs = (P(None, ("srv", "grp"), None), P())
    return jax.shard_map(
        per_device, mesh=mesh, in_specs=in_specs, out_specs=out_specs, check_vma=False
    )
```

profile of v0, /device:TPU:0, one launch (start us, length us, event | category | flops | bytes accessed | tf_op | source)
XLA Modules:
  0.0 77.2 jit_solution(11390154502908591722)
XLA Ops:
  0.6 0.0 copy-start
  0.6 0.0 copy-start.1
  0.6 1.2 %copy.19 = f32[16,4,1536]{2,0,1:T(8,128)S(1)} copy(f32[16,4,1536]{2,1,0:T(4,128)} %param.5) | data formatting | bytes 786432 | tf_op args[2]
  1.9 4.0 %all_to_all.18 = f32[16,4,1536]{2,0,1:T(8,128)S(1)} all-to-all(f32[16,4,1536]{2,0,1:T(8,128)S(1)} %copy.19), channel_id=1, replica_groups=mesh['srv'=16,'grp'=2] {'grp'}, dimensions={1} | all-to-all | bytes 786432 | tf_op jit(solution)/shard_map/all_to_all | solution.py:20
  5.9 1.1 %copy.41 = f32[16,2,2,1536]{3,1,0,2:T(2,128)} copy(f32[16,2,2,1536]{3,0,2,1:T(8,128)S(1)} %bitcast.35) | data formatting | bytes 786432 | tf_op jit(solution)/shard_map/all_to_all | solution.py:20
  7.0 0.3 copy.42
  7.3 0.0 copy-done
  7.3 0.0 copy-done.1
  7.3 0.5 copy_multiply_fusion
  7.8 0.5 fusion.17
  8.4 2.1 %all_to_all.16 = f32[16,2,3072]{2,0,1:T(8,128)} reshape(f32[16,2,2,1536]{3,2,0,1:T(2,128)} %bitcast.38) | data formatting | bytes 786432 | tf_op jit(solution)/shard_map/all_to_all | solution.py:20
  10.4 3.4 %fusion.10 = f32[80,80]{0,1:T(8,128)} fusion(f32[16,2,3072]{2,0,1:T(8,128)} %all_to_all.16, f32[64,2,3072]{2,0,1:T(8,128)S(1)} %copy_multiply_fusion), kind=kOutput, calls=%fused_computation.11 | convolution fusion | flops 472357120 | bytes 1991680 | tf_op jit(solution)/shard_map/dot_general | solution.py:23
  13.9 42.4 %psum.7 = f32[80,80]{0,1:T(8,128)S(1)} all-reduce(f32[80,80]{0,1:T(8,128)} %fusion.10), channel_id=1, replica_groups=mesh['srv'=16,'grp'=2] {'srv','grp'}, use_global_device_ids=true, to_apply=%region_0.0 | all-reduce | flops 6400 | bytes 51200 | tf_op jit(solution)/shard_map/psum | solution.py:11
  56.2 0.1 copy.23
  56.3 7.3 %cholesky.17 = f32[80,80]{1,0:T(8,128)S(1)} custom-call(f32[80,80]{1,0:T(8,128)S(1)} %fusion.14), custom_call_target="Cholesky" | custom-call | tf_op jit(solution)/shard_map/jit(cholesky)/cholesky | solution.py:11
  63.7 0.6 compare_reduce_fusion
  64.3 1.3 %select_bitcast_fusion = (f32[1,80,80]{2,1,0:T(8,128)S(1)}, f32[80,80]{1,0:T(8,128)}) fusion(f32[80,80]{1,0:T(8,128)S(1)} %cholesky.17, pred[]{:T(512)} %compare_reduce_fusion), kind=kLoop, calls=%fused_computation.17 | loop fusion | flops 25600 | bytes 76801 | tf_op jit(solution)/shard_map/triangular_solve | solution.py:27
  65.6 6.1 %custom-call.6 = f32[1,80,80]{1,2,0:T(8,128)S(1)} custom-call(f32[1,80,80]{2,1,0:T(8,128)S(1)} %get-tuple-element.8), custom_call_target="InvertDiagBlocksLowerTriangular" | custom-call | tf_op jit(solution)/shard_map/triangular_solve | solution.py:27
  71.7 0.2 convolution_bitcast_fusion
  72.0 0.3 concatenate.12
  72.3 0.1 copy.31
  72.4 0.1 pad_maximum_fusion
  72.6 1.8 %fusion = f32[80,2,3072]{2,0,1:T(8,128)S(1)} fusion(f32[80,80,1]{1,0,2:T(8,128)S(1)} %convolution_bitcast_fusion, f32[10,2,8,3072]{3,2,1,0:T(8,128)S(1)} %bitcast.33), kind=kOutput, calls=%fused_computation | convolution fusion | flops 471859200 | bytes 3957760 | tf_op jit(solution)/shard_map/dot_general | solution.py:30
  74.4 2.8 %copy.26 = f32[80,2,3072]{2,1,0:T(2,128)} copy(f32[80,2,3072]{2,0,1:T(8,128)S(1)} %fusion) | data formatting | bytes 3932160
  (2 shorter events, 0.0 us)
Async XLA Ops:
  0.6 6.7 %copy-start = (f32[64,2,3072]{2,1,0:T(2,128)S(1)}, f32[64,2,3072]{2,1,0:T(2,128)}, u32[]{:S(2)}) copy-start(f32[64,2,3072]{2,1,0:T(2,128)} %param.3) | copy-start | bytes 4718596
  0.6 6.7 %copy-start.1 = (f32[64]{0:T(128)S(1)}, f32[64]{0:T(128)}, u32[]{:S(2)}) copy-start(f32[64]{0:T(128)} %param.4) | copy-start | bytes 772
where the time goes:
time: 77.6 us; the launch traced here: 77.2 us
  blocking collectives  46.4 us (60%)
  other arithmetic  16.6 us (21%)
  local copies, waits for them, and re-layouts  7.98 us (10%)
  matrix products  5.45 us (7%)
    psum x1, blocking collectives, merged_factor(): return jnp.linalg.cholesky(lax.psum(local_gram, ('srv', 'grp')))  42.4 us
    another operation x3, other arithmetic, merged_factor(): return jnp.linalg.cholesky(lax.psum(local_gram, ('srv', 'grp')))  7.98 us
    another operation x2, other arithmetic, per_device(): lax.linalg.triangular_solve(factor, jnp.eye(width, dtype=jnp.float32), le...  7.4 us
    all_to_all x1, blocking collectives, per_device(): lax.all_to_all(snapshots, 'grp', split_axis=1, concat_axis=2, tiled=True)  4.05 us
    unnamed x6, local copies, waits for them, and re-layouts  4.04 us
    all_to_all x3, local copies, waits for them, and re-layouts, per_device(): lax.all_to_all(snapshots, 'grp', split_axis=1, concat_axis=2, tiled=True)  3.43 us
    dot_general x1, matrix products, per_device(): jnp.dot(panel, panel.T, precision=lax.Precision.HIGHEST, preferred_elemen...  3.41 us
    dot_general x1, matrix products, per_device(): jnp.dot(inverse, panel, precision=lax.Precision.HIGHEST, preferred_elemen...  1.82 us

commit v1 on v0

--- a/solution.py
+++ b/solution.py
@@ -7,8 +7,22 @@
 SNAPS = 16
 
 
+AXES = ("srv", "grp")
+
+
+def total(value):
+    servers, cores = lax.axis_size("srv"), lax.axis_size("grp")
+    if servers & (servers - 1) or cores != 2:
+        return lax.psum(value, AXES)
+    count = servers * cores
+    masks = [1] + [2 * bit + 1 for bit in (1 << p for p in range(servers.bit_length() - 1))]
+    for mask in masks:
+        value = value + lax.ppermute(value, AXES, [(i, i ^ mask) for i in range(count)])
+    return value
+
+
 def merged_factor(local_gram):
-    return jnp.linalg.cholesky(lax.psum(local_gram, ("srv", "grp")))
+    return jnp.linalg.cholesky(total(local_gram))
 
 
 def per_device(basis_modes, weights, snapshots):

time: 77.6 us -> 48.8 us (0.63)
  blocking collectives: 46.4 us -> 4.05 us
  starting transfers between devices: 0 us -> 9.54 us
  waiting for transfers between devices: 0 us -> 6.7 us
  local copies, waits for them, and re-layouts: 7.98 us -> 5.51 us
  matrix products: 5.45 us -> 3.72 us
  other arithmetic: 16.6 us -> 18 us
    psum x1 -> x0, blocking collectives: 42.4 us -> none  [merged_factor(): return jnp.linalg.cholesky(lax.psum(local_gram, ('srv', 'grp')))]
    ppermute x0 -> x5, starting transfers between devices: none -> 9.54 us  [total(): lax.ppermute(value, AXES, [(i, i ^ mask) for i in range(count)])]
    ppermute x0 -> x5, waiting for transfers between devices: none -> 6.7 us  [total(): lax.ppermute(value, AXES, [(i, i ^ mask) for i in range(count)])]
    all_to_all x3, local copies, waits for them, and re-layouts: 3.43 us -> 0.95 us  [per_device(): lax.all_to_all(snapshots, 'grp', split_axis=1, concat_axis=2, tiled=True)]
    dot_general x1, matrix products: 3.41 us -> 1.69 us  [per_device(): jnp.dot(panel, panel.T, precision=lax.Precision.HIGHEST, preferred_elemen...]
    add x0 -> x5, other arithmetic: none -> 1.45 us  [total(): value + lax.ppermute(value, AXES, [(i, i ^ mask) for i in range(count)])]
  transfers between devices with their start and end apart: 0 -> 5, of which waited for: 0 -> 5; matrix products, arithmetic and copies ran while one was open for 0% -> 3% of each run, Pallas kernels for 0% -> 0%
where the time goes in v1:
time: 48.8 us; the launch traced here: 48.3 us
  other arithmetic  18 us (37%)
  starting transfers between devices  9.54 us (20%)
  waiting for transfers between devices  6.7 us (14%)
  local copies, waits for them, and re-layouts  5.51 us (11%)
  blocking collectives  4.05 us (8%)
  matrix products  3.72 us (8%)
  between operations  0.77 us (2%)
    ppermute x5, starting transfers between devices, total(): lax.ppermute(value, AXES, [(i, i ^ mask) for i in range(count)])  9.54 us
    another operation x3, other arithmetic, merged_factor(): return jnp.linalg.cholesky(total(local_gram))  7.98 us
    another operation x2, other arithmetic, per_device(): lax.linalg.triangular_solve(factor, jnp.eye(width, dtype=jnp.float32), le...  7.4 us
    ppermute x5, waiting for transfers between devices, total(): lax.ppermute(value, AXES, [(i, i ^ mask) for i in range(count)])  6.7 us
    all_to_all x1, blocking collectives, per_device(): lax.all_to_all(snapshots, 'grp', split_axis=1, concat_axis=2, tiled=True)  4.05 us
    unnamed x6, local copies, waits for them, and re-layouts  4.04 us
    dot_general x1, matrix products, per_device(): jnp.dot(inverse, panel, precision=lax.Precision.HIGHEST, preferred_elemen...  1.81 us
    dot_general x1, matrix products, per_device(): jnp.dot(panel, panel.T, precision=lax.Precision.HIGHEST, preferred_elemen...  1.69 us
  transfers between devices with their start and end apart: 5, of which 5 were waited for; matrix products, arithmetic and copies ran while one was open for 3% of the time, Pallas kernels for 0%

profile of v1, /device:TPU:0, one launch (start us, length us, event | category | flops | bytes accessed | tf_op | source)
XLA Modules:
  0.0 48.3 jit_solution(16693603747344181661)
XLA Ops:
  0.6 0.0 copy-start
  0.6 0.0 copy-start.1
  0.6 1.2 %copy.19 = f32[16,4,1536]{2,0,1:T(8,128)S(1)} copy(f32[16,4,1536]{2,1,0:T(4,128)} %param.5) | data formatting | bytes 786432 | tf_op args[2]
  1.9 4.0 %all_to_all.18 = f32[16,4,1536]{2,0,1:T(8,128)S(1)} all-to-all(f32[16,4,1536]{2,0,1:T(8,128)S(1)} %copy.19), channel_id=1, replica_groups=mesh['srv'=16,'grp'=2] {'grp'}, dimensions={1} | all-to-all | bytes 786432 | tf_op jit(solution)/shard_map/all_to_all | solution.py:34
  5.9 0.3 copy.41
  6.3 0.3 all_to_all.16
  6.6 0.0 copy-done
  6.6 0.0 copy-done.1
  6.6 0.5 %copy_multiply_fusion = f32[64,2,3072]{2,0,1:T(8,128)S(1)} fusion(f32[64,2,3072]{2,1,0:T(2,128)S(1)} %copy-done, f32[64]{0:T(128)S(1)} %copy-done.1), kind=kLoop, calls=%fused_computation.8 | loop fusion | flops 393216 | bytes 3145984 | tf_op jit(solution)/shard_map/mul | solution.py:33
  7.1 1.7 %fusion.10 = f32[80,80]{0,1:T(8,128)S(1)} fusion(f32[16,2,3072]{2,0,1:T(8,128)S(1)} %all_to_all.16, f32[64,2,3072]{2,0,1:T(8,128)S(1)} %copy_multiply_fusion), kind=kOutput, calls=%fused_computation.11 | convolution fusion | flops 472357120 | bytes 1991680 | tf_op jit(solution)/shard_map/dot_general | solution.py:37
  8.8 0.2 collective-permute-start
  9.0 1.1 %collective-permute-done = f32[80,80]{0,1:T(8,128)S(1)} collective-permute-done((f32[80,80]{0,1:T(8,128)S(1)}, f32[80,80]{0,1:T(8,128)S(1)}, u32[]{:S(2)}, u32[]{:S(2)}) %collective-permute-start) | collective-permute-done | bytes 25632 | tf_op jit(solution)/shard_map/ppermute | solution.py:20
  10.1 2.7 %collective-permute-start.1 = (f32[80,80]{0,1:T(8,128)S(1)}, f32[80,80]{0,1:T(8,128)S(1)}, u32[]{:S(2)}, u32[]{:S(2)}) collective-permute-start(f32[80,80]{0,1:T(8,128)S(1)} %add.26), channel_id=1, source_target_pairs={{0,3},{1,2},{2,1},{3,0},{4,7},{5,6},{6,5},{7,4},{8,11},{9,10},{10,... | collective-permute-start | bytes 76808 | tf_op jit(solution)/shard_map/ppermute | solution.py:20
  12.9 1.7 %collective-permute-done.1 = f32[80,80]{0,1:T(8,128)S(1)} collective-permute-done((f32[80,80]{0,1:T(8,128)S(1)}, f32[80,80]{0,1:T(8,128)S(1)}, u32[]{:S(2)}, u32[]{:S(2)}) %collective-permute-start.1) | collective-permute-done | bytes 25632 | tf_op jit(solution)/shard_map/ppermute | solution.py:20
  14.5 1.9 %collective-permute-start.2 = (f32[80,80]{0,1:T(8,128)S(1)}, f32[80,80]{0,1:T(8,128)S(1)}, u32[]{:S(2)}, u32[]{:S(2)}) collective-permute-start(f32[80,80]{0,1:T(8,128)S(1)} %add.27), channel_id=1, source_target_pairs={{0,5},{1,4},{2,7},{3,6},{4,1},{5,0},{6,3},{7,2},{8,13},{9,12},{10,... | collective-permute-start | bytes 76808 | tf_op jit(solution)/shard_map/ppermute | solution.py:20
  16.4 1.7 %collective-permute-done.2 = f32[80,80]{0,1:T(8,128)S(1)} collective-permute-done((f32[80,80]{0,1:T(8,128)S(1)}, f32[80,80]{0,1:T(8,128)S(1)}, u32[]{:S(2)}, u32[]{:S(2)}) %collective-permute-start.2) | collective-permute-done | bytes 25632 | tf_op jit(solution)/shard_map/ppermute | solution.py:20
  18.1 0.6 %add.28 = f32[80,80]{0,1:T(8,128)} add(f32[80,80]{0,1:T(8,128)S(1)} %add.27, f32[80,80]{0,1:T(8,128)S(1)} %collective-permute-done.2) | non-fusion elementwise | flops 6400 | bytes 76800 | tf_op jit(solution)/shard_map/add | solution.py:20
  18.7 1.9 %collective-permute-start.3 = (f32[80,80]{0,1:T(8,128)}, f32[80,80]{0,1:T(8,128)}, u32[]{:S(2)}, u32[]{:S(2)}) collective-permute-start(f32[80,80]{0,1:T(8,128)} %add.28), channel_id=1, source_target_pairs={{0,9},{1,8},{2,11},{3,10},{4,13},{5,12},{6,15},{7,14},{8,1},{9,0},... | collective-permute-start | bytes 76808 | tf_op jit(solution)/shard_map/ppermute | solution.py:20
  20.6 0.5 %fusion.17 = f32[2,8,8,3072]{3,2,1,0:T(8,128)S(1)} fusion(f32[64]{0:T(128)S(1)} %copy-done.1, f32[64,2,3072]{2,1,0:T(2,128)S(1)} %copy-done), kind=kLoop, calls=%fused_computation.24 | loop fusion | flops 393216 | bytes 3145984
  21.1 0.3 copy.42
  21.5 0.3 concatenate.12
  21.8 0.1 copy.31
  21.9 0.7 %collective-permute-done.3 = f32[80,80]{0,1:T(8,128)} collective-permute-done((f32[80,80]{0,1:T(8,128)}, f32[80,80]{0,1:T(8,128)}, u32[]{:S(2)}, u32[]{:S(2)}) %collective-permute-start.3) | collective-permute-done | bytes 25632 | tf_op jit(solution)/shard_map/ppermute | solution.py:20
  22.6 0.8 %add.29 = f32[80,80]{0,1:T(8,128)S(1)} add(f32[80,80]{0,1:T(8,128)} %add.28, f32[80,80]{0,1:T(8,128)} %collective-permute-done.3) | non-fusion elementwise | flops 6400 | bytes 76800 | tf_op jit(solution)/shard_map/add | solution.py:20
  23.4 2.8 %collective-permute-start.4 = (f32[80,80]{0,1:T(8,128)S(1)}, f32[80,80]{0,1:T(8,128)S(1)}, u32[]{:S(2)}, u32[]{:S(2)}) collective-permute-start(f32[80,80]{0,1:T(8,128)S(1)} %add.29), channel_id=1, source_target_pairs={{0,17},{1,16},{2,19},{3,18},{4,21},{5,20},{6,23},{7,22},{8,25},{9,... | collective-permute-start | bytes 76808 | tf_op jit(solution)/shard_map/ppermute | solution.py:20
  26.3 0.1 pad_maximum_fusion
  26.4 1.5 %collective-permute-done.4 = f32[80,80]{0,1:T(8,128)S(1)} collective-permute-done((f32[80,80]{0,1:T(8,128)S(1)}, f32[80,80]{0,1:T(8,128)S(1)}, u32[]{:S(2)}, u32[]{:S(2)}) %collective-permute-start.4) | collective-permute-done | bytes 25632 | tf_op jit(solution)/shard_map/ppermute | solution.py:20
  28.0 0.1 copy.23
  28.1 7.3 %cholesky.17 = f32[80,80]{1,0:T(8,128)S(1)} custom-call(f32[80,80]{1,0:T(8,128)S(1)} %fusion.14), custom_call_target="Cholesky" | custom-call | tf_op jit(solution)/shard_map/jit(cholesky)/cholesky | solution.py:25
  35.4 0.6 %compare_reduce_fusion = pred[]{:T(512)} fusion(f32[80]{0:T(128)S(1)} %select_reduce_fusion), kind=kLoop, calls=%fused_computation.22 | loop fusion | flops 159 | bytes 321 | tf_op jit(solution)/shard_map/jit(cholesky)/cholesky | solution.py:25
  36.1 1.3 %select_bitcast_fusion = (f32[1,80,80]{2,1,0:T(8,128)S(1)}, f32[80,80]{1,0:T(8,128)}) fusion(f32[80,80]{1,0:T(8,128)S(1)} %cholesky.17, pred[]{:T(512)} %compare_reduce_fusion), kind=kLoop, calls=%fused_computation.17 | loop fusion | flops 25600 | bytes 76801 | tf_op jit(solution)/shard_map/triangular_solve | solution.py:41
  37.3 6.1 %custom-call.6 = f32[1,80,80]{1,2,0:T(8,128)S(1)} custom-call(f32[1,80,80]{2,1,0:T(8,128)S(1)} %get-tuple-element.8), custom_call_target="InvertDiagBlocksLowerTriangular" | custom-call | tf_op jit(solution)/shard_map/triangular_solve | solution.py:41
  43.5 0.2 convolution_bitcast_fusion
  43.7 1.8 %fusion = f32[80,2,3072]{2,0,1:T(8,128)S(1)} fusion(f32[80,80,1]{1,0,2:T(8,128)S(1)} %convolution_bitcast_fusion, f32[10,2,8,3072]{3,2,1,0:T(8,128)S(1)} %bitcast.33), kind=kOutput, calls=%fused_computation | convolution fusion | flops 471859200 | bytes 3957760 | tf_op jit(solution)/shard_map/dot_general | solution.py:44
  45.5 2.8 %copy.26 = f32[80,2,3072]{2,1,0:T(2,128)} copy(f32[80,2,3072]{2,0,1:T(8,128)S(1)} %fusion) | data formatting | bytes 3932160
  (5 shorter events, 0.1 us)
Async XLA Ops:
  0.6 6.0 %copy-start = (f32[64,2,3072]{2,1,0:T(2,128)S(1)}, f32[64,2,3072]{2,1,0:T(2,128)}, u32[]{:S(2)}) copy-start(f32[64,2,3072]{2,1,0:T(2,128)} %param.3) | copy-start | bytes 4718596
  0.6 6.0 %copy-start.1 = (f32[64]{0:T(128)S(1)}, f32[64]{0:T(128)}, u32[]{:S(2)}) copy-start(f32[64]{0:T(128)} %param.4) | copy-start | bytes 772
  8.8 1.3 %collective-permute-start = (f32[80,80]{0,1:T(8,128)S(1)}, f32[80,80]{0,1:T(8,128)S(1)}, u32[]{:S(2)}, u32[]{:S(2)}) collective-permute-start(f32[80,80]{0,1:T(8,128)S(1)} %fusion.10), channel_id=1, source_target_pairs={{0,1},{1,0},{2,3},{3,2},{4,5},{5,4},{6,7},{7,6},{8,9},{9,8},{10,11... | collective-permute-start | bytes 76808 | tf_op jit(solution)/shard_map/ppermute | solution.py:20
  10.1 4.4 %collective-permute-start.1 = (f32[80,80]{0,1:T(8,128)S(1)}, f32[80,80]{0,1:T(8,128)S(1)}, u32[]{:S(2)}, u32[]{:S(2)}) collective-permute-start(f32[80,80]{0,1:T(8,128)S(1)} %add.26), channel_id=1, source_target_pairs={{0,3},{1,2},{2,1},{3,0},{4,7},{5,6},{6,5},{7,4},{8,11},{9,10},{10,... | collective-permute-start | bytes 76808 | tf_op jit(solution)/shard_map/ppermute | solution.py:20
  14.5 3.6 %collective-permute-start.2 = (f32[80,80]{0,1:T(8,128)S(1)}, f32[80,80]{0,1:T(8,128)S(1)}, u32[]{:S(2)}, u32[]{:S(2)}) collective-permute-start(f32[80,80]{0,1:T(8,128)S(1)} %add.27), channel_id=1, source_target_pairs={{0,5},{1,4},{2,7},{3,6},{4,1},{5,0},{6,3},{7,2},{8,13},{9,12},{10,... | collective-permute-start | bytes 76808 | tf_op jit(solution)/shard_map/ppermute | solution.py:20
  18.7 3.9 %collective-permute-start.3 = (f32[80,80]{0,1:T(8,128)}, f32[80,80]{0,1:T(8,128)}, u32[]{:S(2)}, u32[]{:S(2)}) collective-permute-start(f32[80,80]{0,1:T(8,128)} %add.28), channel_id=1, source_target_pairs={{0,9},{1,8},{2,11},{3,10},{4,13},{5,12},{6,15},{7,14},{8,1},{9,0},... | collective-permute-start | bytes 76808 | tf_op jit(solution)/shard_map/ppermute | solution.py:20
  23.4 4.5 %collective-permute-start.4 = (f32[80,80]{0,1:T(8,128)S(1)}, f32[80,80]{0,1:T(8,128)S(1)}, u32[]{:S(2)}, u32[]{:S(2)}) collective-permute-start(f32[80,80]{0,1:T(8,128)S(1)} %add.29), channel_id=1, source_target_pairs={{0,17},{1,16},{2,19},{3,18},{4,21},{5,20},{6,23},{7,22},{8,25},{9,... | collective-permute-start | bytes 76808 | tf_op jit(solution)/shard_map/ppermute | solution.py:20

commit v2 on v1

v2 whole, which is shorter than its diff:
```python
import functools
import jax
import jax.numpy as jnp
from jax import lax
from jax.experimental import pallas as pl
from jax.experimental.pallas import tpu as pltpu
from jax.sharding import PartitionSpec as P

AXES = ("srv", "grp")
LANES = 128
TILE = 8
F32, BF16 = jnp.float32, jnp.bfloat16
VMEM = pl.BlockSpec(memory_space=pltpu.VMEM)
ANY = pl.BlockSpec(memory_space=pl.ANY)
PARAMS = pltpu.CompilerParams(vmem_limit_bytes=16 * 2**20)


def total(value):
    servers, cores = lax.axis_size("srv"), lax.axis_size("grp")
    if servers & (servers - 1) or cores != 2:
        return lax.psum(value, AXES)
    count = servers * cores
    masks = [1] + [2 * bit + 1 for bit in (1 << p for p in range(servers.bit_length() - 1))]
    for mask in masks:
        value = value + lax.ppermute(value, AXES, [(i, i ^ mask) for i in range(count)])
    return value


def split(x):
    high = x.astype(BF16)
    return high, (x - high.astype(F32)).astype(BF16)


def rows_times_rows(a, b):
    return lax.dot_general(a, b, (((1,), (1,)), ((), ())), preferred_element_type=F32)


def modes_kernel(modes, panel, gram, buf, sems):
    count, slabs, _ = modes.shape
    chunks = sems.shape[0]
    step = slabs // chunks
    copies = []
    for c in range(chunks):
        part = (slice(None), pl.ds(c * step, step))
        copies.append(pltpu.make_async_copy(modes.at[part], buf.at[part], sems.at[c]))
        copies[-1].start()
    acc = None
    for c in range(chunks):
        copies[c].wait()
        for i in range(c * step, (c + 1) * step):
            high, low = split(buf[:, i, :])
            panel[:count, i * LANES:(i + 1) * LANES] = high
            panel[count:, i * LANES:(i + 1) * LANES] = low
        cols = slice(c * step * LANES, (c + 1) * step * LANES)
        term = rows_times_rows(panel[:, cols], panel[:count, cols])
        acc = term if acc is None else acc + term
    cross = acc[count:]
    gram[...] = acc[:count] + cross + cross.T


def snaps_kernel(first, second, modes_panel, modes_gram, panel, packed):
    snaps, half, _ = first.shape
    modes = modes_gram.shape[0]
    for h, part in enumerate((first, second)):
        for i in range(half):
            high, low = split(part[:, i, :])
            at = (h * half + i) * LANES
            panel[:snaps, at:at + LANES] = high
            panel[snaps:, at:at + LANES] = low
    with_modes = rows_times_rows(panel[...], modes_panel[...])
    own = rows_times_rows(panel[...], panel[:snaps])
    low_row = (with_modes[:snaps, :modes] + with_modes[:snaps, modes:]) + with_modes[snaps:, :modes]
    own = own[:snaps] + own[snaps:] + own[snaps:].T
    width = modes + snaps
    mid = width // 2
    a = modes_gram[...]
    left = jnp.concatenate(
        [
            jnp.concatenate([a[mid:], jnp.zeros((modes - mid, snaps), F32)], axis=1),
            jnp.concatenate([low_row, own], axis=1),
        ],
        axis=0,
    )
    packed[...] = jnp.concatenate(
        [left, a[:mid, :mid], jnp.zeros((mid, LANES - width - mid), F32)], axis=1
    )


def spread_row(x, i):
    return jnp.broadcast_to(x[i:i + 1, :], (TILE, LANES))


def spread_column(x, j):
    return jnp.broadcast_to(x[:, j:j + 1], (x.shape[0], LANES))


def factor_tiles(tiles):
    lane = lax.broadcasted_iota(jnp.int32, (TILE, LANES), 1)
    sub = lax.broadcasted_iota(jnp.int32, (TILE, LANES), 0)
    tiles = list(tiles)
    upper, inverse = [], []
    for t in range(len(tiles)):
        at = t * TILE
        columns = [[spread_column(x, at + j) for j in range(TILE)] for x in tiles[t:]]
        a = {(i, j): spread_row(columns[0][j], i) for j in range(TILE) for i in range(j, TILE)}
        l, m, root = {}, {}, []
        for j in range(TILE):
            r = lax.rsqrt(a[j, j])
            root.append(r)
            for i in range(j + 1, TILE):
                l[i, j] = a[i, j] * r
            for k in range(j + 1, TILE):
                for i in range(k, TILE):
                    a[i, k] = a[i, k] - l[i, j] * l[k, j]
            m[j, j] = r
            for k in range(j):
                dot = l[j, k] * m[k, k]
                for q in range(k + 1, j):
                    dot = dot + l[j, q] * m[q, k]
                m[j, k] = -(dot * r)
        def column_of(k):
            out = jnp.zeros((TILE, LANES), F32)
            for i in range(k, TILE):
                out = jnp.where(sub == i, m[i, k], out)
            return out
        def row_of(i):
            out = jnp.zeros((TILE, LANES), F32)
            for k in range(i + 1):
                out = jnp.where(sub == k, m[i, k], out)
            return out
        m_columns = [column_of(k) for k in range(TILE)]
        row = sum(m_columns[k] * spread_row(tiles[t], k) for k in range(TILE))
        block = (lane >= at) & (lane < at + TILE)
        placed = jnp.zeros((TILE, LANES), F32)
        for k in range(TILE):
            placed = jnp.where(lane == at + k, m_columns[k], placed)
        upper.append(row)
        inv_row = jnp.where(block, placed, jnp.where(lane < at, row, 0.0))
        inverse.append(inv_row)
        if t + 1 == len(tiles):
            break
        mixed = jnp.where(block, placed, row)
        solved = sum(row_of(i) * spread_row(mixed, i) for i in range(TILE))
        rows = [spread_row(solved, j) for j in range(TILE)]
        for s in range(t + 1, len(tiles)):
            x = jnp.where(block, 0.0, tiles[s])
            c = columns[s - t]
            x = x - sum(c[j] * rows[j] for j in range(TILE))
            tiles[s] = x
    return upper, inverse


def apply_kernel(cells, packed, scale, modes_panel, snaps_panel, out, factor, left, buf, sems):
    modes, snaps = modes_panel.shape[0] // 2, snaps_panel.shape[0] // 2
    width = modes + snaps
    mid = width // 2
    both = packed[...] * (1.0 / cells)
    lane = lax.broadcasted_iota(jnp.int32, (mid, LANES), 1)
    top = jnp.where(lane < mid, pltpu.roll(both, LANES - width, 1), 0.0)
    low = jnp.where(lane < width, both, 0.0)
    lower = jnp.concatenate([top, low, jnp.zeros((LANES - width, LANES), F32)], axis=0)
    r = lax.broadcasted_iota(jnp.int32, (LANES, LANES), 0)
    c = lax.broadcasted_iota(jnp.int32, (LANES, LANES), 1)
    full = jnp.where(r >= c, lower, lower.T)
    upper, inverse = factor_tiles([full[i:i + TILE] for i in range(0, width, TILE)])
    for i, x in enumerate(inverse):
        left[i * TILE:(i + 1) * TILE, :] = x
    whole = jnp.concatenate(upper + [jnp.zeros((LANES - width, LANES), F32)], axis=0).T
    whole = jnp.where(r >= c, whole, 0.0)[:width, :width]
    factor[...] = whole * scale[...]
    w_high, w_low = split(left[:, :width])
    wm = jnp.concatenate([w_high[:, :modes], w_low[:, :modes]], axis=0)
    ws = jnp.concatenate([w_high[:, modes:], w_low[:, modes:]], axis=0)
    both_w = jnp.concatenate([wm, wm, ws, ws], axis=1)
    chunks = sems.shape[0]
    slabs = buf.shape[1]
    step = slabs // chunks
    copies = []
    for k in range(chunks):
        cols = slice(k * step * LANES, (k + 1) * step * LANES)
        right = jnp.concatenate([modes_panel[:, cols], snaps_panel[:, cols]], axis=0)
        res = jnp.dot(both_w, right, preferred_element_type=F32)
        res = res[:width] + res[width:]
        for i in range(step):
            buf[:, k * step + i, :] = res[:, i * LANES:(i + 1) * LANES]
        part = (slice(None), pl.ds(k * step, step))
        copies.append(pltpu.make_async_copy(buf.at[part], out.at[part], sems.at[k]))
        copies[-1].start()
    for copy in copies:
        copy.wait()


def per_device(basis_modes, weights, snapshots):
    modes, rows, cols = basis_modes.shape
    snaps = snapshots.shape[0]
    width = modes + snaps
    tiles = cols // LANES
    slabs = rows * tiles
    cores = lax.axis_size("grp")
    cells = rows * cols * lax.axis_size("srv") * cores
    core = lax.axis_index("grp")
    fields = basis_modes.reshape(modes, rows, tiles, LANES).transpose(0, 2, 1, 3)
    fields = fields.reshape(modes, slabs, LANES)
    own = snapshots.reshape(snaps, cores, rows, tiles // cores, LANES).transpose(0, 3, 1, 2, 4)
    keep = jnp.where(core == 0, own[:, :, 0], own[:, :, 1]).reshape(snaps, slabs // cores, LANES)
    send = jnp.where(core == 0, own[:, :, 1], own[:, :, 0]).reshape(snaps, slabs // cores, LANES)
    got = lax.ppermute(send, "grp", [(0, 1), (1, 0)])
    first = jnp.where(core == 0, keep, got)
    second = jnp.where(core == 0, got, keep)

    chunk = 6
    modes_panel, modes_gram = pl.pallas_call(
        modes_kernel,
        out_shape=(
            jax.ShapeDtypeStruct((2 * modes, slabs * LANES), BF16),
            jax.ShapeDtypeStruct((modes, modes), F32),
        ),
        in_specs=[ANY],
        out_specs=(VMEM, VMEM),
        scratch_shapes=[pltpu.VMEM((modes, slabs, LANES), F32), pltpu.SemaphoreType.DMA((chunk,))],
        cost_estimate=pl.CostEstimate(flops=10**8, bytes_accessed=fields.size * 4, transcendentals=0),
        compiler_params=PARAMS,
        name="modes_gram",
    )(fields)
    snaps_panel, packed = pl.pallas_call(
        snaps_kernel,
        out_shape=(
            jax.ShapeDtypeStruct((2 * snaps, slabs * LANES), BF16),
            jax.ShapeDtypeStruct((width // 2, LANES), F32),
        ),
        in_specs=[VMEM] * 4,
        out_specs=(VMEM, VMEM),
        compiler_params=PARAMS,
        name="snaps_gram",
    )(first, second, modes_panel, modes_gram)
    packed = total(packed)
    scale = jnp.concatenate([weights, jnp.ones((snaps,), F32)])
    new_modes, factor = pl.pallas_call(
        functools.partial(apply_kernel, cells),
        out_shape=(
            jax.ShapeDtypeStruct((width, slabs, LANES), F32),
            jax.ShapeDtypeStruct((width, width), F32),
        ),
        in_specs=[VMEM] * 4,
        out_specs=(ANY, VMEM),
        scratch_shapes=[
            pltpu.VMEM((width, LANES), F32),
            pltpu.VMEM((width, slabs, LANES), F32),
            pltpu.SemaphoreType.DMA((chunk,)),
        ],
        compiler_params=PARAMS,
        name="factor_apply",
    )(packed, scale[:, None], modes_panel, snaps_panel)
    new_modes = new_modes.reshape(width, tiles, rows, LANES).transpose(0, 2, 1, 3)
    return new_modes.reshape(width, rows, cols), factor


def solution(mesh):
    in_specs = (P(None, AXES, None), P(), P(None, "srv", "grp"))
    out_specs = (P(None, AXES, None), P())
    return jax.shard_map(
        per_device, mesh=mesh, in_specs=in_specs, out_specs=out_specs, check_vma=False
    )
```

time: 48.8 us -> 32.4 us (0.66)
  other arithmetic: 18 us -> 0.09 us
  Pallas kernels: 0 us -> 12.8 us
  blocking collectives: 4.05 us -> 0 us
  matrix products: 3.72 us -> 0 us
  local copies, waits for them, and re-layouts: 5.51 us -> 2.01 us
    another operation x5 -> x0, other arithmetic: 15.4 us -> none  [the longest x3 7.98 us: merged_factor(): return jnp.linalg.cholesky(total(local_gram))]
    pallas_call x0 -> x3, Pallas kernels: none -> 12.8 us  [the longest x1 5.91 us: per_device(): pl.pallas_call(functools.partial(apply_kernel, cells), out_shape=(jax.Sha...]
    all_to_all x1 -> x0, blocking collectives: 4.05 us -> none  [per_device(): lax.all_to_all(snapshots, 'grp', split_axis=1, concat_axis=2, tiled=True)]
    dot_general x2 -> x0, matrix products: 3.5 us -> none  [the longest x1 1.81 us: per_device(): jnp.dot(inverse, panel, precision=lax.Precision.HIGHEST, preferred_elemen...]
    unnamed x6 -> x5, local copies, waits for them, and re-layouts: 4.04 us -> 1.53 us
    add x5, other arithmetic: 1.45 us -> 0.02 us  [total(): value + lax.ppermute(value, AXES, [(i, i ^ mask) for i in range(count)])]
    all_to_all x3 -> x0, local copies, waits for them, and re-layouts: 0.95 us -> none  [per_device(): lax.all_to_all(snapshots, 'grp', split_axis=1, concat_axis=2, tiled=True)]
    ppermute x0 -> x1, starting transfers between devices: none -> 0.56 us  [per_device(): got = lax.ppermute(send, 'grp', [(0, 1), (1, 0)])]
  transfers between devices with their start and end apart: 5 -> 6, of which waited for: 5 -> 5; matrix products, arithmetic and copies ran while one was open for 3% -> 1% of each run, Pallas kernels for 0% -> 17%
where the time goes in v2:
time: 32.4 us; the launch traced here: 32.2 us
  Pallas kernels  12.8 us (40%)
  starting transfers between devices  9.92 us (31%)
  waiting for transfers between devices  6.67 us (21%)
  local copies, waits for them, and re-layouts  2.01 us (6%)
  between operations  0.72 us (2%)
    ppermute x5, starting transfers between devices, total(): lax.ppermute(value, AXES, [(i, i ^ mask) for i in range(count)])  9.36 us
    ppermute x5, waiting for transfers between devices, total(): lax.ppermute(value, AXES, [(i, i ^ mask) for i in range(count)])  6.66 us
    pallas_call x1, Pallas kernels, per_device(): pl.pallas_call(functools.partial(apply_kernel, cells), out_shape=(jax.Sha...  5.91 us
    pallas_call x1, Pallas kernels, per_device(): pl.pallas_call(modes_kernel, out_shape=(jax.ShapeDtypeStruct((2 * modes,...  5.38 us
    unnamed x5, local copies, waits for them, and re-layouts  1.53 us
    pallas_call x1, Pallas kernels, per_device(): pl.pallas_call(snaps_kernel, out_shape=(jax.ShapeDtypeStruct((2 * snaps,...  1.48 us
  transfers between devices with their start and end apart: 6, of which 5 were waited for; matrix products, arithmetic and copies ran while one was open for 1% of the time, Pallas kernels for 17%

profile of v2, /device:TPU:0, one launch (start us, length us, event | category | flops | bytes accessed | tf_op | source)
XLA Modules:
  0.0 32.2 jit_solution(8686225104442033151)
XLA Ops:
  0.6 1.1 %copy.9 = f32[16,4,1536]{2,0,1:T(8,128)S(1)} copy(f32[16,4,1536]{2,1,0:T(4,128)} %param.5) | data formatting | bytes 786432 | tf_op args[2]
  1.8 0.0 copy-start
  1.8 0.1 reshape.29
  1.9 0.2 copy.11
  2.1 0.6 %collective-permute-start = (f32[16,24,128]{2,1,0:T(8,128)S(1)}, f32[16,24,128]{2,1,0:T(8,128)S(1)}, u32[]{:S(2)}, u32[]{:S(2)}) collective-permute-start(f32[16,24,128]{2,1,0:T(8,128)S(1)} %bitcast.20), channel_id=1, source_target_pairs={{0,1},{1,0},{2,3},{3,2},{4,5},{5,4},{6,7},{7,6},{8,9},{9,8},{10,11... | collective-permute-start | bytes 589832 | tf_op jit(solution)/shard_map/ppermute | solution.py:207
  2.6 0.2 copy.10
  2.8 0.4 %copy-done = f32[64,2,3072]{2,1,0:T(2,128)S(1)} copy-done((f32[64,2,3072]{2,1,0:T(2,128)S(1)}, f32[64,2,3072]{2,1,0:T(2,128)}, u32[]{:S(2)}) %copy-start) | copy-done | bytes 1572888
  3.2 5.4 %modes_gram.1 = (bf16[128,6144]{1,0:T(8,128)(2,1)S(1)}, f32[64,64]{1,0:T(8,128)S(1)}) custom-call(f32[64,48,128]{2,1,0:T(8,128)S(1)} %bitcast.17), custom_call_target="tpu_custom_call" | custom-call | flops 100000000 | bytes 1572864 | tf_op jit(solution)/shard_map/modes_gram/pallas_call | solution.py:212
  8.6 0.0 copy-start.1
  8.6 0.0 collective-permute-done
  8.6 1.5 %snaps_gram.1 = (bf16[32,6144]{1,0:T(8,128)(2,1)S(1)}, f32[40,128]{1,0:T(8,128)S(1)}) custom-call(f32[16,24,128]{2,1,0:T(8,128)S(1)} %get-tuple-element.17.first, f32[16,24,128]{2,1,0:T(8,128)S(1)} %get-tuple-element.16.second, bf16[128,6144]{1,0:T(8,128)(2,1)S(1)} %get-tuple-element.8.modes_panel, f32[64,64]{1,0:T(8,128)S(1)} %get-tuple-element.9.modes_gram), custom_call_target="tpu_custom_call" | custom-call | tf_op jit(solution)/shard_map/snaps_gram/pallas_call | solution.py:225
  10.1 0.5 %collective-permute-start.1 = (f32[40,128]{1,0:T(8,128)S(1)}, f32[40,128]{1,0:T(8,128)S(1)}, u32[]{:S(2)}, u32[]{:S(2)}) collective-permute-start(f32[40,128]{1,0:T(8,128)S(1)} %get-tuple-element.10), channel_id=1, source_target_pairs={{0,1},{1,0},{2,3},{3,2},{4,5},{5,4},{6,7},{7,6},{8,9},{9,8},{10,11... | collective-permute-start | bytes 61448 | tf_op jit(solution)/shard_map/ppermute | solution.py:25
  10.6 0.8 %collective-permute-done.1 = f32[40,128]{1,0:T(8,128)S(1)} collective-permute-done((f32[40,128]{1,0:T(8,128)S(1)}, f32[40,128]{1,0:T(8,128)S(1)}, u32[]{:S(2)}, u32[]{:S(2)}) %collective-permute-start.1) | collective-permute-done | bytes 20512 | tf_op jit(solution)/shard_map/ppermute | solution.py:25
  11.5 2.6 %collective-permute-start.2 = (f32[40,128]{1,0:T(8,128)S(1)}, f32[40,128]{1,0:T(8,128)S(1)}, u32[]{:S(2)}, u32[]{:S(2)}) collective-permute-start(f32[40,128]{1,0:T(8,128)S(1)} %add.17), channel_id=1, source_target_pairs={{0,3},{1,2},{2,1},{3,0},{4,7},{5,6},{6,5},{7,4},{8,11},{9,10},{10,... | collective-permute-start | bytes 61448 | tf_op jit(solution)/shard_map/ppermute | solution.py:25
  14.0 1.5 %collective-permute-done.2 = f32[40,128]{1,0:T(8,128)S(1)} collective-permute-done((f32[40,128]{1,0:T(8,128)S(1)}, f32[40,128]{1,0:T(8,128)S(1)}, u32[]{:S(2)}, u32[]{:S(2)}) %collective-permute-start.2) | collective-permute-done | bytes 20512 | tf_op jit(solution)/shard_map/ppermute | solution.py:25
  15.5 1.8 %collective-permute-start.3 = (f32[40,128]{1,0:T(8,128)S(1)}, f32[40,128]{1,0:T(8,128)S(1)}, u32[]{:S(2)}, u32[]{:S(2)}) collective-permute-start(f32[40,128]{1,0:T(8,128)S(1)} %add.18), channel_id=1, source_target_pairs={{0,5},{1,4},{2,7},{3,6},{4,1},{5,0},{6,3},{7,2},{8,13},{9,12},{10,... | collective-permute-start | bytes 61448 | tf_op jit(solution)/shard_map/ppermute | solution.py:25
  17.3 1.5 %collective-permute-done.3 = f32[40,128]{1,0:T(8,128)S(1)} collective-permute-done((f32[40,128]{1,0:T(8,128)S(1)}, f32[40,128]{1,0:T(8,128)S(1)}, u32[]{:S(2)}, u32[]{:S(2)}) %collective-permute-start.3) | collective-permute-done | bytes 20512 | tf_op jit(solution)/shard_map/ppermute | solution.py:25
  18.8 1.8 %collective-permute-start.4 = (f32[40,128]{1,0:T(8,128)S(1)}, f32[40,128]{1,0:T(8,128)S(1)}, u32[]{:S(2)}, u32[]{:S(2)}) collective-permute-start(f32[40,128]{1,0:T(8,128)S(1)} %add.19), channel_id=1, source_target_pairs={{0,9},{1,8},{2,11},{3,10},{4,13},{5,12},{6,15},{7,14},{8,1},{9,0},... | collective-permute-start | bytes 61448 | tf_op jit(solution)/shard_map/ppermute | solution.py:25
  20.6 1.5 %collective-permute-done.4 = f32[40,128]{1,0:T(8,128)S(1)} collective-permute-done((f32[40,128]{1,0:T(8,128)S(1)}, f32[40,128]{1,0:T(8,128)S(1)}, u32[]{:S(2)}, u32[]{:S(2)}) %collective-permute-start.4) | collective-permute-done | bytes 20512 | tf_op jit(solution)/shard_map/ppermute | solution.py:25
  22.0 2.7 %collective-permute-start.5 = (f32[40,128]{1,0:T(8,128)S(1)}, f32[40,128]{1,0:T(8,128)S(1)}, u32[]{:S(2)}, u32[]{:S(2)}) collective-permute-start(f32[40,128]{1,0:T(8,128)S(1)} %add.20), channel_id=1, source_target_pairs={{0,17},{1,16},{2,19},{3,18},{4,21},{5,20},{6,23},{7,22},{8,25},{9,... | collective-permute-start | bytes 61448 | tf_op jit(solution)/shard_map/ppermute | solution.py:25
  24.8 0.0 copy-done.1
  24.8 0.1 copy.13.scale
  24.9 1.4 %collective-permute-done.5 = f32[40,128]{1,0:T(8,128)S(1)} collective-permute-done((f32[40,128]{1,0:T(8,128)S(1)}, f32[40,128]{1,0:T(8,128)S(1)}, u32[]{:S(2)}, u32[]{:S(2)}) %collective-permute-start.5) | collective-permute-done | bytes 20512 | tf_op jit(solution)/shard_map/ppermute | solution.py:25
  26.3 5.9 %factor_apply.1 = (f32[80,48,128]{2,1,0:T(8,128)}, f32[80,80]{1,0:T(8,128)}) custom-call(f32[40,128]{1,0:T(8,128)S(1)} %add.21.packed, f32[80,1]{1,0:T(8,128)S(1)} %copy.13.scale, bf16[128,6144]{1,0:T(8,128)(2,1)S(1)} %get-tuple-element.8.modes_panel, bf16[32,6144]{1,0:T(8,128)(2,1)S(1)} %get-tuple-element.11.snaps_panel), custom_call_target="tpu_custom_call" | custom-call | tf_op jit(solution)/shard_map/factor_apply/pallas_call | solution.py:238
  (8 shorter events, 0.1 us)
Async XLA Ops:
  1.8 1.4 %copy-start = (f32[64,2,3072]{2,1,0:T(2,128)S(1)}, f32[64,2,3072]{2,1,0:T(2,128)}, u32[]{:S(2)}) copy-start(f32[64,2,3072]{2,1,0:T(2,128)} %param.3) | copy-start | bytes 4718596
  2.1 6.5 %collective-permute-start = (f32[16,24,128]{2,1,0:T(8,128)S(1)}, f32[16,24,128]{2,1,0:T(8,128)S(1)}, u32[]{:S(2)}, u32[]{:S(2)}) collective-permute-start(f32[16,24,128]{2,1,0:T(8,128)S(1)} %bitcast.20), channel_id=1, source_target_pairs={{0,1},{1,0},{2,3},{3,2},{4,5},{5,4},{6,7},{7,6},{8,9},{9,8},{10,11... | collective-permute-start | bytes 589832 | tf_op jit(solution)/shard_map/ppermute | solution.py:207
  8.6 16.2 %copy-start.1 = (f32[64]{0:T(128)S(1)}, f32[64]{0:T(128)}, u32[]{:S(2)}) copy-start(f32[64]{0:T(128)} %param.4) | copy-start | bytes 772
  10.1 1.3 %collective-permute-start.1 = (f32[40,128]{1,0:T(8,128)S(1)}, f32[40,128]{1,0:T(8,128)S(1)}, u32[]{:S(2)}, u32[]{:S(2)}) collective-permute-start(f32[40,128]{1,0:T(8,128)S(1)} %get-tuple-element.10), channel_id=1, source_target_pairs={{0,1},{1,0},{2,3},{3,2},{4,5},{5,4},{6,7},{7,6},{8,9},{9,8},{10,11... | collective-permute-start | bytes 61448 | tf_op jit(solution)/shard_map/ppermute | solution.py:25
  11.5 4.1 %collective-permute-start.2 = (f32[40,128]{1,0:T(8,128)S(1)}, f32[40,128]{1,0:T(8,128)S(1)}, u32[]{:S(2)}, u32[]{:S(2)}) collective-permute-start(f32[40,128]{1,0:T(8,128)S(1)} %add.17), channel_id=1, source_target_pairs={{0,3},{1,2},{2,1},{3,0},{4,7},{5,6},{6,5},{7,4},{8,11},{9,10},{10,... | collective-permute-start | bytes 61448 | tf_op jit(solution)/shard_map/ppermute | solution.py:25
  15.5 3.2 %collective-permute-start.3 = (f32[40,128]{1,0:T(8,128)S(1)}, f32[40,128]{1,0:T(8,128)S(1)}, u32[]{:S(2)}, u32[]{:S(2)}) collective-permute-start(f32[40,128]{1,0:T(8,128)S(1)} %add.18), channel_id=1, source_target_pairs={{0,5},{1,4},{2,7},{3,6},{4,1},{5,0},{6,3},{7,2},{8,13},{9,12},{10,... | collective-permute-start | bytes 61448 | tf_op jit(solution)/shard_map/ppermute | solution.py:25
  18.8 3.3 %collective-permute-start.4 = (f32[40,128]{1,0:T(8,128)S(1)}, f32[40,128]{1,0:T(8,128)S(1)}, u32[]{:S(2)}, u32[]{:S(2)}) collective-permute-start(f32[40,128]{1,0:T(8,128)S(1)} %add.19), channel_id=1, source_target_pairs={{0,9},{1,8},{2,11},{3,10},{4,13},{5,12},{6,15},{7,14},{8,1},{9,0},... | collective-permute-start | bytes 61448 | tf_op jit(solution)/shard_map/ppermute | solution.py:25
  22.0 4.2 %collective-permute-start.5 = (f32[40,128]{1,0:T(8,128)S(1)}, f32[40,128]{1,0:T(8,128)S(1)}, u32[]{:S(2)}, u32[]{:S(2)}) collective-permute-start(f32[40,128]{1,0:T(8,128)S(1)} %add.20), channel_id=1, source_target_pairs={{0,17},{1,16},{2,19},{3,18},{4,21},{5,20},{6,23},{7,22},{8,25},{9,... | collective-permute-start | bytes 61448 | tf_op jit(solution)/shard_map/ppermute | solution.py:25

commit v3 on v2

--- a/solution.py
+++ b/solution.py
@@ -35,35 +35,24 @@
     return lax.dot_general(a, b, (((1,), (1,)), ((), ())), preferred_element_type=F32)
 
 
-def modes_kernel(modes, panel, gram, buf, sems):
-    count, slabs, _ = modes.shape
-    chunks = sems.shape[0]
-    step = slabs // chunks
-    copies = []
-    for c in range(chunks):
-        part = (slice(None), pl.ds(c * step, step))
-        copies.append(pltpu.make_async_copy(modes.at[part], buf.at[part], sems.at[c]))
-        copies[-1].start()
-    acc = None
-    for c in range(chunks):
-        copies[c].wait()
-        for i in range(c * step, (c + 1) * step):
-            high, low = split(buf[:, i, :])
-            panel[:count, i * LANES:(i + 1) * LANES] = high
-            panel[count:, i * LANES:(i + 1) * LANES] = low
-        cols = slice(c * step * LANES, (c + 1) * step * LANES)
-        term = rows_times_rows(panel[:, cols], panel[:count, cols])
-        acc = term if acc is None else acc + term
+def modes_kernel(modes, panel, gram):
+    count = gram.shape[0]
+    slabs = modes.shape[0] // count
+    for i in range(slabs):
+        high, low = split(modes[pl.ds(i, count, stride=slabs), :])
+        panel[:count, i * LANES:(i + 1) * LANES] = high
+        panel[count:, i * LANES:(i + 1) * LANES] = low
+    acc = rows_times_rows(panel[...], panel[:count])
     cross = acc[count:]
     gram[...] = acc[:count] + cross + cross.T
 
 
 def snaps_kernel(first, second, modes_panel, modes_gram, panel, packed):
-    snaps, half, _ = first.shape
-    modes = modes_gram.shape[0]
+    snaps, modes = panel.shape[0] // 2, modes_gram.shape[0]
+    half = first.shape[0] // snaps
     for h, part in enumerate((first, second)):
         for i in range(half):
-            high, low = split(part[:, i, :])
+            high, low = split(part[pl.ds(i, snaps, stride=half), :])
             at = (h * half + i) * LANES
             panel[:snaps, at:at + LANES] = high
             panel[snaps:, at:at + LANES] = low
@@ -173,7 +162,7 @@
     ws = jnp.concatenate([w_high[:, modes:], w_low[:, modes:]], axis=0)
     both_w = jnp.concatenate([wm, wm, ws, ws], axis=1)
     chunks = sems.shape[0]
-    slabs = buf.shape[1]
+    slabs = buf.shape[0] // width
     step = slabs // chunks
     copies = []
     for k in range(chunks):
@@ -182,12 +171,10 @@
         res = jnp.dot(both_w, right, preferred_element_type=F32)
         res = res[:width] + res[width:]
         for i in range(step):
-            buf[:, k * step + i, :] = res[:, i * LANES:(i + 1) * LANES]
-        part = (slice(None), pl.ds(k * step, step))
-        copies.append(pltpu.make_async_copy(buf.at[part], out.at[part], sems.at[k]))
-        copies[-1].start()
-    for copy in copies:
-        copy.wait()
+            buf[pl.ds(k * step + i, width, stride=slabs), :] = res[:, i * LANES:(i + 1) * LANES]
+    copy = pltpu.make_async_copy(buf, out, sems.at[0])
+    copy.start()
+    copy.wait()
 
 
 def per_device(basis_modes, weights, snapshots):
@@ -200,10 +187,10 @@
     cells = rows * cols * lax.axis_size("srv") * cores
     core = lax.axis_index("grp")
     fields = basis_modes.reshape(modes, rows, tiles, LANES).transpose(0, 2, 1, 3)
-    fields = fields.reshape(modes, slabs, LANES)
+    fields = fields.reshape(modes * slabs, LANES)
     own = snapshots.reshape(snaps, cores, rows, tiles // cores, LANES).transpose(0, 3, 1, 2, 4)
-    keep = jnp.where(core == 0, own[:, :, 0], own[:, :, 1]).reshape(snaps, slabs // cores, LANES)
-    send = jnp.where(core == 0, own[:, :, 1], own[:, :, 0]).reshape(snaps, slabs // cores, LANES)
+    keep = jnp.where(core == 0, own[:, :, 0], own[:, :, 1]).reshape(snaps * slabs // cores, LANES)
+    send = jnp.where(core == 0, own[:, :, 1], own[:, :, 0]).reshape(snaps * slabs // cores, LANES)
     got = lax.ppermute(send, "grp", [(0, 1), (1, 0)])
     first = jnp.where(core == 0, keep, got)
     second = jnp.where(core == 0, got, keep)
@@ -215,9 +202,8 @@
             jax.ShapeDtypeStruct((2 * modes, slabs * LANES), BF16),
             jax.ShapeDtypeStruct((modes, modes), F32),
         ),
-        in_specs=[ANY],
+        in_specs=[VMEM],
         out_specs=(VMEM, VMEM),
-        scratch_shapes=[pltpu.VMEM((modes, slabs, LANES), F32), pltpu.SemaphoreType.DMA((chunk,))],
         cost_estimate=pl.CostEstimate(flops=10**8, bytes_accessed=fields.size * 4, transcendentals=0),
         compiler_params=PARAMS,
         name="modes_gram",
@@ -238,14 +224,14 @@
     new_modes, factor = pl.pallas_call(
         functools.partial(apply_kernel, cells),
         out_shape=(
-            jax.ShapeDtypeStruct((width, slabs, LANES), F32),
+            jax.ShapeDtypeStruct((width * slabs, LANES), F32),
             jax.ShapeDtypeStruct((width, width), F32),
         ),
         in_specs=[VMEM] * 4,
         out_specs=(ANY, VMEM),
         scratch_shapes=[
             pltpu.VMEM((width, LANES), F32),
-            pltpu.VMEM((width, slabs, LANES), F32),
+            pltpu.VMEM((width * slabs, LANES), F32),
             pltpu.SemaphoreType.DMA((chunk,)),
         ],
         compiler_params=PARAMS,

time: 32.4 us -> 27.3 us (0.84)
  Pallas kernels: 12.8 us -> 7.73 us
    pallas_call x1, Pallas kernels: 5.38 us -> 1.03 us  [per_device(): pl.pallas_call(modes_kernel, out_shape=(jax.ShapeDtypeStruct((2 * modes,...]
    pallas_call x1, Pallas kernels: 1.48 us -> 0.86 us  [per_device(): pl.pallas_call(snaps_kernel, out_shape=(jax.ShapeDtypeStruct((2 * snaps,...]
  transfers between devices with their start and end apart: 6 -> 6, of which waited for: 5 -> 5; matrix products, arithmetic and copies ran while one was open for 1% -> 1% of each run, Pallas kernels for 17% -> 4%
where the time goes in v3:
time: 27.3 us; the launch traced here: 27.1 us
  starting transfers between devices  9.92 us (36%)
  Pallas kernels  7.73 us (28%)
  waiting for transfers between devices  6.67 us (24%)
  local copies, waits for them, and re-layouts  2.01 us (7%)
  between operations  0.72 us (3%)
    ppermute x5, starting transfers between devices, total(): lax.ppermute(value, AXES, [(i, i ^ mask) for i in range(count)])  9.37 us
    ppermute x5, waiting for transfers between devices, total(): lax.ppermute(value, AXES, [(i, i ^ mask) for i in range(count)])  6.66 us
    pallas_call x1, Pallas kernels, per_device(): pl.pallas_call(functools.partial(apply_kernel, cells), out_shape=(jax.Sha...  5.84 us
    unnamed x5, local copies, waits for them, and re-layouts  1.53 us
    pallas_call x1, Pallas kernels, per_device(): pl.pallas_call(modes_kernel, out_shape=(jax.ShapeDtypeStruct((2 * modes,...  1.03 us
    pallas_call x1, Pallas kernels, per_device(): pl.pallas_call(snaps_kernel, out_shape=(jax.ShapeDtypeStruct((2 * snaps,...  0.86 us
    ppermute x1, starting transfers between devices, per_device(): got = lax.ppermute(send, 'grp', [(0, 1), (1, 0)])  0.56 us
  transfers between devices with their start and end apart: 6, of which 5 were waited for; matrix products, arithmetic and copies ran while one was open for 1% of the time, Pallas kernels for 4%

profile of v3, /device:TPU:0, one launch (start us, length us, event | category | flops | bytes accessed | tf_op | source)
XLA Modules:
  0.0 27.1 jit_solution(2391909143772903818)
XLA Ops:
  0.6 1.1 %copy.9 = f32[16,4,1536]{2,0,1:T(8,128)S(1)} copy(f32[16,4,1536]{2,1,0:T(4,128)} %param.5) | data formatting | bytes 786432 | tf_op args[2]
  1.8 0.0 copy-start
  1.8 0.1 reshape.29
  1.9 0.2 copy.11
  2.1 0.6 %collective-permute-start = (f32[384,128]{1,0:T(8,128)S(1)}, f32[384,128]{1,0:T(8,128)S(1)}, u32[]{:S(2)}, u32[]{:S(2)}) collective-permute-start(f32[384,128]{1,0:T(8,128)S(1)} %bitcast.20), channel_id=1, source_target_pairs={{0,1},{1,0},{2,3},{3,2},{4,5},{5,4},{6,7},{7,6},{8,9},{9,8},{10,11... | collective-permute-start | bytes 589832 | tf_op jit(solution)/shard_map/ppermute | solution.py:194
  2.6 0.2 copy.10
  2.8 0.4 %copy-done = f32[64,2,3072]{2,1,0:T(2,128)S(1)} copy-done((f32[64,2,3072]{2,1,0:T(2,128)S(1)}, f32[64,2,3072]{2,1,0:T(2,128)}, u32[]{:S(2)}) %copy-start) | copy-done | bytes 1572888
  3.2 1.0 %modes_gram.1 = (bf16[128,6144]{1,0:T(8,128)(2,1)S(1)}, f32[64,64]{1,0:T(8,128)S(1)}) custom-call(f32[3072,128]{1,0:T(8,128)S(1)} %bitcast.17), custom_call_target="tpu_custom_call" | custom-call | flops 100000000 | bytes 1572864 | tf_op jit(solution)/shard_map/modes_gram/pallas_call | solution.py:199
  4.2 0.0 copy-start.1
  4.2 0.0 collective-permute-done
  4.3 0.9 %snaps_gram.1 = (bf16[32,6144]{1,0:T(8,128)(2,1)S(1)}, f32[40,128]{1,0:T(8,128)S(1)}) custom-call(f32[384,128]{1,0:T(8,128)S(1)} %get-tuple-element.17.first, f32[384,128]{1,0:T(8,128)S(1)} %get-tuple-element.16.second, bf16[128,6144]{1,0:T(8,128)(2,1)S(1)} %get-tuple-element.8.modes_panel, f32[64,64]{1,0:T(8,128)S(1)} %get-tuple-element.9.modes_gram), custom_call_target="tpu_custom_call" | custom-call | tf_op jit(solution)/shard_map/snaps_gram/pallas_call | solution.py:211
  5.1 0.5 %collective-permute-start.1 = (f32[40,128]{1,0:T(8,128)S(1)}, f32[40,128]{1,0:T(8,128)S(1)}, u32[]{:S(2)}, u32[]{:S(2)}) collective-permute-start(f32[40,128]{1,0:T(8,128)S(1)} %get-tuple-element.10), channel_id=1, source_target_pairs={{0,1},{1,0},{2,3},{3,2},{4,5},{5,4},{6,7},{7,6},{8,9},{9,8},{10,11... | collective-permute-start | bytes 61448 | tf_op jit(solution)/shard_map/ppermute | solution.py:25
  5.6 0.8 %collective-permute-done.1 = f32[40,128]{1,0:T(8,128)S(1)} collective-permute-done((f32[40,128]{1,0:T(8,128)S(1)}, f32[40,128]{1,0:T(8,128)S(1)}, u32[]{:S(2)}, u32[]{:S(2)}) %collective-permute-start.1) | collective-permute-done | bytes 20512 | tf_op jit(solution)/shard_map/ppermute | solution.py:25
  6.5 2.6 %collective-permute-start.2 = (f32[40,128]{1,0:T(8,128)S(1)}, f32[40,128]{1,0:T(8,128)S(1)}, u32[]{:S(2)}, u32[]{:S(2)}) collective-permute-start(f32[40,128]{1,0:T(8,128)S(1)} %add.17), channel_id=1, source_target_pairs={{0,3},{1,2},{2,1},{3,0},{4,7},{5,6},{6,5},{7,4},{8,11},{9,10},{10,... | collective-permute-start | bytes 61448 | tf_op jit(solution)/shard_map/ppermute | solution.py:25
  9.1 1.5 %collective-permute-done.2 = f32[40,128]{1,0:T(8,128)S(1)} collective-permute-done((f32[40,128]{1,0:T(8,128)S(1)}, f32[40,128]{1,0:T(8,128)S(1)}, u32[]{:S(2)}, u32[]{:S(2)}) %collective-permute-start.2) | collective-permute-done | bytes 20512 | tf_op jit(solution)/shard_map/ppermute | solution.py:25
  10.6 1.8 %collective-permute-start.3 = (f32[40,128]{1,0:T(8,128)S(1)}, f32[40,128]{1,0:T(8,128)S(1)}, u32[]{:S(2)}, u32[]{:S(2)}) collective-permute-start(f32[40,128]{1,0:T(8,128)S(1)} %add.18), channel_id=1, source_target_pairs={{0,5},{1,4},{2,7},{3,6},{4,1},{5,0},{6,3},{7,2},{8,13},{9,12},{10,... | collective-permute-start | bytes 61448 | tf_op jit(solution)/shard_map/ppermute | solution.py:25
  12.3 1.5 %collective-permute-done.3 = f32[40,128]{1,0:T(8,128)S(1)} collective-permute-done((f32[40,128]{1,0:T(8,128)S(1)}, f32[40,128]{1,0:T(8,128)S(1)}, u32[]{:S(2)}, u32[]{:S(2)}) %collective-permute-start.3) | collective-permute-done | bytes 20512 | tf_op jit(solution)/shard_map/ppermute | solution.py:25
  13.8 1.8 %collective-permute-start.4 = (f32[40,128]{1,0:T(8,128)S(1)}, f32[40,128]{1,0:T(8,128)S(1)}, u32[]{:S(2)}, u32[]{:S(2)}) collective-permute-start(f32[40,128]{1,0:T(8,128)S(1)} %add.19), channel_id=1, source_target_pairs={{0,9},{1,8},{2,11},{3,10},{4,13},{5,12},{6,15},{7,14},{8,1},{9,0},... | collective-permute-start | bytes 61448 | tf_op jit(solution)/shard_map/ppermute | solution.py:25
  15.6 1.5 %collective-permute-done.4 = f32[40,128]{1,0:T(8,128)S(1)} collective-permute-done((f32[40,128]{1,0:T(8,128)S(1)}, f32[40,128]{1,0:T(8,128)S(1)}, u32[]{:S(2)}, u32[]{:S(2)}) %collective-permute-start.4) | collective-permute-done | bytes 20512 | tf_op jit(solution)/shard_map/ppermute | solution.py:25
  17.1 2.7 %collective-permute-start.5 = (f32[40,128]{1,0:T(8,128)S(1)}, f32[40,128]{1,0:T(8,128)S(1)}, u32[]{:S(2)}, u32[]{:S(2)}) collective-permute-start(f32[40,128]{1,0:T(8,128)S(1)} %add.20), channel_id=1, source_target_pairs={{0,17},{1,16},{2,19},{3,18},{4,21},{5,20},{6,23},{7,22},{8,25},{9,... | collective-permute-start | bytes 61448 | tf_op jit(solution)/shard_map/ppermute | solution.py:25
  19.8 0.0 copy-done.1
  19.8 0.1 copy.13.scale
  19.9 1.4 %collective-permute-done.5 = f32[40,128]{1,0:T(8,128)S(1)} collective-permute-done((f32[40,128]{1,0:T(8,128)S(1)}, f32[40,128]{1,0:T(8,128)S(1)}, u32[]{:S(2)}, u32[]{:S(2)}) %collective-permute-start.5) | collective-permute-done | bytes 20512 | tf_op jit(solution)/shard_map/ppermute | solution.py:25
  21.3 5.8 %factor_apply.1 = (f32[3840,128]{1,0:T(8,128)}, f32[80,80]{1,0:T(8,128)}) custom-call(f32[40,128]{1,0:T(8,128)S(1)} %add.21.packed, f32[80,1]{1,0:T(8,128)S(1)} %copy.13.scale, bf16[128,6144]{1,0:T(8,128)(2,1)S(1)} %get-tuple-element.8.modes_panel, bf16[32,6144]{1,0:T(8,128)(2,1)S(1)} %get-tuple-element.11.snaps_panel), custom_call_target="tpu_custom_call" | custom-call | tf_op jit(solution)/shard_map/factor_apply/pallas_call | solution.py:224
  (8 shorter events, 0.1 us)
Async XLA Ops:
  1.8 1.4 %copy-start = (f32[64,2,3072]{2,1,0:T(2,128)S(1)}, f32[64,2,3072]{2,1,0:T(2,128)}, u32[]{:S(2)}) copy-start(f32[64,2,3072]{2,1,0:T(2,128)} %param.3) | copy-start | bytes 4718596
  2.1 2.2 %collective-permute-start = (f32[384,128]{1,0:T(8,128)S(1)}, f32[384,128]{1,0:T(8,128)S(1)}, u32[]{:S(2)}, u32[]{:S(2)}) collective-permute-start(f32[384,128]{1,0:T(8,128)S(1)} %bitcast.20), channel_id=1, source_target_pairs={{0,1},{1,0},{2,3},{3,2},{4,5},{5,4},{6,7},{7,6},{8,9},{9,8},{10,11... | collective-permute-start | bytes 589832 | tf_op jit(solution)/shard_map/ppermute | solution.py:194
  4.2 15.6 %copy-start.1 = (f32[64]{0:T(128)S(1)}, f32[64]{0:T(128)}, u32[]{:S(2)}) copy-start(f32[64]{0:T(128)} %param.4) | copy-start | bytes 772
  5.1 1.3 %collective-permute-start.1 = (f32[40,128]{1,0:T(8,128)S(1)}, f32[40,128]{1,0:T(8,128)S(1)}, u32[]{:S(2)}, u32[]{:S(2)}) collective-permute-start(f32[40,128]{1,0:T(8,128)S(1)} %get-tuple-element.10), channel_id=1, source_target_pairs={{0,1},{1,0},{2,3},{3,2},{4,5},{5,4},{6,7},{7,6},{8,9},{9,8},{10,11... | collective-permute-start | bytes 61448 | tf_op jit(solution)/shard_map/ppermute | solution.py:25
  6.5 4.1 %collective-permute-start.2 = (f32[40,128]{1,0:T(8,128)S(1)}, f32[40,128]{1,0:T(8,128)S(1)}, u32[]{:S(2)}, u32[]{:S(2)}) collective-permute-start(f32[40,128]{1,0:T(8,128)S(1)} %add.17), channel_id=1, source_target_pairs={{0,3},{1,2},{2,1},{3,0},{4,7},{5,6},{6,5},{7,4},{8,11},{9,10},{10,... | collective-permute-start | bytes 61448 | tf_op jit(solution)/shard_map/ppermute | solution.py:25
  10.6 3.2 %collective-permute-start.3 = (f32[40,128]{1,0:T(8,128)S(1)}, f32[40,128]{1,0:T(8,128)S(1)}, u32[]{:S(2)}, u32[]{:S(2)}) collective-permute-start(f32[40,128]{1,0:T(8,128)S(1)} %add.18), channel_id=1, source_target_pairs={{0,5},{1,4},{2,7},{3,6},{4,1},{5,0},{6,3},{7,2},{8,13},{9,12},{10,... | collective-permute-start | bytes 61448 | tf_op jit(solution)/shard_map/ppermute | solution.py:25
  13.8 3.3 %collective-permute-start.4 = (f32[40,128]{1,0:T(8,128)S(1)}, f32[40,128]{1,0:T(8,128)S(1)}, u32[]{:S(2)}, u32[]{:S(2)}) collective-permute-start(f32[40,128]{1,0:T(8,128)S(1)} %add.19), channel_id=1, source_target_pairs={{0,9},{1,8},{2,11},{3,10},{4,13},{5,12},{6,15},{7,14},{8,1},{9,0},... | collective-permute-start | bytes 61448 | tf_op jit(solution)/shard_map/ppermute | solution.py:25
  17.1 4.2 %collective-permute-start.5 = (f32[40,128]{1,0:T(8,128)S(1)}, f32[40,128]{1,0:T(8,128)S(1)}, u32[]{:S(2)}, u32[]{:S(2)}) collective-permute-start(f32[40,128]{1,0:T(8,128)S(1)} %add.20), channel_id=1, source_target_pairs={{0,17},{1,16},{2,19},{3,18},{4,21},{5,20},{6,23},{7,22},{8,25},{9,... | collective-permute-start | bytes 61448 | tf_op jit(solution)/shard_map/ppermute | solution.py:25

commit v4 on v3

--- a/solution.py
+++ b/solution.py
@@ -2,6 +2,7 @@
 import jax
 import jax.numpy as jnp
 from jax import lax
+from jax.experimental.layout import Layout, with_layout_constraint
 from jax.experimental import pallas as pl
 from jax.experimental.pallas import tpu as pltpu
 from jax.sharding import PartitionSpec as P
@@ -47,18 +48,30 @@
     gram[...] = acc[:count] + cross + cross.T
 
 
-def snaps_kernel(first, second, modes_panel, modes_gram, panel, packed):
+def pick_kernel(rows, snaps, keep, send):
+    core = lax.axis_index("grp")
+    count = keep.shape[0] // rows
+    stride = snaps.shape[0] // count
+    for r in range(rows):
+        at = slice(r * count, (r + 1) * count)
+        keep[at] = snaps[pl.ds(core * rows + r, count, stride=stride), :]
+        send[at] = snaps[pl.ds((1 - core) * rows + r, count, stride=stride), :]
+
+
+def snaps_kernel(rows, first, second, modes_panel, modes_gram, panel, packed):
     snaps, modes = panel.shape[0] // 2, modes_gram.shape[0]
-    half = first.shape[0] // snaps
+    tiles = first.shape[0] // (snaps * rows)
     for h, part in enumerate((first, second)):
-        for i in range(half):
-            high, low = split(part[pl.ds(i, snaps, stride=half), :])
-            at = (h * half + i) * LANES
+        for i in range(tiles * rows):
+            start = (i % rows) * snaps * tiles + i // rows
+            high, low = split(part[pl.ds(start, snaps, stride=tiles), :])
+            at = (h * tiles * rows + i) * LANES
             panel[:snaps, at:at + LANES] = high
             panel[snaps:, at:at + LANES] = low
-    with_modes = rows_times_rows(panel[...], modes_panel[...])
+    with_modes = rows_times_rows(modes_panel[...], panel[...])
     own = rows_times_rows(panel[...], panel[:snaps])
-    low_row = (with_modes[:snaps, :modes] + with_modes[:snaps, modes:]) + with_modes[snaps:, :modes]
+    top = with_modes[:modes]
+    low_row = (top[:, :snaps] + top[:, snaps:] + with_modes[modes:, :snaps]).T
     own = own[:snaps] + own[snaps:] + own[snaps:].T
     width = modes + snaps
     mid = width // 2
@@ -162,7 +175,8 @@
     ws = jnp.concatenate([w_high[:, modes:], w_low[:, modes:]], axis=0)
     both_w = jnp.concatenate([wm, wm, ws, ws], axis=1)
     chunks = sems.shape[0]
-    slabs = buf.shape[0] // width
+    slabs = buf.shape[1]
+    flat = buf.reshape(width * slabs, LANES)
     step = slabs // chunks
     copies = []
     for k in range(chunks):
@@ -171,10 +185,12 @@
         res = jnp.dot(both_w, right, preferred_element_type=F32)
         res = res[:width] + res[width:]
         for i in range(step):
-            buf[pl.ds(k * step + i, width, stride=slabs), :] = res[:, i * LANES:(i + 1) * LANES]
-    copy = pltpu.make_async_copy(buf, out, sems.at[0])
-    copy.start()
-    copy.wait()
+            flat[pl.ds(k * step + i, width, stride=slabs), :] = res[:, i * LANES:(i + 1) * LANES]
+        part = (slice(None), pl.ds(k * step, step))
+        copies.append(pltpu.make_async_copy(buf.at[part], out.at[part], sems.at[k]))
+        copies[-1].start()
+    for copy in copies:
+        copy.wait()
 
 
 def per_device(basis_modes, weights, snapshots):
@@ -188,9 +204,18 @@
     core = lax.axis_index("grp")
     fields = basis_modes.reshape(modes, rows, tiles, LANES).transpose(0, 2, 1, 3)
     fields = fields.reshape(modes * slabs, LANES)
-    own = snapshots.reshape(snaps, cores, rows, tiles // cores, LANES).transpose(0, 3, 1, 2, 4)
-    keep = jnp.where(core == 0, own[:, :, 0], own[:, :, 1]).reshape(snaps * slabs // cores, LANES)
-    send = jnp.where(core == 0, own[:, :, 1], own[:, :, 0]).reshape(snaps * slabs // cores, LANES)
+    own = snapshots.reshape(snaps, cores * rows, tiles // cores, LANES)
+    own = with_layout_constraint(own, Layout((0, 2, 1, 3))).transpose(0, 2, 1, 3)
+    own = own.reshape(snaps * tiles * rows, LANES)
+    part = jax.ShapeDtypeStruct((own.shape[0] // cores, LANES), F32)
+    keep, send = pl.pallas_call(
+        functools.partial(pick_kernel, rows),
+        out_shape=(part, part),
+        in_specs=[VMEM],
+        out_specs=(VMEM, VMEM),
+        compiler_params=PARAMS,
+        name="pick_rows",
+    )(own)
     got = lax.ppermute(send, "grp", [(0, 1), (1, 0)])
     first = jnp.where(core == 0, keep, got)
     second = jnp.where(core == 0, got, keep)
@@ -209,7 +234,7 @@
         name="modes_gram",
     )(fields)
     snaps_panel, packed = pl.pallas_call(
-        snaps_kernel,
+        functools.partial(snaps_kernel, rows),
         out_shape=(
             jax.ShapeDtypeStruct((2 * snaps, slabs * LANES), BF16),
             jax.ShapeDtypeStruct((width // 2, LANES), F32),
@@ -224,14 +249,14 @@
     new_modes, factor = pl.pallas_call(
         functools.partial(apply_kernel, cells),
         out_shape=(
-            jax.ShapeDtypeStruct((width * slabs, LANES), F32),
+            jax.ShapeDtypeStruct((width, slabs, LANES), F32),
             jax.ShapeDtypeStruct((width, width), F32),
         ),
         in_specs=[VMEM] * 4,
         out_specs=(ANY, VMEM),
         scratch_shapes=[
             pltpu.VMEM((width, LANES), F32),
-            pltpu.VMEM((width * slabs, LANES), F32),
+            pltpu.VMEM((width, slabs, LANES), F32),
             pltpu.SemaphoreType.DMA((chunk,)),
         ],
         compiler_params=PARAMS,

time: 27.3 us -> 27 us (0.989)
  Pallas kernels: 7.73 us -> 7.1 us
  local copies, waits for them, and re-layouts: 2.01 us -> 2.51 us
  starting transfers between devices: 9.92 us -> 9.51 us
  waiting for transfers between devices: 6.67 us -> 6.99 us
    unnamed x5 -> x6, local copies, waits for them, and re-layouts: 1.53 us -> 2.4 us
    pallas_call x1, Pallas kernels: 5.84 us -> 5.29 us  [per_device(): pl.pallas_call(functools.partial(apply_kernel, cells), out_shape=(jax.Sha...]
    ppermute x5, starting transfers between devices: 9.37 us -> 8.95 us  [total(): lax.ppermute(value, AXES, [(i, i ^ mask) for i in range(count)])]
    ppermute x5, waiting for transfers between devices: 6.66 us -> 6.99 us  [total(): lax.ppermute(value, AXES, [(i, i ^ mask) for i in range(count)])]
    select_n x2 -> x0, local copies, waits for them, and re-layouts: 0.31 us -> none  [the longest x1 0.15 us: per_device(): jnp.where(core == 0, own[:, :, 1], own[:, :, 0])]
    pallas_call x1 -> x2, Pallas kernels: 0.86 us -> 0.8 us  [the longest x1 0.77 us: per_device(): pl.pallas_call(functools.partial(snaps_kernel, rows), out_shape=(jax.Shap...]
  transfers between devices with their start and end apart: 6 -> 6, of which waited for: 5 -> 5; matrix products, arithmetic and copies ran while one was open for 1% -> 0% of each run, Pallas kernels for 4% -> 4%
where the time goes in v4:
time: 27 us; the launch traced here: 26.9 us
  starting transfers between devices  9.51 us (35%)
  Pallas kernels  7.1 us (26%)
  waiting for transfers between devices  6.99 us (26%)
  local copies, waits for them, and re-layouts  2.51 us (9%)
  between operations  0.69 us (3%)
    ppermute x5, starting transfers between devices, total(): lax.ppermute(value, AXES, [(i, i ^ mask) for i in range(count)])  8.95 us
    ppermute x5, waiting for transfers between devices, total(): lax.ppermute(value, AXES, [(i, i ^ mask) for i in range(count)])  6.99 us
    pallas_call x1, Pallas kernels, per_device(): pl.pallas_call(functools.partial(apply_kernel, cells), out_shape=(jax.Sha...  5.29 us
    unnamed x6, local copies, waits for them, and re-layouts  2.4 us
    pallas_call x1, Pallas kernels, per_device(): pl.pallas_call(modes_kernel, out_shape=(jax.ShapeDtypeStruct((2 * modes,...  1.02 us
    pallas_call x1, Pallas kernels, per_device(): pl.pallas_call(functools.partial(snaps_kernel, rows), out_shape=(jax.Shap...  0.77 us
    ppermute x1, starting transfers between devices, per_device(): got = lax.ppermute(send, 'grp', [(0, 1), (1, 0)])  0.56 us
  transfers between devices with their start and end apart: 6, of which 5 were waited for; matrix products, arithmetic and copies ran while one was open for 0% of the time, Pallas kernels for 4%

profile of v4, /device:TPU:0, one launch (start us, length us, event | category | flops | bytes accessed | tf_op | source)
XLA Modules:
  0.0 26.9 jit_solution(12166199032802980540)
XLA Ops:
  0.6 0.0 copy-start.1
  0.6 1.0 %copy-done.1 = f32[16,4,1536]{2,1,0:T(4,128)S(1)} copy-done((f32[16,4,1536]{2,1,0:T(4,128)S(1)}, f32[16,4,1536]{2,1,0:T(4,128)}, u32[]{:S(2)}) %copy-start.1) | copy-done | bytes 393240
  1.7 0.6 %collective-permute-start = (f32[384,128]{1,0:T(8,128)S(1)}, f32[384,128]{1,0:T(8,128)S(1)}, u32[]{:S(2)}, u32[]{:S(2)}) collective-permute-start(f32[384,128]{1,0:T(8,128)S(1)} %get-tuple-element.11), channel_id=1, source_target_pairs={{0,1},{1,0},{2,3},{3,2},{4,5},{5,4},{6,7},{7,6},{8,9},{9,8},{10,11... | collective-permute-start | bytes 589832 | tf_op jit(solution)/shard_map/ppermute | solution.py:219
  2.2 0.0 copy-start
  2.2 1.4 %copy-done = f32[64,2,3072]{2,1,0:T(2,128)S(1)} copy-done((f32[64,2,3072]{2,1,0:T(2,128)S(1)}, f32[64,2,3072]{2,1,0:T(2,128)}, u32[]{:S(2)}) %copy-start) | copy-done | bytes 1572888
  3.6 1.0 %modes_gram.1 = (bf16[128,6144]{1,0:T(8,128)(2,1)S(1)}, f32[64,64]{1,0:T(8,128)S(1)}) custom-call(f32[3072,128]{1,0:T(8,128)S(1)} %bitcast.17), custom_call_target="tpu_custom_call" | custom-call | flops 100000000 | bytes 1572864 | tf_op jit(solution)/shard_map/modes_gram/pallas_call | solution.py:224
  4.6 0.0 copy-start.2
  4.7 0.0 collective-permute-done
  4.7 0.8 %snaps_gram.1 = (bf16[32,6144]{1,0:T(8,128)(2,1)S(1)}, f32[40,128]{1,0:T(8,128)S(1)}) custom-call(f32[384,128]{1,0:T(8,128)S(1)} %get-tuple-element.19.first, f32[384,128]{1,0:T(8,128)S(1)} %get-tuple-element.18.second, bf16[128,6144]{1,0:T(8,128)(2,1)S(1)} %get-tuple-element.12.modes_panel, f32[64,64]{1,0:T(8,128)S(1)} %get-tuple-element.13.modes_gram), custom_call_target="tpu_custom_call" | custom-call | tf_op jit(solution)/shard_map/snaps_gram/pallas_call | solution.py:236
  5.5 0.1 collective-permute-start.1
  5.6 1.2 %collective-permute-done.1 = f32[40,128]{1,0:T(8,128)S(1)} collective-permute-done((f32[40,128]{1,0:T(8,128)S(1)}, f32[40,128]{1,0:T(8,128)S(1)}, u32[]{:S(2)}, u32[]{:S(2)}) %collective-permute-start.1) | collective-permute-done | bytes 20512 | tf_op jit(solution)/shard_map/ppermute | solution.py:26
  6.7 2.6 %collective-permute-start.2 = (f32[40,128]{1,0:T(8,128)S(1)}, f32[40,128]{1,0:T(8,128)S(1)}, u32[]{:S(2)}, u32[]{:S(2)}) collective-permute-start(f32[40,128]{1,0:T(8,128)S(1)} %add.17), channel_id=1, source_target_pairs={{0,3},{1,2},{2,1},{3,0},{4,7},{5,6},{6,5},{7,4},{8,11},{9,10},{10,... | collective-permute-start | bytes 61448 | tf_op jit(solution)/shard_map/ppermute | solution.py:26
  9.3 1.5 %collective-permute-done.2 = f32[40,128]{1,0:T(8,128)S(1)} collective-permute-done((f32[40,128]{1,0:T(8,128)S(1)}, f32[40,128]{1,0:T(8,128)S(1)}, u32[]{:S(2)}, u32[]{:S(2)}) %collective-permute-start.2) | collective-permute-done | bytes 20512 | tf_op jit(solution)/shard_map/ppermute | solution.py:26
  10.8 1.8 %collective-permute-start.3 = (f32[40,128]{1,0:T(8,128)S(1)}, f32[40,128]{1,0:T(8,128)S(1)}, u32[]{:S(2)}, u32[]{:S(2)}) collective-permute-start(f32[40,128]{1,0:T(8,128)S(1)} %add.18), channel_id=1, source_target_pairs={{0,5},{1,4},{2,7},{3,6},{4,1},{5,0},{6,3},{7,2},{8,13},{9,12},{10,... | collective-permute-start | bytes 61448 | tf_op jit(solution)/shard_map/ppermute | solution.py:26
  12.6 1.5 %collective-permute-done.3 = f32[40,128]{1,0:T(8,128)S(1)} collective-permute-done((f32[40,128]{1,0:T(8,128)S(1)}, f32[40,128]{1,0:T(8,128)S(1)}, u32[]{:S(2)}, u32[]{:S(2)}) %collective-permute-start.3) | collective-permute-done | bytes 20512 | tf_op jit(solution)/shard_map/ppermute | solution.py:26
  14.1 1.8 %collective-permute-start.4 = (f32[40,128]{1,0:T(8,128)S(1)}, f32[40,128]{1,0:T(8,128)S(1)}, u32[]{:S(2)}, u32[]{:S(2)}) collective-permute-start(f32[40,128]{1,0:T(8,128)S(1)} %add.19), channel_id=1, source_target_pairs={{0,9},{1,8},{2,11},{3,10},{4,13},{5,12},{6,15},{7,14},{8,1},{9,0},... | collective-permute-start | bytes 61448 | tf_op jit(solution)/shard_map/ppermute | solution.py:26
  15.8 1.5 %collective-permute-done.4 = f32[40,128]{1,0:T(8,128)S(1)} collective-permute-done((f32[40,128]{1,0:T(8,128)S(1)}, f32[40,128]{1,0:T(8,128)S(1)}, u32[]{:S(2)}, u32[]{:S(2)}) %collective-permute-start.4) | collective-permute-done | bytes 20512 | tf_op jit(solution)/shard_map/ppermute | solution.py:26
  17.3 2.7 %collective-permute-start.5 = (f32[40,128]{1,0:T(8,128)S(1)}, f32[40,128]{1,0:T(8,128)S(1)}, u32[]{:S(2)}, u32[]{:S(2)}) collective-permute-start(f32[40,128]{1,0:T(8,128)S(1)} %add.20), channel_id=1, source_target_pairs={{0,17},{1,16},{2,19},{3,18},{4,21},{5,20},{6,23},{7,22},{8,25},{9,... | collective-permute-start | bytes 61448 | tf_op jit(solution)/shard_map/ppermute | solution.py:26
  20.1 0.0 copy-done.2
  20.1 0.1 copy.6.scale
  20.2 1.4 %collective-permute-done.5 = f32[40,128]{1,0:T(8,128)S(1)} collective-permute-done((f32[40,128]{1,0:T(8,128)S(1)}, f32[40,128]{1,0:T(8,128)S(1)}, u32[]{:S(2)}, u32[]{:S(2)}) %collective-permute-start.5) | collective-permute-done | bytes 20512 | tf_op jit(solution)/shard_map/ppermute | solution.py:26
  21.6 5.3 %factor_apply.1 = (f32[80,48,128]{2,1,0:T(8,128)}, f32[80,80]{1,0:T(8,128)}) custom-call(f32[40,128]{1,0:T(8,128)S(1)} %add.21.packed, f32[80,1]{1,0:T(8,128)S(1)} %copy.6.scale, bf16[128,6144]{1,0:T(8,128)(2,1)S(1)} %get-tuple-element.12.modes_panel, bf16[32,6144]{1,0:T(8,128)(2,1)S(1)} %get-tuple-element.15.snaps_panel), custom_call_target="tpu_custom_call" | custom-call | tf_op jit(solution)/shard_map/factor_apply/pallas_call | solution.py:249
  (8 shorter events, 0.1 us)
Async XLA Ops:
  0.6 1.0 %copy-start.1 = (f32[16,4,1536]{2,1,0:T(4,128)S(1)}, f32[16,4,1536]{2,1,0:T(4,128)}, u32[]{:S(2)}) copy-start(f32[16,4,1536]{2,1,0:T(4,128)} %param.5) | copy-start | bytes 1179652
  1.7 3.0 %collective-permute-start = (f32[384,128]{1,0:T(8,128)S(1)}, f32[384,128]{1,0:T(8,128)S(1)}, u32[]{:S(2)}, u32[]{:S(2)}) collective-permute-start(f32[384,128]{1,0:T(8,128)S(1)} %get-tuple-element.11), channel_id=1, source_target_pairs={{0,1},{1,0},{2,3},{3,2},{4,5},{5,4},{6,7},{7,6},{8,9},{9,8},{10,11... | collective-permute-start | bytes 589832 | tf_op jit(solution)/shard_map/ppermute | solution.py:219
  2.2 1.4 %copy-start = (f32[64,2,3072]{2,1,0:T(2,128)S(1)}, f32[64,2,3072]{2,1,0:T(2,128)}, u32[]{:S(2)}) copy-start(f32[64,2,3072]{2,1,0:T(2,128)} %param.3) | copy-start | bytes 4718596
  4.6 15.4 %copy-start.2 = (f32[64]{0:T(128)S(1)}, f32[64]{0:T(128)}, u32[]{:S(2)}) copy-start(f32[64]{0:T(128)} %param.4) | copy-start | bytes 772
  5.5 1.3 %collective-permute-start.1 = (f32[40,128]{1,0:T(8,128)S(1)}, f32[40,128]{1,0:T(8,128)S(1)}, u32[]{:S(2)}, u32[]{:S(2)}) collective-permute-start(f32[40,128]{1,0:T(8,128)S(1)} %get-tuple-element.14), channel_id=1, source_target_pairs={{0,1},{1,0},{2,3},{3,2},{4,5},{5,4},{6,7},{7,6},{8,9},{9,8},{10,11... | collective-permute-start | bytes 61448 | tf_op jit(solution)/shard_map/ppermute | solution.py:26
  6.7 4.1 %collective-permute-start.2 = (f32[40,128]{1,0:T(8,128)S(1)}, f32[40,128]{1,0:T(8,128)S(1)}, u32[]{:S(2)}, u32[]{:S(2)}) collective-permute-start(f32[40,128]{1,0:T(8,128)S(1)} %add.17), channel_id=1, source_target_pairs={{0,3},{1,2},{2,1},{3,0},{4,7},{5,6},{6,5},{7,4},{8,11},{9,10},{10,... | collective-permute-start | bytes 61448 | tf_op jit(solution)/shard_map/ppermute | solution.py:26
  10.8 3.2 %collective-permute-start.3 = (f32[40,128]{1,0:T(8,128)S(1)}, f32[40,128]{1,0:T(8,128)S(1)}, u32[]{:S(2)}, u32[]{:S(2)}) collective-permute-start(f32[40,128]{1,0:T(8,128)S(1)} %add.18), channel_id=1, source_target_pairs={{0,5},{1,4},{2,7},{3,6},{4,1},{5,0},{6,3},{7,2},{8,13},{9,12},{10,... | collective-permute-start | bytes 61448 | tf_op jit(solution)/shard_map/ppermute | solution.py:26
  14.1 3.3 %collective-permute-start.4 = (f32[40,128]{1,0:T(8,128)S(1)}, f32[40,128]{1,0:T(8,128)S(1)}, u32[]{:S(2)}, u32[]{:S(2)}) collective-permute-start(f32[40,128]{1,0:T(8,128)S(1)} %add.19), channel_id=1, source_target_pairs={{0,9},{1,8},{2,11},{3,10},{4,13},{5,12},{6,15},{7,14},{8,1},{9,0},... | collective-permute-start | bytes 61448 | tf_op jit(solution)/shard_map/ppermute | solution.py:26
  17.3 4.2 %collective-permute-start.5 = (f32[40,128]{1,0:T(8,128)S(1)}, f32[40,128]{1,0:T(8,128)S(1)}, u32[]{:S(2)}, u32[]{:S(2)}) collective-permute-start(f32[40,128]{1,0:T(8,128)S(1)} %add.20), channel_id=1, source_target_pairs={{0,17},{1,16},{2,19},{3,18},{4,21},{5,20},{6,23},{7,22},{8,25},{9,... | collective-permute-start | bytes 61448 | tf_op jit(solution)/shard_map/ppermute | solution.py:26

commit v5 on v4

--- a/solution.py
+++ b/solution.py
@@ -13,6 +13,7 @@
 F32, BF16 = jnp.float32, jnp.bfloat16
 VMEM = pl.BlockSpec(memory_space=pltpu.VMEM)
 ANY = pl.BlockSpec(memory_space=pl.ANY)
+HBM = pl.BlockSpec(memory_space=pltpu.HBM)
 PARAMS = pltpu.CompilerParams(vmem_limit_bytes=16 * 2**20)
 
 
@@ -48,7 +49,10 @@
     gram[...] = acc[:count] + cross + cross.T
 
 
-def pick_kernel(rows, snaps, keep, send):
+def pick_kernel(rows, source, keep, send, snaps, sem):
+    copy = pltpu.make_async_copy(source, snaps, sem)
+    copy.start()
+    copy.wait()
     core = lax.axis_index("grp")
     count = keep.shape[0] // rows
     stride = snaps.shape[0] // count
@@ -58,13 +62,14 @@
         send[at] = snaps[pl.ds((1 - core) * rows + r, count, stride=stride), :]
 
 
-def snaps_kernel(rows, first, second, modes_panel, modes_gram, panel, packed):
+def snaps_kernel(rows, keep, got, modes_panel, modes_gram, panel, packed):
     snaps, modes = panel.shape[0] // 2, modes_gram.shape[0]
-    tiles = first.shape[0] // (snaps * rows)
-    for h, part in enumerate((first, second)):
+    tiles = keep.shape[0] // (snaps * rows)
+    kept = [lax.axis_index("grp") == h for h in (0, 1)]
+    for h in (0, 1):
         for i in range(tiles * rows):
-            start = (i % rows) * snaps * tiles + i // rows
-            high, low = split(part[pl.ds(start, snaps, stride=tiles), :])
+            place = pl.ds((i % rows) * snaps * tiles + i // rows, snaps, stride=tiles)
+            high, low = split(jnp.where(kept[h], keep[place, :], got[place, :]))
             at = (h * tiles * rows + i) * LANES
             panel[:snaps, at:at + LANES] = high
             panel[snaps:, at:at + LANES] = low
@@ -201,24 +206,24 @@
     slabs = rows * tiles
     cores = lax.axis_size("grp")
     cells = rows * cols * lax.axis_size("srv") * cores
-    core = lax.axis_index("grp")
     fields = basis_modes.reshape(modes, rows, tiles, LANES).transpose(0, 2, 1, 3)
     fields = fields.reshape(modes * slabs, LANES)
     own = snapshots.reshape(snaps, cores * rows, tiles // cores, LANES)
     own = with_layout_constraint(own, Layout((0, 2, 1, 3))).transpose(0, 2, 1, 3)
     own = own.reshape(snaps * tiles * rows, LANES)
+    own = pltpu.with_memory_space_constraint(own, pltpu.HBM)
     part = jax.ShapeDtypeStruct((own.shape[0] // cores, LANES), F32)
     keep, send = pl.pallas_call(
         functools.partial(pick_kernel, rows),
         out_shape=(part, part),
-        in_specs=[VMEM],
+        in_specs=[HBM],
         out_specs=(VMEM, VMEM),
-        compiler_params=PARAMS,
+        scratch_shapes=[pltpu.VMEM(own.shape, F32), pltpu.SemaphoreType.DMA],
+        compiler_params=PARAMS,
+        cost_estimate=pl.CostEstimate(flops=10**9, bytes_accessed=own.size * 8, transcendentals=0),
         name="pick_rows",
     )(own)
     got = lax.ppermute(send, "grp", [(0, 1), (1, 0)])
-    first = jnp.where(core == 0, keep, got)
-    second = jnp.where(core == 0, got, keep)
 
     chunk = 6
     modes_panel, modes_gram = pl.pallas_call(
@@ -242,8 +247,9 @@
         in_specs=[VMEM] * 4,
         out_specs=(VMEM, VMEM),
         compiler_params=PARAMS,
+        cost_estimate=pl.CostEstimate(flops=10**8, bytes_accessed=10**6, transcendentals=0),
         name="snaps_gram",
-    )(first, second, modes_panel, modes_gram)
+    )(keep, got, modes_panel, modes_gram)
     packed = total(packed)
     scale = jnp.concatenate([weights, jnp.ones((snaps,), F32)])
     new_modes, factor = pl.pallas_call(

time: 27 us -> 25.8 us (0.956)
  local copies, waits for them, and re-layouts: 2.51 us -> 0.11 us
  Pallas kernels: 7.1 us -> 8.25 us
  starting transfers between devices: 9.51 us -> 9.85 us
  waiting for transfers between devices: 6.99 us -> 6.7 us
    unnamed x6 -> x4, local copies, waits for them, and re-layouts: 2.4 us -> 0.01 us
    pallas_call x1, Pallas kernels: 0.03 us -> 1.15 us  [per_device(): pl.pallas_call(functools.partial(pick_kernel, rows), out_shape=(part, par...]
    ppermute x5, starting transfers between devices: 8.95 us -> 9.3 us  [total(): lax.ppermute(value, AXES, [(i, i ^ mask) for i in range(count)])]
    ppermute x5, waiting for transfers between devices: 6.99 us -> 6.66 us  [total(): lax.ppermute(value, AXES, [(i, i ^ mask) for i in range(count)])]
where the time goes in v5:
time: 25.8 us; the launch traced here: 25.6 us
  starting transfers between devices  9.85 us (38%)
  Pallas kernels  8.25 us (32%)
  waiting for transfers between devices  6.7 us (26%)
  between operations  0.67 us (3%)
    ppermute x5, starting transfers between devices, total(): lax.ppermute(value, AXES, [(i, i ^ mask) for i in range(count)])  9.3 us
    ppermute x5, waiting for transfers between devices, total(): lax.ppermute(value, AXES, [(i, i ^ mask) for i in range(count)])  6.66 us
    pallas_call x1, Pallas kernels, per_device(): pl.pallas_call(functools.partial(apply_kernel, cells), out_shape=(jax.Sha...  5.3 us
    pallas_call x1, Pallas kernels, per_device(): pl.pallas_call(functools.partial(pick_kernel, rows), out_shape=(part, par...  1.15 us
    pallas_call x1, Pallas kernels, per_device(): pl.pallas_call(modes_kernel, out_shape=(jax.ShapeDtypeStruct((2 * modes,...  1.02 us
    pallas_call x1, Pallas kernels, per_device(): pl.pallas_call(functools.partial(snaps_kernel, rows), out_shape=(jax.Shap...  0.79 us
    ppermute x1, starting transfers between devices, per_device(): got = lax.ppermute(send, 'grp', [(0, 1), (1, 0)])  0.56 us
  transfers between devices with their start and end apart: 6, of which 5 were waited for; matrix products, arithmetic and copies ran while one was open for 0% of the time, Pallas kernels for 4%

profile of v5, /device:TPU:0, one launch (start us, length us, event | category | flops | bytes accessed | tf_op | source)
XLA Modules:
  0.0 25.6 jit_solution(4142163605816493644)
XLA Ops:
  0.6 0.0 copy-start
  0.6 1.1 %pick_rows.1 = (f32[384,128]{1,0:T(8,128)S(1)}, f32[384,128]{1,0:T(8,128)S(1)}) custom-call(f32[768,128]{1,0:T(8,128)} %bitcast.19), custom_call_target="tpu_custom_call" | custom-call | flops 1000000000 | bytes 786432 | tf_op jit(solution)/shard_map/pick_rows/pallas_call | solution.py:216
  1.8 0.6 %collective-permute-start = (f32[384,128]{1,0:T(8,128)S(1)}, f32[384,128]{1,0:T(8,128)S(1)}, u32[]{:S(2)}, u32[]{:S(2)}) collective-permute-start(f32[384,128]{1,0:T(8,128)S(1)} %get-tuple-element.11), channel_id=1, source_target_pairs={{0,1},{1,0},{2,3},{3,2},{4,5},{5,4},{6,7},{7,6},{8,9},{9,8},{10,11... | collective-permute-start | bytes 589832 | tf_op jit(solution)/shard_map/ppermute | solution.py:226
  2.4 0.0 copy-done
  2.4 0.0 copy-start.1
  2.4 1.0 %modes_gram.1 = (bf16[128,6144]{1,0:T(8,128)(2,1)S(1)}, f32[64,64]{1,0:T(8,128)S(1)}) custom-call(f32[3072,128]{1,0:T(8,128)S(1)} %bitcast.17), custom_call_target="tpu_custom_call" | custom-call | flops 100000000 | bytes 1572864 | tf_op jit(solution)/shard_map/modes_gram/pallas_call | solution.py:229
  3.4 0.0 collective-permute-done.got
  3.4 0.8 %snaps_gram.1 = (bf16[32,6144]{1,0:T(8,128)(2,1)S(1)}, f32[40,128]{1,0:T(8,128)S(1)}) custom-call(f32[384,128]{1,0:T(8,128)S(1)} %get-tuple-element.10.keep, f32[384,128]{1,0:T(8,128)S(1)} %collective-permute-done.got, bf16[128,6144]{1,0:T(8,128)(2,1)S(1)} %get-tuple-element.12.modes_panel, f32[64,64]{1,0:T(8,128)S(1)} %get-tuple-element.13.modes_gram), custom_call_target="tpu_custom_call" | custom-call | flops 100000000 | bytes 1000000 | tf_op jit(solution)/shard_map/snaps_gram/pallas_call | solution.py:241
  4.2 0.4 %collective-permute-start.1 = (f32[40,128]{1,0:T(8,128)S(1)}, f32[40,128]{1,0:T(8,128)S(1)}, u32[]{:S(2)}, u32[]{:S(2)}) collective-permute-start(f32[40,128]{1,0:T(8,128)S(1)} %get-tuple-element.14), channel_id=1, source_target_pairs={{0,1},{1,0},{2,3},{3,2},{4,5},{5,4},{6,7},{7,6},{8,9},{9,8},{10,11... | collective-permute-start | bytes 61448 | tf_op jit(solution)/shard_map/ppermute | solution.py:27
  4.7 0.8 %collective-permute-done.1 = f32[40,128]{1,0:T(8,128)S(1)} collective-permute-done((f32[40,128]{1,0:T(8,128)S(1)}, f32[40,128]{1,0:T(8,128)S(1)}, u32[]{:S(2)}, u32[]{:S(2)}) %collective-permute-start.1) | collective-permute-done | bytes 20512 | tf_op jit(solution)/shard_map/ppermute | solution.py:27
  5.5 2.6 %collective-permute-start.2 = (f32[40,128]{1,0:T(8,128)S(1)}, f32[40,128]{1,0:T(8,128)S(1)}, u32[]{:S(2)}, u32[]{:S(2)}) collective-permute-start(f32[40,128]{1,0:T(8,128)S(1)} %add.17), channel_id=1, source_target_pairs={{0,3},{1,2},{2,1},{3,0},{4,7},{5,6},{6,5},{7,4},{8,11},{9,10},{10,... | collective-permute-start | bytes 61448 | tf_op jit(solution)/shard_map/ppermute | solution.py:27
  8.1 1.5 %collective-permute-done.2 = f32[40,128]{1,0:T(8,128)S(1)} collective-permute-done((f32[40,128]{1,0:T(8,128)S(1)}, f32[40,128]{1,0:T(8,128)S(1)}, u32[]{:S(2)}, u32[]{:S(2)}) %collective-permute-start.2) | collective-permute-done | bytes 20512 | tf_op jit(solution)/shard_map/ppermute | solution.py:27
  9.6 1.8 %collective-permute-start.3 = (f32[40,128]{1,0:T(8,128)S(1)}, f32[40,128]{1,0:T(8,128)S(1)}, u32[]{:S(2)}, u32[]{:S(2)}) collective-permute-start(f32[40,128]{1,0:T(8,128)S(1)} %add.18), channel_id=1, source_target_pairs={{0,5},{1,4},{2,7},{3,6},{4,1},{5,0},{6,3},{7,2},{8,13},{9,12},{10,... | collective-permute-start | bytes 61448 | tf_op jit(solution)/shard_map/ppermute | solution.py:27
  11.3 1.5 %collective-permute-done.3 = f32[40,128]{1,0:T(8,128)S(1)} collective-permute-done((f32[40,128]{1,0:T(8,128)S(1)}, f32[40,128]{1,0:T(8,128)S(1)}, u32[]{:S(2)}, u32[]{:S(2)}) %collective-permute-start.3) | collective-permute-done | bytes 20512 | tf_op jit(solution)/shard_map/ppermute | solution.py:27
  12.8 1.8 %collective-permute-start.4 = (f32[40,128]{1,0:T(8,128)S(1)}, f32[40,128]{1,0:T(8,128)S(1)}, u32[]{:S(2)}, u32[]{:S(2)}) collective-permute-start(f32[40,128]{1,0:T(8,128)S(1)} %add.19), channel_id=1, source_target_pairs={{0,9},{1,8},{2,11},{3,10},{4,13},{5,12},{6,15},{7,14},{8,1},{9,0},... | collective-permute-start | bytes 61448 | tf_op jit(solution)/shard_map/ppermute | solution.py:27
  14.6 1.5 %collective-permute-done.4 = f32[40,128]{1,0:T(8,128)S(1)} collective-permute-done((f32[40,128]{1,0:T(8,128)S(1)}, f32[40,128]{1,0:T(8,128)S(1)}, u32[]{:S(2)}, u32[]{:S(2)}) %collective-permute-start.4) | collective-permute-done | bytes 20512 | tf_op jit(solution)/shard_map/ppermute | solution.py:27
  16.1 2.7 %collective-permute-start.5 = (f32[40,128]{1,0:T(8,128)S(1)}, f32[40,128]{1,0:T(8,128)S(1)}, u32[]{:S(2)}, u32[]{:S(2)}) collective-permute-start(f32[40,128]{1,0:T(8,128)S(1)} %add.20), channel_id=1, source_target_pairs={{0,17},{1,16},{2,19},{3,18},{4,21},{5,20},{6,23},{7,22},{8,25},{9,... | collective-permute-start | bytes 61448 | tf_op jit(solution)/shard_map/ppermute | solution.py:27
  18.8 0.0 copy-done.1
  18.8 0.1 copy.6.scale
  18.9 1.4 %collective-permute-done.5 = f32[40,128]{1,0:T(8,128)S(1)} collective-permute-done((f32[40,128]{1,0:T(8,128)S(1)}, f32[40,128]{1,0:T(8,128)S(1)}, u32[]{:S(2)}, u32[]{:S(2)}) %collective-permute-start.5) | collective-permute-done | bytes 20512 | tf_op jit(solution)/shard_map/ppermute | solution.py:27
  20.3 5.3 %factor_apply.1 = (f32[80,48,128]{2,1,0:T(8,128)}, f32[80,80]{1,0:T(8,128)}) custom-call(f32[40,128]{1,0:T(8,128)S(1)} %add.21.packed, f32[80,1]{1,0:T(8,128)S(1)} %copy.6.scale, bf16[128,6144]{1,0:T(8,128)(2,1)S(1)} %get-tuple-element.12.modes_panel, bf16[32,6144]{1,0:T(8,128)(2,1)S(1)} %get-tuple-element.15.snaps_panel), custom_call_target="tpu_custom_call" | custom-call | tf_op jit(solution)/shard_map/factor_apply/pallas_call | solution.py:255
  (6 shorter events, 0.0 us)
Async XLA Ops:
  0.6 1.7 %copy-start = (f32[64,2,3072]{2,1,0:T(2,128)S(1)}, f32[64,2,3072]{2,1,0:T(2,128)}, u32[]{:S(2)}) copy-start(f32[64,2,3072]{2,1,0:T(2,128)} %param.3) | copy-start | bytes 4718596
  1.8 1.6 %collective-permute-start = (f32[384,128]{1,0:T(8,128)S(1)}, f32[384,128]{1,0:T(8,128)S(1)}, u32[]{:S(2)}, u32[]{:S(2)}) collective-permute-start(f32[384,128]{1,0:T(8,128)S(1)} %get-tuple-element.11), channel_id=1, source_target_pairs={{0,1},{1,0},{2,3},{3,2},{4,5},{5,4},{6,7},{7,6},{8,9},{9,8},{10,11... | collective-permute-start | bytes 589832 | tf_op jit(solution)/shard_map/ppermute | solution.py:226
  2.4 16.5 %copy-start.1 = (f32[64]{0:T(128)S(1)}, f32[64]{0:T(128)}, u32[]{:S(2)}) copy-start(f32[64]{0:T(128)} %param.4) | copy-start | bytes 772
  4.2 1.3 %collective-permute-start.1 = (f32[40,128]{1,0:T(8,128)S(1)}, f32[40,128]{1,0:T(8,128)S(1)}, u32[]{:S(2)}, u32[]{:S(2)}) collective-permute-start(f32[40,128]{1,0:T(8,128)S(1)} %get-tuple-element.14), channel_id=1, source_target_pairs={{0,1},{1,0},{2,3},{3,2},{4,5},{5,4},{6,7},{7,6},{8,9},{9,8},{10,11... | collective-permute-start | bytes 61448 | tf_op jit(solution)/shard_map/ppermute | solution.py:27
  5.5 4.1 %collective-permute-start.2 = (f32[40,128]{1,0:T(8,128)S(1)}, f32[40,128]{1,0:T(8,128)S(1)}, u32[]{:S(2)}, u32[]{:S(2)}) collective-permute-start(f32[40,128]{1,0:T(8,128)S(1)} %add.17), channel_id=1, source_target_pairs={{0,3},{1,2},{2,1},{3,0},{4,7},{5,6},{6,5},{7,4},{8,11},{9,10},{10,... | collective-permute-start | bytes 61448 | tf_op jit(solution)/shard_map/ppermute | solution.py:27
  9.6 3.2 %collective-permute-start.3 = (f32[40,128]{1,0:T(8,128)S(1)}, f32[40,128]{1,0:T(8,128)S(1)}, u32[]{:S(2)}, u32[]{:S(2)}) collective-permute-start(f32[40,128]{1,0:T(8,128)S(1)} %add.18), channel_id=1, source_target_pairs={{0,5},{1,4},{2,7},{3,6},{4,1},{5,0},{6,3},{7,2},{8,13},{9,12},{10,... | collective-permute-start | bytes 61448 | tf_op jit(solution)/shard_map/ppermute | solution.py:27
  12.8 3.3 %collective-permute-start.4 = (f32[40,128]{1,0:T(8,128)S(1)}, f32[40,128]{1,0:T(8,128)S(1)}, u32[]{:S(2)}, u32[]{:S(2)}) collective-permute-start(f32[40,128]{1,0:T(8,128)S(1)} %add.19), channel_id=1, source_target_pairs={{0,9},{1,8},{2,11},{3,10},{4,13},{5,12},{6,15},{7,14},{8,1},{9,0},... | collective-permute-start | bytes 61448 | tf_op jit(solution)/shard_map/ppermute | solution.py:27
  16.1 4.2 %collective-permute-start.5 = (f32[40,128]{1,0:T(8,128)S(1)}, f32[40,128]{1,0:T(8,128)S(1)}, u32[]{:S(2)}, u32[]{:S(2)}) collective-permute-start(f32[40,128]{1,0:T(8,128)S(1)} %add.20), channel_id=1, source_target_pairs={{0,17},{1,16},{2,19},{3,18},{4,21},{5,20},{6,23},{7,22},{8,25},{9,... | collective-permute-start | bytes 61448 | tf_op jit(solution)/shard_map/ppermute | solution.py:27

commit v6 on v5

--- a/solution.py
+++ b/solution.py
@@ -101,63 +101,105 @@
     return jnp.broadcast_to(x[:, j:j + 1], (x.shape[0], LANES))
 
 
-def factor_tiles(tiles):
+def total_of(terms):
+    terms = list(terms)
+    while len(terms) > 1:
+        terms = [sum(terms[i:i + 2]) for i in range(0, len(terms), 2)]
+    return terms[0]
+
+
+def everywhere(ref, row):
+    return jnp.broadcast_to(ref[row:row + 1, :], (TILE, LANES))
+
+
+def block_inverse(a):
+    a = dict(a)
+    l, m = {}, {}
+    for p in range(0, TILE, 2):
+        q = p + 1
+        root = lax.rsqrt(a[p, p])
+        det = a[p, p] * a[q, q] - a[q, p] * a[q, p]
+        root_det = lax.rsqrt(det)
+        over_det = root_det * root_det
+        m[p, p] = root
+        m[q, q] = root_det * (a[p, p] * root)
+        l[q, p] = a[q, p] * root
+        both = root_det * root
+        w, z = {}, {}
+        for i in range(q + 1, TILE):
+            w[i] = a[p, p] * a[i, q] - a[q, p] * a[i, p]
+            z[i] = a[q, q] * a[i, p] - a[q, p] * a[i, q]
+            l[i, p] = a[i, p] * root
+            l[i, q] = w[i] * both
+        for k in range(q + 1, TILE):
+            for i in range(k, TILE):
+                a[i, k] = a[i, k] - (a[i, p] * z[k] + a[i, q] * w[k]) * over_det
+        for i in (p, q):
+            for k in range(i):
+                m[i, k] = -m[i, i] * total_of(l[i, j] * m[j, k] for j in range(k, i))
+    return m
+
+
+def factor_tiles(tiles, entries, columns_of, rows_of, solved_of):
+    count = len(tiles)
     lane = lax.broadcasted_iota(jnp.int32, (TILE, LANES), 1)
-    sub = lax.broadcasted_iota(jnp.int32, (TILE, LANES), 0)
     tiles = list(tiles)
     upper, inverse = [], []
-    for t in range(len(tiles)):
+    square = TILE * TILE
+    for b in range(2):
+        columns_of[b] = jnp.zeros((square, LANES), F32)
+        rows_of[b] = jnp.zeros((square, LANES), F32)
+    diagonal = [spread_column(tiles[0], j) for j in range(TILE)]
+    below = [[spread_column(x, j) for j in range(TILE)] for x in tiles[1:]]
+    following = [spread_column(tiles[1], TILE + j) for j in range(TILE)]
+    for t in range(count):
         at = t * TILE
-        columns = [[spread_column(x, at + j) for j in range(TILE)] for x in tiles[t:]]
-        a = {(i, j): spread_row(columns[0][j], i) for j in range(TILE) for i in range(j, TILE)}
-        l, m, root = {}, {}, []
+        slot = entries.at[t]
         for j in range(TILE):
-            r = lax.rsqrt(a[j, j])
-            root.append(r)
-            for i in range(j + 1, TILE):
-                l[i, j] = a[i, j] * r
-            for k in range(j + 1, TILE):
-                for i in range(k, TILE):
-                    a[i, k] = a[i, k] - l[i, j] * l[k, j]
-            m[j, j] = r
-            for k in range(j):
-                dot = l[j, k] * m[k, k]
-                for q in range(k + 1, j):
-                    dot = dot + l[j, q] * m[q, k]
-                m[j, k] = -(dot * r)
-        def column_of(k):
-            out = jnp.zeros((TILE, LANES), F32)
-            for i in range(k, TILE):
-                out = jnp.where(sub == i, m[i, k], out)
-            return out
-        def row_of(i):
-            out = jnp.zeros((TILE, LANES), F32)
+            slot[j * TILE:(j + 1) * TILE, :] = diagonal[j]
+        m = block_inverse(
+            {(i, j): everywhere(slot, j * TILE + i) for j in range(TILE) for i in range(j, TILE)}
+        )
+        if t + 1 < count:
+            ahead = solved_of.at[t]
+            for i in range(TILE):
+                solved = total_of(m[i, j] * below[0][j] for j in range(i + 1))
+                ahead[i * TILE:(i + 1) * TILE, :] = solved
+            kept = [ahead[i * TILE:(i + 1) * TILE, :] for i in range(TILE)]
+            diagonal = [
+                following[k]
+                - total_of(kept[i] * everywhere(ahead, i * TILE + k) for i in range(TILE))
+                for k in range(TILE)
+            ]
+        by_column, by_row = columns_of.at[t % 2], rows_of.at[t % 2]
+        for i in range(TILE):
             for k in range(i + 1):
-                out = jnp.where(sub == k, m[i, k], out)
-            return out
-        m_columns = [column_of(k) for k in range(TILE)]
-        row = sum(m_columns[k] * spread_row(tiles[t], k) for k in range(TILE))
+                by_column[k * TILE + i:k * TILE + i + 1, :] = m[i, k][:1]
+                by_row[i * TILE + k:i * TILE + k + 1, :] = m[i, k][:1]
+        m_columns = [by_column[k * TILE:(k + 1) * TILE, :] for k in range(TILE)]
+        row = total_of(m_columns[k] * spread_row(tiles[t], k) for k in range(TILE))
         block = (lane >= at) & (lane < at + TILE)
-        placed = jnp.zeros((TILE, LANES), F32)
+        mixed = row
         for k in range(TILE):
-            placed = jnp.where(lane == at + k, m_columns[k], placed)
+            mixed = jnp.where(lane == at + k, m_columns[k], mixed)
         upper.append(row)
-        inv_row = jnp.where(block, placed, jnp.where(lane < at, row, 0.0))
-        inverse.append(inv_row)
-        if t + 1 == len(tiles):
+        inverse.append(jnp.where(lane < at + TILE, mixed, 0.0))
+        if t + 1 == count:
             break
-        mixed = jnp.where(block, placed, row)
-        solved = sum(row_of(i) * spread_row(mixed, i) for i in range(TILE))
+        solved = total_of(
+            by_row[i * TILE:(i + 1) * TILE, :] * spread_row(mixed, i) for i in range(TILE)
+        )
         rows = [spread_row(solved, j) for j in range(TILE)]
-        for s in range(t + 1, len(tiles)):
-            x = jnp.where(block, 0.0, tiles[s])
-            c = columns[s - t]
-            x = x - sum(c[j] * rows[j] for j in range(TILE))
-            tiles[s] = x
+        for s in range(t + 1, count):
+            c = below[s - t - 1]
+            tiles[s] = jnp.where(block, 0.0, tiles[s]) - total_of(c[j] * rows[j] for j in range(TILE))
+        below = [[spread_column(x, at + TILE + j) for j in range(TILE)] for x in tiles[t + 2:]]
+        if t + 2 < count:
+            following = [spread_column(tiles[t + 2], at + 2 * TILE + j) for j in range(TILE)]
     return upper, inverse
 
 
-def apply_kernel(cells, packed, scale, modes_panel, snaps_panel, out, factor, left, buf, sems):
+def apply_kernel(cells, packed, scale, modes_panel, snaps_panel, out, factor, left, buf, sems, *spread):
     modes, snaps = modes_panel.shape[0] // 2, snaps_panel.shape[0] // 2
     width = modes + snaps
     mid = width // 2
@@ -169,7 +211,7 @@
     r = lax.broadcasted_iota(jnp.int32, (LANES, LANES), 0)
     c = lax.broadcasted_iota(jnp.int32, (LANES, LANES), 1)
     full = jnp.where(r >= c, lower, lower.T)
-    upper, inverse = factor_tiles([full[i:i + TILE] for i in range(0, width, TILE)])
+    upper, inverse = factor_tiles([full[i:i + TILE] for i in range(0, width, TILE)], *spread)
     for i, x in enumerate(inverse):
         left[i * TILE:(i + 1) * TILE, :] = x
     whole = jnp.concatenate(upper + [jnp.zeros((LANES - width, LANES), F32)], axis=0).T
@@ -264,6 +306,7 @@
             pltpu.VMEM((width, LANES), F32),
             pltpu.VMEM((width, slabs, LANES), F32),
             pltpu.SemaphoreType.DMA((chunk,)),
+            *(pltpu.VMEM((n, TILE * TILE, LANES), F32) for n in (width // TILE, 2, 2, width // TILE)),
         ],
         compiler_params=PARAMS,
         name="factor_apply",

time: 25.8 us -> 24.3 us (0.942)
  Pallas kernels: 8.25 us -> 6.81 us
    pallas_call x1, Pallas kernels: 5.3 us -> 3.85 us  [per_device(): pl.pallas_call(functools.partial(apply_kernel, cells), out_shape=(jax.Sha...]
where the time goes in v6:
time: 24.3 us; the launch traced here: 24.2 us
  starting transfers between devices  9.85 us (41%)
  Pallas kernels  6.81 us (28%)
  waiting for transfers between devices  6.7 us (28%)
  between operations  0.67 us (3%)
    ppermute x5, starting transfers between devices, total(): lax.ppermute(value, AXES, [(i, i ^ mask) for i in range(count)])  9.3 us
    ppermute x5, waiting for transfers between devices, total(): lax.ppermute(value, AXES, [(i, i ^ mask) for i in range(count)])  6.66 us
    pallas_call x1, Pallas kernels, per_device(): pl.pallas_call(functools.partial(apply_kernel, cells), out_shape=(jax.Sha...  3.85 us
    pallas_call x1, Pallas kernels, per_device(): pl.pallas_call(functools.partial(pick_kernel, rows), out_shape=(part, par...  1.15 us
    pallas_call x1, Pallas kernels, per_device(): pl.pallas_call(modes_kernel, out_shape=(jax.ShapeDtypeStruct((2 * modes,...  1.02 us
    pallas_call x1, Pallas kernels, per_device(): pl.pallas_call(functools.partial(snaps_kernel, rows), out_shape=(jax.Shap...  0.79 us
    ppermute x1, starting transfers between devices, per_device(): got = lax.ppermute(send, 'grp', [(0, 1), (1, 0)])  0.56 us
  transfers between devices with their start and end apart: 6, of which 5 were waited for; matrix products, arithmetic and copies ran while one was open for 0% of the time, Pallas kernels for 4%

profile of v6, /device:TPU:0, one launch (start us, length us, event | category | flops | bytes accessed | tf_op | source)
XLA Modules:
  0.0 24.2 jit_solution(7299481995400806570)
XLA Ops:
  0.6 0.0 copy-start
  0.6 1.1 %pick_rows.1 = (f32[384,128]{1,0:T(8,128)S(1)}, f32[384,128]{1,0:T(8,128)S(1)}) custom-call(f32[768,128]{1,0:T(8,128)} %bitcast.19), custom_call_target="tpu_custom_call" | custom-call | flops 1000000000 | bytes 786432 | tf_op jit(solution)/shard_map/pick_rows/pallas_call | solution.py:258
  1.8 0.6 %collective-permute-start = (f32[384,128]{1,0:T(8,128)S(1)}, f32[384,128]{1,0:T(8,128)S(1)}, u32[]{:S(2)}, u32[]{:S(2)}) collective-permute-start(f32[384,128]{1,0:T(8,128)S(1)} %get-tuple-element.11), channel_id=1, source_target_pairs={{0,1},{1,0},{2,3},{3,2},{4,5},{5,4},{6,7},{7,6},{8,9},{9,8},{10,11... | collective-permute-start | bytes 589832 | tf_op jit(solution)/shard_map/ppermute | solution.py:268
  2.4 0.0 copy-done
  2.4 0.0 copy-start.1
  2.4 1.0 %modes_gram.1 = (bf16[128,6144]{1,0:T(8,128)(2,1)S(1)}, f32[64,64]{1,0:T(8,128)S(1)}) custom-call(f32[3072,128]{1,0:T(8,128)S(1)} %bitcast.17), custom_call_target="tpu_custom_call" | custom-call | flops 100000000 | bytes 1572864 | tf_op jit(solution)/shard_map/modes_gram/pallas_call | solution.py:271
  3.4 0.0 collective-permute-done.got
  3.4 0.8 %snaps_gram.1 = (bf16[32,6144]{1,0:T(8,128)(2,1)S(1)}, f32[40,128]{1,0:T(8,128)S(1)}) custom-call(f32[384,128]{1,0:T(8,128)S(1)} %get-tuple-element.10.keep, f32[384,128]{1,0:T(8,128)S(1)} %collective-permute-done.got, bf16[128,6144]{1,0:T(8,128)(2,1)S(1)} %get-tuple-element.12.modes_panel, f32[64,64]{1,0:T(8,128)S(1)} %get-tuple-element.13.modes_gram), custom_call_target="tpu_custom_call" | custom-call | flops 100000000 | bytes 1000000 | tf_op jit(solution)/shard_map/snaps_gram/pallas_call | solution.py:283
  4.2 0.4 %collective-permute-start.1 = (f32[40,128]{1,0:T(8,128)S(1)}, f32[40,128]{1,0:T(8,128)S(1)}, u32[]{:S(2)}, u32[]{:S(2)}) collective-permute-start(f32[40,128]{1,0:T(8,128)S(1)} %get-tuple-element.14), channel_id=1, source_target_pairs={{0,1},{1,0},{2,3},{3,2},{4,5},{5,4},{6,7},{7,6},{8,9},{9,8},{10,11... | collective-permute-start | bytes 61448 | tf_op jit(solution)/shard_map/ppermute | solution.py:27
  4.7 0.8 %collective-permute-done.1 = f32[40,128]{1,0:T(8,128)S(1)} collective-permute-done((f32[40,128]{1,0:T(8,128)S(1)}, f32[40,128]{1,0:T(8,128)S(1)}, u32[]{:S(2)}, u32[]{:S(2)}) %collective-permute-start.1) | collective-permute-done | bytes 20512 | tf_op jit(solution)/shard_map/ppermute | solution.py:27
  5.5 2.6 %collective-permute-start.2 = (f32[40,128]{1,0:T(8,128)S(1)}, f32[40,128]{1,0:T(8,128)S(1)}, u32[]{:S(2)}, u32[]{:S(2)}) collective-permute-start(f32[40,128]{1,0:T(8,128)S(1)} %add.17), channel_id=1, source_target_pairs={{0,3},{1,2},{2,1},{3,0},{4,7},{5,6},{6,5},{7,4},{8,11},{9,10},{10,... | collective-permute-start | bytes 61448 | tf_op jit(solution)/shard_map/ppermute | solution.py:27
  8.1 1.5 %collective-permute-done.2 = f32[40,128]{1,0:T(8,128)S(1)} collective-permute-done((f32[40,128]{1,0:T(8,128)S(1)}, f32[40,128]{1,0:T(8,128)S(1)}, u32[]{:S(2)}, u32[]{:S(2)}) %collective-permute-start.2) | collective-permute-done | bytes 20512 | tf_op jit(solution)/shard_map/ppermute | solution.py:27
  9.6 1.8 %collective-permute-start.3 = (f32[40,128]{1,0:T(8,128)S(1)}, f32[40,128]{1,0:T(8,128)S(1)}, u32[]{:S(2)}, u32[]{:S(2)}) collective-permute-start(f32[40,128]{1,0:T(8,128)S(1)} %add.18), channel_id=1, source_target_pairs={{0,5},{1,4},{2,7},{3,6},{4,1},{5,0},{6,3},{7,2},{8,13},{9,12},{10,... | collective-permute-start | bytes 61448 | tf_op jit(solution)/shard_map/ppermute | solution.py:27
  11.3 1.5 %collective-permute-done.3 = f32[40,128]{1,0:T(8,128)S(1)} collective-permute-done((f32[40,128]{1,0:T(8,128)S(1)}, f32[40,128]{1,0:T(8,128)S(1)}, u32[]{:S(2)}, u32[]{:S(2)}) %collective-permute-start.3) | collective-permute-done | bytes 20512 | tf_op jit(solution)/shard_map/ppermute | solution.py:27
  12.8 1.8 %collective-permute-start.4 = (f32[40,128]{1,0:T(8,128)S(1)}, f32[40,128]{1,0:T(8,128)S(1)}, u32[]{:S(2)}, u32[]{:S(2)}) collective-permute-start(f32[40,128]{1,0:T(8,128)S(1)} %add.19), channel_id=1, source_target_pairs={{0,9},{1,8},{2,11},{3,10},{4,13},{5,12},{6,15},{7,14},{8,1},{9,0},... | collective-permute-start | bytes 61448 | tf_op jit(solution)/shard_map/ppermute | solution.py:27
  14.6 1.5 %collective-permute-done.4 = f32[40,128]{1,0:T(8,128)S(1)} collective-permute-done((f32[40,128]{1,0:T(8,128)S(1)}, f32[40,128]{1,0:T(8,128)S(1)}, u32[]{:S(2)}, u32[]{:S(2)}) %collective-permute-start.4) | collective-permute-done | bytes 20512 | tf_op jit(solution)/shard_map/ppermute | solution.py:27
  16.1 2.7 %collective-permute-start.5 = (f32[40,128]{1,0:T(8,128)S(1)}, f32[40,128]{1,0:T(8,128)S(1)}, u32[]{:S(2)}, u32[]{:S(2)}) collective-permute-start(f32[40,128]{1,0:T(8,128)S(1)} %add.20), channel_id=1, source_target_pairs={{0,17},{1,16},{2,19},{3,18},{4,21},{5,20},{6,23},{7,22},{8,25},{9,... | collective-permute-start | bytes 61448 | tf_op jit(solution)/shard_map/ppermute | solution.py:27
  18.8 0.0 copy-done.1
  18.8 0.1 copy.6.scale
  18.9 1.4 %collective-permute-done.5 = f32[40,128]{1,0:T(8,128)S(1)} collective-permute-done((f32[40,128]{1,0:T(8,128)S(1)}, f32[40,128]{1,0:T(8,128)S(1)}, u32[]{:S(2)}, u32[]{:S(2)}) %collective-permute-start.5) | collective-permute-done | bytes 20512 | tf_op jit(solution)/shard_map/ppermute | solution.py:27
  20.3 3.9 %factor_apply.1 = (f32[80,48,128]{2,1,0:T(8,128)}, f32[80,80]{1,0:T(8,128)}) custom-call(f32[40,128]{1,0:T(8,128)S(1)} %add.21.packed, f32[80,1]{1,0:T(8,128)S(1)} %copy.6.scale, bf16[128,6144]{1,0:T(8,128)(2,1)S(1)} %get-tuple-element.12.modes_panel, bf16[32,6144]{1,0:T(8,128)(2,1)S(1)} %get-tuple-element.15.snaps_panel), custom_call_target="tpu_custom_call" | custom-call | tf_op jit(solution)/shard_map/factor_apply/pallas_call | solution.py:297
  (6 shorter events, 0.0 us)
Async XLA Ops:
  0.6 1.7 %copy-start = (f32[64,2,3072]{2,1,0:T(2,128)S(1)}, f32[64,2,3072]{2,1,0:T(2,128)}, u32[]{:S(2)}) copy-start(f32[64,2,3072]{2,1,0:T(2,128)} %param.3) | copy-start | bytes 4718596
  1.8 1.6 %collective-permute-start = (f32[384,128]{1,0:T(8,128)S(1)}, f32[384,128]{1,0:T(8,128)S(1)}, u32[]{:S(2)}, u32[]{:S(2)}) collective-permute-start(f32[384,128]{1,0:T(8,128)S(1)} %get-tuple-element.11), channel_id=1, source_target_pairs={{0,1},{1,0},{2,3},{3,2},{4,5},{5,4},{6,7},{7,6},{8,9},{9,8},{10,11... | collective-permute-start | bytes 589832 | tf_op jit(solution)/shard_map/ppermute | solution.py:268
  2.4 16.5 %copy-start.1 = (f32[64]{0:T(128)S(1)}, f32[64]{0:T(128)}, u32[]{:S(2)}) copy-start(f32[64]{0:T(128)} %param.4) | copy-start | bytes 772
  4.2 1.3 %collective-permute-start.1 = (f32[40,128]{1,0:T(8,128)S(1)}, f32[40,128]{1,0:T(8,128)S(1)}, u32[]{:S(2)}, u32[]{:S(2)}) collective-permute-start(f32[40,128]{1,0:T(8,128)S(1)} %get-tuple-element.14), channel_id=1, source_target_pairs={{0,1},{1,0},{2,3},{3,2},{4,5},{5,4},{6,7},{7,6},{8,9},{9,8},{10,11... | collective-permute-start | bytes 61448 | tf_op jit(solution)/shard_map/ppermute | solution.py:27
  5.5 4.1 %collective-permute-start.2 = (f32[40,128]{1,0:T(8,128)S(1)}, f32[40,128]{1,0:T(8,128)S(1)}, u32[]{:S(2)}, u32[]{:S(2)}) collective-permute-start(f32[40,128]{1,0:T(8,128)S(1)} %add.17), channel_id=1, source_target_pairs={{0,3},{1,2},{2,1},{3,0},{4,7},{5,6},{6,5},{7,4},{8,11},{9,10},{10,... | collective-permute-start | bytes 61448 | tf_op jit(solution)/shard_map/ppermute | solution.py:27
  9.6 3.2 %collective-permute-start.3 = (f32[40,128]{1,0:T(8,128)S(1)}, f32[40,128]{1,0:T(8,128)S(1)}, u32[]{:S(2)}, u32[]{:S(2)}) collective-permute-start(f32[40,128]{1,0:T(8,128)S(1)} %add.18), channel_id=1, source_target_pairs={{0,5},{1,4},{2,7},{3,6},{4,1},{5,0},{6,3},{7,2},{8,13},{9,12},{10,... | collective-permute-start | bytes 61448 | tf_op jit(solution)/shard_map/ppermute | solution.py:27
  12.8 3.3 %collective-permute-start.4 = (f32[40,128]{1,0:T(8,128)S(1)}, f32[40,128]{1,0:T(8,128)S(1)}, u32[]{:S(2)}, u32[]{:S(2)}) collective-permute-start(f32[40,128]{1,0:T(8,128)S(1)} %add.19), channel_id=1, source_target_pairs={{0,9},{1,8},{2,11},{3,10},{4,13},{5,12},{6,15},{7,14},{8,1},{9,0},... | collective-permute-start | bytes 61448 | tf_op jit(solution)/shard_map/ppermute | solution.py:27
  16.1 4.2 %collective-permute-start.5 = (f32[40,128]{1,0:T(8,128)S(1)}, f32[40,128]{1,0:T(8,128)S(1)}, u32[]{:S(2)}, u32[]{:S(2)}) collective-permute-start(f32[40,128]{1,0:T(8,128)S(1)} %add.20), channel_id=1, source_target_pairs={{0,17},{1,16},{2,19},{3,18},{4,21},{5,20},{6,23},{7,22},{8,25},{9,... | collective-permute-start | bytes 61448 | tf_op jit(solution)/shard_map/ppermute | solution.py:27

commit v7 on v6

--- a/solution.py
+++ b/solution.py
@@ -10,6 +10,7 @@
 AXES = ("srv", "grp")
 LANES = 128
 TILE = 8
+BLOCK = 16
 F32, BF16 = jnp.float32, jnp.bfloat16
 VMEM = pl.BlockSpec(memory_space=pltpu.VMEM)
 ANY = pl.BlockSpec(memory_space=pl.ANY)
@@ -26,6 +27,18 @@
     for mask in masks:
         value = value + lax.ppermute(value, AXES, [(i, i ^ mask) for i in range(count)])
     return value
+
+
+def packing(width):
+    groups = []
+    for r in reversed(range(width // BLOCK)):
+        for group in groups:
+            if sum(q + 1 for q in group) + r + 1 <= LANES // BLOCK:
+                group.append(r)
+                break
+        else:
+            groups.append([r])
+    return groups
 
 
 def split(x):
@@ -78,19 +91,19 @@
     top = with_modes[:modes]
     low_row = (top[:, :snaps] + top[:, snaps:] + with_modes[modes:, :snaps]).T
     own = own[:snaps] + own[snaps:] + own[snaps:].T
-    width = modes + snaps
-    mid = width // 2
-    a = modes_gram[...]
-    left = jnp.concatenate(
+    whole = jnp.concatenate(
         [
-            jnp.concatenate([a[mid:], jnp.zeros((modes - mid, snaps), F32)], axis=1),
+            jnp.concatenate([modes_gram[...], jnp.zeros((modes, snaps), F32)], axis=1),
             jnp.concatenate([low_row, own], axis=1),
         ],
         axis=0,
     )
-    packed[...] = jnp.concatenate(
-        [left, a[:mid, :mid], jnp.zeros((mid, LANES - width - mid), F32)], axis=1
-    )
+    for g, group in enumerate(packing(modes + snaps)):
+        parts = [whole[r * BLOCK:(r + 1) * BLOCK, :(r + 1) * BLOCK] for r in group]
+        spare = LANES - sum(p.shape[1] for p in parts)
+        if spare:
+            parts.append(jnp.zeros((BLOCK, spare), F32))
+        packed[g * BLOCK:(g + 1) * BLOCK, :] = jnp.concatenate(parts, axis=1)
 
 
 def spread_row(x, i):
@@ -199,15 +212,20 @@
     return upper, inverse
 
 
-def apply_kernel(cells, packed, scale, modes_panel, snaps_panel, out, factor, left, buf, sems, *spread):
+def apply_kernel(cells, packed, scale, modes_panel, snaps_panel, out, factor, left, buf, lower_out, sems, *spread):
     modes, snaps = modes_panel.shape[0] // 2, snaps_panel.shape[0] // 2
     width = modes + snaps
-    mid = width // 2
-    both = packed[...] * (1.0 / cells)
-    lane = lax.broadcasted_iota(jnp.int32, (mid, LANES), 1)
-    top = jnp.where(lane < mid, pltpu.roll(both, LANES - width, 1), 0.0)
-    low = jnp.where(lane < width, both, 0.0)
-    lower = jnp.concatenate([top, low, jnp.zeros((LANES - width, LANES), F32)], axis=0)
+    lane = lax.broadcasted_iota(jnp.int32, (BLOCK, LANES), 1)
+    parts = {}
+    for g, group in enumerate(packing(width)):
+        strip = packed[g * BLOCK:(g + 1) * BLOCK, :] * (1.0 / cells)
+        used = 0
+        for r in group:
+            piece = pltpu.roll(strip, LANES - used, 1) if used else strip
+            parts[r] = jnp.where(lane < (r + 1) * BLOCK, piece, 0.0)
+            used += (r + 1) * BLOCK
+    lower = [parts[r] for r in range(width // BLOCK)] + [jnp.zeros((LANES - width, LANES), F32)]
+    lower = jnp.concatenate(lower, axis=0)
     r = lax.broadcasted_iota(jnp.int32, (LANES, LANES), 0)
     c = lax.broadcasted_iota(jnp.int32, (LANES, LANES), 1)
     full = jnp.where(r >= c, lower, lower.T)
@@ -216,16 +234,17 @@
         left[i * TILE:(i + 1) * TILE, :] = x
     whole = jnp.concatenate(upper + [jnp.zeros((LANES - width, LANES), F32)], axis=0).T
     whole = jnp.where(r >= c, whole, 0.0)[:width, :width]
-    factor[...] = whole * scale[...]
+    lower_out[...] = whole * scale[...]
+    chunks = sems.shape[0] - 1
+    copies = [pltpu.make_async_copy(lower_out, factor, sems.at[chunks])]
+    copies[0].start()
     w_high, w_low = split(left[:, :width])
     wm = jnp.concatenate([w_high[:, :modes], w_low[:, :modes]], axis=0)
     ws = jnp.concatenate([w_high[:, modes:], w_low[:, modes:]], axis=0)
     both_w = jnp.concatenate([wm, wm, ws, ws], axis=1)
-    chunks = sems.shape[0]
     slabs = buf.shape[1]
     flat = buf.reshape(width * slabs, LANES)
     step = slabs // chunks
-    copies = []
     for k in range(chunks):
         cols = slice(k * step * LANES, (k + 1) * step * LANES)
         right = jnp.concatenate([modes_panel[:, cols], snaps_panel[:, cols]], axis=0)
@@ -284,7 +303,7 @@
         functools.partial(snaps_kernel, rows),
         out_shape=(
             jax.ShapeDtypeStruct((2 * snaps, slabs * LANES), BF16),
-            jax.ShapeDtypeStruct((width // 2, LANES), F32),
+            jax.ShapeDtypeStruct((len(packing(width)) * BLOCK, LANES), F32),
         ),
         in_specs=[VMEM] * 4,
         out_specs=(VMEM, VMEM),
@@ -301,11 +320,12 @@
             jax.ShapeDtypeStruct((width, width), F32),
         ),
         in_specs=[VMEM] * 4,
-        out_specs=(ANY, VMEM),
+        out_specs=(ANY, ANY),
         scratch_shapes=[
             pltpu.VMEM((width, LANES), F32),
             pltpu.VMEM((width, slabs, LANES), F32),
-            pltpu.SemaphoreType.DMA((chunk,)),
+            pltpu.VMEM((width, width), F32),
+            pltpu.SemaphoreType.DMA((chunk + 1,)),
             *(pltpu.VMEM((n, TILE * TILE, LANES), F32) for n in (width // TILE, 2, 2, width // TILE)),
         ],
         compiler_params=PARAMS,

time: 24.3 us -> 23.5 us (0.967)
  Pallas kernels: 6.81 us -> 6.2 us
    pallas_call x1, Pallas kernels: 3.85 us -> 3.25 us  [per_device(): pl.pallas_call(functools.partial(apply_kernel, cells), out_shape=(jax.Sha...]
where the time goes in v7:
time: 23.5 us; the launch traced here: 23.4 us
  starting transfers between devices  9.84 us (42%)
  waiting for transfers between devices  6.54 us (28%)
  Pallas kernels  6.2 us (26%)
  between operations  0.66 us (3%)
    ppermute x5, starting transfers between devices, total(): lax.ppermute(value, AXES, [(i, i ^ mask) for i in range(count)])  9.28 us
    ppermute x5, waiting for transfers between devices, total(): lax.ppermute(value, AXES, [(i, i ^ mask) for i in range(count)])  6.5 us
    pallas_call x1, Pallas kernels, per_device(): pl.pallas_call(functools.partial(apply_kernel, cells), out_shape=(jax.Sha...  3.25 us
    pallas_call x1, Pallas kernels, per_device(): pl.pallas_call(functools.partial(pick_kernel, rows), out_shape=(part, par...  1.15 us
    pallas_call x1, Pallas kernels, per_device(): pl.pallas_call(modes_kernel, out_shape=(jax.ShapeDtypeStruct((2 * modes,...  1.02 us
    pallas_call x1, Pallas kernels, per_device(): pl.pallas_call(functools.partial(snaps_kernel, rows), out_shape=(jax.Shap...  0.79 us
    ppermute x1, starting transfers between devices, per_device(): got = lax.ppermute(send, 'grp', [(0, 1), (1, 0)])  0.56 us
  transfers between devices with their start and end apart: 6, of which 5 were waited for; matrix products, arithmetic and copies ran while one was open for 0% of the time, Pallas kernels for 4%

profile of v7, /device:TPU:0, one launch (start us, length us, event | category | flops | bytes accessed | tf_op | source)
XLA Modules:
  0.0 23.4 jit_solution(11216642871352354539)
XLA Ops:
  0.6 0.0 copy-start
  0.6 1.1 %pick_rows.1 = (f32[384,128]{1,0:T(8,128)S(1)}, f32[384,128]{1,0:T(8,128)S(1)}) custom-call(f32[768,128]{1,0:T(8,128)} %bitcast.19), custom_call_target="tpu_custom_call" | custom-call | flops 1000000000 | bytes 786432 | tf_op jit(solution)/shard_map/pick_rows/pallas_call | solution.py:277
  1.8 0.6 %collective-permute-start = (f32[384,128]{1,0:T(8,128)S(1)}, f32[384,128]{1,0:T(8,128)S(1)}, u32[]{:S(2)}, u32[]{:S(2)}) collective-permute-start(f32[384,128]{1,0:T(8,128)S(1)} %get-tuple-element.11), channel_id=1, source_target_pairs={{0,1},{1,0},{2,3},{3,2},{4,5},{5,4},{6,7},{7,6},{8,9},{9,8},{10,11... | collective-permute-start | bytes 589832 | tf_op jit(solution)/shard_map/ppermute | solution.py:287
  2.4 0.0 copy-done
  2.4 0.0 copy-start.1
  2.4 1.0 %modes_gram.1 = (bf16[128,6144]{1,0:T(8,128)(2,1)S(1)}, f32[64,64]{1,0:T(8,128)S(1)}) custom-call(f32[3072,128]{1,0:T(8,128)S(1)} %bitcast.17), custom_call_target="tpu_custom_call" | custom-call | flops 100000000 | bytes 1572864 | tf_op jit(solution)/shard_map/modes_gram/pallas_call | solution.py:290
  3.4 0.0 collective-permute-done.got
  3.4 0.8 %snaps_gram.1 = (bf16[32,6144]{1,0:T(8,128)(2,1)S(1)}, f32[32,128]{1,0:T(8,128)S(1)}) custom-call(f32[384,128]{1,0:T(8,128)S(1)} %get-tuple-element.10.keep, f32[384,128]{1,0:T(8,128)S(1)} %collective-permute-done.got, bf16[128,6144]{1,0:T(8,128)(2,1)S(1)} %get-tuple-element.12.modes_panel, f32[64,64]{1,0:T(8,128)S(1)} %get-tuple-element.13.modes_gram), custom_call_target="tpu_custom_call" | custom-call | flops 100000000 | bytes 1000000 | tf_op jit(solution)/shard_map/snaps_gram/pallas_call | solution.py:302
  4.2 0.4 %collective-permute-start.1 = (f32[32,128]{1,0:T(8,128)S(1)}, f32[32,128]{1,0:T(8,128)S(1)}, u32[]{:S(2)}, u32[]{:S(2)}) collective-permute-start(f32[32,128]{1,0:T(8,128)S(1)} %get-tuple-element.14), channel_id=1, source_target_pairs={{0,1},{1,0},{2,3},{3,2},{4,5},{5,4},{6,7},{7,6},{8,9},{9,8},{10,11... | collective-permute-start | bytes 49160 | tf_op jit(solution)/shard_map/ppermute | solution.py:28
  4.6 0.8 %collective-permute-done.1 = f32[32,128]{1,0:T(8,128)S(1)} collective-permute-done((f32[32,128]{1,0:T(8,128)S(1)}, f32[32,128]{1,0:T(8,128)S(1)}, u32[]{:S(2)}, u32[]{:S(2)}) %collective-permute-start.1) | collective-permute-done | bytes 16416 | tf_op jit(solution)/shard_map/ppermute | solution.py:28
  5.5 2.6 %collective-permute-start.2 = (f32[32,128]{1,0:T(8,128)S(1)}, f32[32,128]{1,0:T(8,128)S(1)}, u32[]{:S(2)}, u32[]{:S(2)}) collective-permute-start(f32[32,128]{1,0:T(8,128)S(1)} %add.17), channel_id=1, source_target_pairs={{0,3},{1,2},{2,1},{3,0},{4,7},{5,6},{6,5},{7,4},{8,11},{9,10},{10,... | collective-permute-start | bytes 49160 | tf_op jit(solution)/shard_map/ppermute | solution.py:28
  8.1 1.4 %collective-permute-done.2 = f32[32,128]{1,0:T(8,128)S(1)} collective-permute-done((f32[32,128]{1,0:T(8,128)S(1)}, f32[32,128]{1,0:T(8,128)S(1)}, u32[]{:S(2)}, u32[]{:S(2)}) %collective-permute-start.2) | collective-permute-done | bytes 16416 | tf_op jit(solution)/shard_map/ppermute | solution.py:28
  9.5 1.7 %collective-permute-start.3 = (f32[32,128]{1,0:T(8,128)S(1)}, f32[32,128]{1,0:T(8,128)S(1)}, u32[]{:S(2)}, u32[]{:S(2)}) collective-permute-start(f32[32,128]{1,0:T(8,128)S(1)} %add.18), channel_id=1, source_target_pairs={{0,5},{1,4},{2,7},{3,6},{4,1},{5,0},{6,3},{7,2},{8,13},{9,12},{10,... | collective-permute-start | bytes 49160 | tf_op jit(solution)/shard_map/ppermute | solution.py:28
  11.3 1.4 %collective-permute-done.3 = f32[32,128]{1,0:T(8,128)S(1)} collective-permute-done((f32[32,128]{1,0:T(8,128)S(1)}, f32[32,128]{1,0:T(8,128)S(1)}, u32[]{:S(2)}, u32[]{:S(2)}) %collective-permute-start.3) | collective-permute-done | bytes 16416 | tf_op jit(solution)/shard_map/ppermute | solution.py:28
  12.7 1.8 %collective-permute-start.4 = (f32[32,128]{1,0:T(8,128)S(1)}, f32[32,128]{1,0:T(8,128)S(1)}, u32[]{:S(2)}, u32[]{:S(2)}) collective-permute-start(f32[32,128]{1,0:T(8,128)S(1)} %add.19), channel_id=1, source_target_pairs={{0,9},{1,8},{2,11},{3,10},{4,13},{5,12},{6,15},{7,14},{8,1},{9,0},... | collective-permute-start | bytes 49160 | tf_op jit(solution)/shard_map/ppermute | solution.py:28
  14.5 1.4 %collective-permute-done.4 = f32[32,128]{1,0:T(8,128)S(1)} collective-permute-done((f32[32,128]{1,0:T(8,128)S(1)}, f32[32,128]{1,0:T(8,128)S(1)}, u32[]{:S(2)}, u32[]{:S(2)}) %collective-permute-start.4) | collective-permute-done | bytes 16416 | tf_op jit(solution)/shard_map/ppermute | solution.py:28
  16.0 2.7 %collective-permute-start.5 = (f32[32,128]{1,0:T(8,128)S(1)}, f32[32,128]{1,0:T(8,128)S(1)}, u32[]{:S(2)}, u32[]{:S(2)}) collective-permute-start(f32[32,128]{1,0:T(8,128)S(1)} %add.20), channel_id=1, source_target_pairs={{0,17},{1,16},{2,19},{3,18},{4,21},{5,20},{6,23},{7,22},{8,25},{9,... | collective-permute-start | bytes 49160 | tf_op jit(solution)/shard_map/ppermute | solution.py:28
  18.7 0.0 copy-done.1
  18.7 0.1 copy.6.scale
  18.8 1.3 %collective-permute-done.5 = f32[32,128]{1,0:T(8,128)S(1)} collective-permute-done((f32[32,128]{1,0:T(8,128)S(1)}, f32[32,128]{1,0:T(8,128)S(1)}, u32[]{:S(2)}, u32[]{:S(2)}) %collective-permute-start.5) | collective-permute-done | bytes 16416 | tf_op jit(solution)/shard_map/ppermute | solution.py:28
  20.1 3.2 %factor_apply.1 = (f32[80,48,128]{2,1,0:T(8,128)}, f32[80,80]{1,0:T(8,128)}) custom-call(f32[32,128]{1,0:T(8,128)S(1)} %add.21.packed, f32[80,1]{1,0:T(8,128)S(1)} %copy.6.scale, bf16[128,6144]{1,0:T(8,128)(2,1)S(1)} %get-tuple-element.12.modes_panel, bf16[32,6144]{1,0:T(8,128)(2,1)S(1)} %get-tuple-element.15.snaps_panel), custom_call_target="tpu_custom_call" | custom-call | tf_op jit(solution)/shard_map/factor_apply/pallas_call | solution.py:316
  (6 shorter events, 0.0 us)
Async XLA Ops:
  0.6 1.7 %copy-start = (f32[64,2,3072]{2,1,0:T(2,128)S(1)}, f32[64,2,3072]{2,1,0:T(2,128)}, u32[]{:S(2)}) copy-start(f32[64,2,3072]{2,1,0:T(2,128)} %param.3) | copy-start | bytes 4718596
  1.8 1.6 %collective-permute-start = (f32[384,128]{1,0:T(8,128)S(1)}, f32[384,128]{1,0:T(8,128)S(1)}, u32[]{:S(2)}, u32[]{:S(2)}) collective-permute-start(f32[384,128]{1,0:T(8,128)S(1)} %get-tuple-element.11), channel_id=1, source_target_pairs={{0,1},{1,0},{2,3},{3,2},{4,5},{5,4},{6,7},{7,6},{8,9},{9,8},{10,11... | collective-permute-start | bytes 589832 | tf_op jit(solution)/shard_map/ppermute | solution.py:287
  2.4 16.3 %copy-start.1 = (f32[64]{0:T(128)S(1)}, f32[64]{0:T(128)}, u32[]{:S(2)}) copy-start(f32[64]{0:T(128)} %param.4) | copy-start | bytes 772
  4.2 1.3 %collective-permute-start.1 = (f32[32,128]{1,0:T(8,128)S(1)}, f32[32,128]{1,0:T(8,128)S(1)}, u32[]{:S(2)}, u32[]{:S(2)}) collective-permute-start(f32[32,128]{1,0:T(8,128)S(1)} %get-tuple-element.14), channel_id=1, source_target_pairs={{0,1},{1,0},{2,3},{3,2},{4,5},{5,4},{6,7},{7,6},{8,9},{9,8},{10,11... | collective-permute-start | bytes 49160 | tf_op jit(solution)/shard_map/ppermute | solution.py:28
  5.5 4.0 %collective-permute-start.2 = (f32[32,128]{1,0:T(8,128)S(1)}, f32[32,128]{1,0:T(8,128)S(1)}, u32[]{:S(2)}, u32[]{:S(2)}) collective-permute-start(f32[32,128]{1,0:T(8,128)S(1)} %add.17), channel_id=1, source_target_pairs={{0,3},{1,2},{2,1},{3,0},{4,7},{5,6},{6,5},{7,4},{8,11},{9,10},{10,... | collective-permute-start | bytes 49160 | tf_op jit(solution)/shard_map/ppermute | solution.py:28
  9.5 3.2 %collective-permute-start.3 = (f32[32,128]{1,0:T(8,128)S(1)}, f32[32,128]{1,0:T(8,128)S(1)}, u32[]{:S(2)}, u32[]{:S(2)}) collective-permute-start(f32[32,128]{1,0:T(8,128)S(1)} %add.18), channel_id=1, source_target_pairs={{0,5},{1,4},{2,7},{3,6},{4,1},{5,0},{6,3},{7,2},{8,13},{9,12},{10,... | collective-permute-start | bytes 49160 | tf_op jit(solution)/shard_map/ppermute | solution.py:28
  12.7 3.2 %collective-permute-start.4 = (f32[32,128]{1,0:T(8,128)S(1)}, f32[32,128]{1,0:T(8,128)S(1)}, u32[]{:S(2)}, u32[]{:S(2)}) collective-permute-start(f32[32,128]{1,0:T(8,128)S(1)} %add.19), channel_id=1, source_target_pairs={{0,9},{1,8},{2,11},{3,10},{4,13},{5,12},{6,15},{7,14},{8,1},{9,0},... | collective-permute-start | bytes 49160 | tf_op jit(solution)/shard_map/ppermute | solution.py:28
  16.0 4.2 %collective-permute-start.5 = (f32[32,128]{1,0:T(8,128)S(1)}, f32[32,128]{1,0:T(8,128)S(1)}, u32[]{:S(2)}, u32[]{:S(2)}) collective-permute-start(f32[32,128]{1,0:T(8,128)S(1)} %add.20), channel_id=1, source_target_pairs={{0,17},{1,16},{2,19},{3,18},{4,21},{5,20},{6,23},{7,22},{8,25},{9,... | collective-permute-start | bytes 49160 | tf_op jit(solution)/shard_map/ppermute | solution.py:28

commit v8 on v7

--- a/solution.py
+++ b/solution.py
@@ -20,12 +20,15 @@
 
 def total(value):
     servers, cores = lax.axis_size("srv"), lax.axis_size("grp")
-    if servers & (servers - 1) or cores != 2:
+    if servers & (servers - 1) or servers < 4 or cores != 2:
         return lax.psum(value, AXES)
     count = servers * cores
-    masks = [1] + [2 * bit + 1 for bit in (1 << p for p in range(servers.bit_length() - 1))]
-    for mask in masks:
-        value = value + lax.ppermute(value, AXES, [(i, i ^ mask) for i in range(count)])
+    masks = [2 << p | 1 for p in range(servers.bit_length() - 1)]
+    rounds = [[1], [masks[0], masks[1], masks[0] | masks[1]]] + [[mask] for mask in masks[2:]]
+    for masks in rounds:
+        parts = [lax.ppermute(value, AXES, [(i, i ^ m) for i in range(count)]) for m in masks]
+        for part in parts:
+            value = value + part
     return value
 
 
@@ -51,15 +54,13 @@
 
 
 def modes_kernel(modes, panel, gram):
-    count = gram.shape[0]
+    count = gram.shape[1]
     slabs = modes.shape[0] // count
     for i in range(slabs):
         high, low = split(modes[pl.ds(i, count, stride=slabs), :])
         panel[:count, i * LANES:(i + 1) * LANES] = high
         panel[count:, i * LANES:(i + 1) * LANES] = low
-    acc = rows_times_rows(panel[...], panel[:count])
-    cross = acc[count:]
-    gram[...] = acc[:count] + cross + cross.T
+    gram[...] = rows_times_rows(panel[...], panel[:count])
 
 
 def pick_kernel(rows, source, keep, send, snaps, sem):
@@ -76,7 +77,7 @@
 
 
 def snaps_kernel(rows, keep, got, modes_panel, modes_gram, panel, packed):
-    snaps, modes = panel.shape[0] // 2, modes_gram.shape[0]
+    snaps, modes = panel.shape[0] // 2, modes_gram.shape[1]
     tiles = keep.shape[0] // (snaps * rows)
     kept = [lax.axis_index("grp") == h for h in (0, 1)]
     for h in (0, 1):
@@ -86,18 +87,13 @@
             at = (h * tiles * rows + i) * LANES
             panel[:snaps, at:at + LANES] = high
             panel[snaps:, at:at + LANES] = low
-    with_modes = rows_times_rows(modes_panel[...], panel[...])
-    own = rows_times_rows(panel[...], panel[:snaps])
-    top = with_modes[:modes]
-    low_row = (top[:, :snaps] + top[:, snaps:] + with_modes[modes:, :snaps]).T
-    own = own[:snaps] + own[snaps:] + own[snaps:].T
-    whole = jnp.concatenate(
-        [
-            jnp.concatenate([modes_gram[...], jnp.zeros((modes, snaps), F32)], axis=1),
-            jnp.concatenate([low_row, own], axis=1),
-        ],
-        axis=0,
-    )
+    high = jnp.concatenate([modes_panel[:modes], panel[:snaps]], axis=0)
+    low = jnp.concatenate([modes_panel[modes:], panel[snaps:]], axis=0)
+    both = rows_times_rows(panel[...], high)
+    last = both[:snaps] + both[snaps:] + rows_times_rows(panel[:snaps], low)
+    cross = modes_gram[modes:]
+    whole = jnp.concatenate([modes_gram[:modes] + cross + cross.T, jnp.zeros((modes, snaps), F32)], axis=1)
+    whole = jnp.concatenate([whole, last], axis=0)
     for g, group in enumerate(packing(modes + snaps)):
         parts = [whole[r * BLOCK:(r + 1) * BLOCK, :(r + 1) * BLOCK] for r in group]
         spare = LANES - sum(p.shape[1] for p in parts)
@@ -153,7 +149,7 @@
     return m
 
 
-def factor_tiles(tiles, entries, columns_of, rows_of, solved_of):
+def factor_tiles(tiles, lower, entries, columns_of, rows_of, solved_of):
     count = len(tiles)
     lane = lax.broadcasted_iota(jnp.int32, (TILE, LANES), 1)
     tiles = list(tiles)
@@ -162,9 +158,9 @@
     for b in range(2):
         columns_of[b] = jnp.zeros((square, LANES), F32)
         rows_of[b] = jnp.zeros((square, LANES), F32)
-    diagonal = [spread_column(tiles[0], j) for j in range(TILE)]
-    below = [[spread_column(x, j) for j in range(TILE)] for x in tiles[1:]]
-    following = [spread_column(tiles[1], TILE + j) for j in range(TILE)]
+    diagonal = [spread_column(lower[0], j) for j in range(TILE)]
+    below = [[spread_column(x, j) for j in range(TILE)] for x in lower[1:]]
+    following = [spread_column(lower[1], TILE + j) for j in range(TILE)]
     for t in range(count):
         at = t * TILE
         slot = entries.at[t]
@@ -212,7 +208,7 @@
     return upper, inverse
 
 
-def apply_kernel(cells, packed, scale, modes_panel, snaps_panel, out, factor, left, buf, lower_out, sems, *spread):
+def apply_kernel(cells, packed, scale, modes_panel, snaps_panel, out, factor, buf, lower_out, sems, *spread):
     modes, snaps = modes_panel.shape[0] // 2, snaps_panel.shape[0] // 2
     width = modes + snaps
     lane = lax.broadcasted_iota(jnp.int32, (BLOCK, LANES), 1)
@@ -229,9 +225,10 @@
     r = lax.broadcasted_iota(jnp.int32, (LANES, LANES), 0)
     c = lax.broadcasted_iota(jnp.int32, (LANES, LANES), 1)
     full = jnp.where(r >= c, lower, lower.T)
-    upper, inverse = factor_tiles([full[i:i + TILE] for i in range(0, width, TILE)], *spread)
-    for i, x in enumerate(inverse):
-        left[i * TILE:(i + 1) * TILE, :] = x
+    upper, inverse = factor_tiles(
+        *([x[i:i + TILE] for i in range(0, width, TILE)] for x in (full, lower)), *spread
+    )
+    left = jnp.concatenate(inverse, axis=0)
     whole = jnp.concatenate(upper + [jnp.zeros((LANES - width, LANES), F32)], axis=0).T
     whole = jnp.where(r >= c, whole, 0.0)[:width, :width]
     lower_out[...] = whole * scale[...]
@@ -291,7 +288,7 @@
         modes_kernel,
         out_shape=(
             jax.ShapeDtypeStruct((2 * modes, slabs * LANES), BF16),
-            jax.ShapeDtypeStruct((modes, modes), F32),
+            jax.ShapeDtypeStruct((2 * modes, modes), F32),
         ),
         in_specs=[VMEM],
         out_specs=(VMEM, VMEM),
@@ -322,7 +319,6 @@
         in_specs=[VMEM] * 4,
         out_specs=(ANY, ANY),
         scratch_shapes=[
-            pltpu.VMEM((width, LANES), F32),
             pltpu.VMEM((width, slabs, LANES), F32),
             pltpu.VMEM((width, width), F32),
             pltpu.SemaphoreType.DMA((chunk + 1,)),

time: 23.5 us -> 23.1 us (0.983)
  starting transfers between devices: 9.84 us -> 8.89 us
  waiting for transfers between devices: 6.54 us -> 7.31 us
  Pallas kernels: 6.2 us -> 5.93 us
    ppermute x5 -> x6, starting transfers between devices: 9.28 us -> 8.33 us  [total(): lax.ppermute(value, AXES, [(i, i ^ m) for i in range(count)])]
    ppermute x5 -> x6, waiting for transfers between devices: 6.5 us -> 7.19 us  [total(): lax.ppermute(value, AXES, [(i, i ^ m) for i in range(count)])]
  transfers between devices with their start and end apart: 6 -> 7, of which waited for: 5 -> 7; matrix products, arithmetic and copies ran while one was open for 0% -> 0% of each run, Pallas kernels for 4% -> 4%
where the time goes in v8:
time: 23.1 us; the launch traced here: 22.9 us
  starting transfers between devices  8.89 us (38%)
  waiting for transfers between devices  7.31 us (32%)
  Pallas kernels  5.93 us (26%)
  between operations  0.66 us (3%)
    ppermute x6, starting transfers between devices, total(): lax.ppermute(value, AXES, [(i, i ^ m) for i in range(count)])  8.33 us
    ppermute x6, waiting for transfers between devices, total(): lax.ppermute(value, AXES, [(i, i ^ m) for i in range(count)])  7.19 us
    pallas_call x1, Pallas kernels, per_device(): pl.pallas_call(functools.partial(apply_kernel, cells), out_shape=(jax.Sha...  3.23 us
    pallas_call x1, Pallas kernels, per_device(): pl.pallas_call(functools.partial(pick_kernel, rows), out_shape=(part, par...  1.15 us
    pallas_call x1, Pallas kernels, per_device(): pl.pallas_call(modes_kernel, out_shape=(jax.ShapeDtypeStruct((2 * modes,...  0.94 us
    pallas_call x1, Pallas kernels, per_device(): pl.pallas_call(functools.partial(snaps_kernel, rows), out_shape=(jax.Shap...  0.61 us
    ppermute x1, starting transfers between devices, per_device(): got = lax.ppermute(send, 'grp', [(0, 1), (1, 0)])  0.56 us
  transfers between devices with their start and end apart: 7, of which 7 were waited for; matrix products, arithmetic and copies ran while one was open for 0% of the time, Pallas kernels for 4%

profile of v8, /device:TPU:0, one launch (start us, length us, event | category | flops | bytes accessed | tf_op | source)
XLA Modules:
  0.0 22.9 jit_solution(2141383270362186210)
XLA Ops:
  0.6 0.0 copy-start
  0.6 1.1 %pick_rows.1 = (f32[384,128]{1,0:T(8,128)S(1)}, f32[384,128]{1,0:T(8,128)S(1)}) custom-call(f32[768,128]{1,0:T(8,128)} %bitcast.19), custom_call_target="tpu_custom_call" | custom-call | flops 1000000000 | bytes 786432 | tf_op jit(solution)/shard_map/pick_rows/pallas_call | solution.py:274
  1.8 0.6 %collective-permute-start = (f32[384,128]{1,0:T(8,128)S(1)}, f32[384,128]{1,0:T(8,128)S(1)}, u32[]{:S(2)}, u32[]{:S(2)}) collective-permute-start(f32[384,128]{1,0:T(8,128)S(1)} %get-tuple-element.11), channel_id=1, source_target_pairs={{0,1},{1,0},{2,3},{3,2},{4,5},{5,4},{6,7},{7,6},{8,9},{9,8},{10,11... | collective-permute-start | bytes 589832 | tf_op jit(solution)/shard_map/ppermute | solution.py:284
  2.4 0.0 copy-done
  2.4 0.0 copy-start.1
  2.4 0.9 %modes_gram.1 = (bf16[128,6144]{1,0:T(8,128)(2,1)S(1)}, f32[128,64]{1,0:T(8,128)S(1)}) custom-call(f32[3072,128]{1,0:T(8,128)S(1)} %bitcast.17), custom_call_target="tpu_custom_call" | custom-call | flops 100000000 | bytes 1572864 | tf_op jit(solution)/shard_map/modes_gram/pallas_call | solution.py:287
  3.3 0.1 collective-permute-done.got
  3.4 0.6 %snaps_gram.1 = (bf16[32,6144]{1,0:T(8,128)(2,1)S(1)}, f32[32,128]{1,0:T(8,128)S(1)}) custom-call(f32[384,128]{1,0:T(8,128)S(1)} %get-tuple-element.10.keep, f32[384,128]{1,0:T(8,128)S(1)} %collective-permute-done.got, bf16[128,6144]{1,0:T(8,128)(2,1)S(1)} %get-tuple-element.12.modes_panel, f32[128,64]{1,0:T(8,128)S(1)} %get-tuple-element.13.modes_gram), custom_call_target="tpu_custom_call" | custom-call | flops 100000000 | bytes 1000000 | tf_op jit(solution)/shard_map/snaps_gram/pallas_call | solution.py:299
  4.0 0.4 %collective-permute-start.1 = (f32[32,128]{1,0:T(8,128)S(1)}, f32[32,128]{1,0:T(8,128)S(1)}, u32[]{:S(2)}, u32[]{:S(2)}) collective-permute-start(f32[32,128]{1,0:T(8,128)S(1)} %get-tuple-element.14), channel_id=1, source_target_pairs={{0,1},{1,0},{2,3},{3,2},{4,5},{5,4},{6,7},{7,6},{8,9},{9,8},{10,11... | collective-permute-start | bytes 49160 | tf_op jit(solution)/shard_map/ppermute | solution.py:29
  4.4 0.8 %collective-permute-done.1 = f32[32,128]{1,0:T(8,128)S(1)} collective-permute-done((f32[32,128]{1,0:T(8,128)S(1)}, f32[32,128]{1,0:T(8,128)S(1)}, u32[]{:S(2)}, u32[]{:S(2)}) %collective-permute-start.1) | collective-permute-done | bytes 16416 | tf_op jit(solution)/shard_map/ppermute | solution.py:29
  5.3 3.5 %collective-permute-start.4 = (f32[32,128]{1,0:T(8,128)S(1)}, f32[32,128]{1,0:T(8,128)S(1)}, u32[]{:S(2)}, u32[]{:S(2)}) collective-permute-start(f32[32,128]{1,0:T(8,128)S(1)} %add.20), channel_id=1, source_target_pairs={{0,7},{1,6},{2,5},{3,4},{4,3},{5,2},{6,1},{7,0},{8,15},{9,14},{10,... | collective-permute-start | bytes 49160 | tf_op jit(solution)/shard_map/ppermute | solution.py:29
  8.8 0.5 %collective-permute-start.3 = (f32[32,128]{1,0:T(8,128)S(1)}, f32[32,128]{1,0:T(8,128)S(1)}, u32[]{:S(2)}, u32[]{:S(2)}) collective-permute-start(f32[32,128]{1,0:T(8,128)S(1)} %add.20), channel_id=1, source_target_pairs={{0,5},{1,4},{2,7},{3,6},{4,1},{5,0},{6,3},{7,2},{8,13},{9,12},{10,... | collective-permute-start | bytes 49160 | tf_op jit(solution)/shard_map/ppermute | solution.py:29
  9.3 0.1 collective-permute-start.2
  9.4 0.9 %collective-permute-done.4 = f32[32,128]{1,0:T(8,128)S(1)} collective-permute-done((f32[32,128]{1,0:T(8,128)S(1)}, f32[32,128]{1,0:T(8,128)S(1)}, u32[]{:S(2)}, u32[]{:S(2)}) %collective-permute-start.4) | collective-permute-done | bytes 16416 | tf_op jit(solution)/shard_map/ppermute | solution.py:29
  10.3 1.7 %collective-permute-done.3 = f32[32,128]{1,0:T(8,128)S(1)} collective-permute-done((f32[32,128]{1,0:T(8,128)S(1)}, f32[32,128]{1,0:T(8,128)S(1)}, u32[]{:S(2)}, u32[]{:S(2)}) %collective-permute-start.3) | collective-permute-done | bytes 16416 | tf_op jit(solution)/shard_map/ppermute | solution.py:29
  12.0 0.5 %collective-permute-done.2 = f32[32,128]{1,0:T(8,128)S(1)} collective-permute-done((f32[32,128]{1,0:T(8,128)S(1)}, f32[32,128]{1,0:T(8,128)S(1)}, u32[]{:S(2)}, u32[]{:S(2)}) %collective-permute-start.2) | collective-permute-done | bytes 16416 | tf_op jit(solution)/shard_map/ppermute | solution.py:29
  12.5 1.4 %collective-permute-start.5 = (f32[32,128]{1,0:T(8,128)S(1)}, f32[32,128]{1,0:T(8,128)S(1)}, u32[]{:S(2)}, u32[]{:S(2)}) collective-permute-start(f32[32,128]{1,0:T(8,128)S(1)} %add_add_fusion), channel_id=1, source_target_pairs={{0,9},{1,8},{2,11},{3,10},{4,13},{5,12},{6,15},{7,14},{8,1},{9,0},... | collective-permute-start | bytes 49160 | tf_op jit(solution)/shard_map/ppermute | solution.py:29
  13.9 1.8 %collective-permute-done.5 = f32[32,128]{1,0:T(8,128)S(1)} collective-permute-done((f32[32,128]{1,0:T(8,128)S(1)}, f32[32,128]{1,0:T(8,128)S(1)}, u32[]{:S(2)}, u32[]{:S(2)}) %collective-permute-start.5) | collective-permute-done | bytes 16416 | tf_op jit(solution)/shard_map/ppermute | solution.py:29
  15.6 2.4 %collective-permute-start.6 = (f32[32,128]{1,0:T(8,128)S(1)}, f32[32,128]{1,0:T(8,128)S(1)}, u32[]{:S(2)}, u32[]{:S(2)}) collective-permute-start(f32[32,128]{1,0:T(8,128)S(1)} %add.24), channel_id=1, source_target_pairs={{0,17},{1,16},{2,19},{3,18},{4,21},{5,20},{6,23},{7,22},{8,25},{9,... | collective-permute-start | bytes 49160 | tf_op jit(solution)/shard_map/ppermute | solution.py:29
  18.0 0.0 copy-done.1
  18.0 0.1 copy.6.scale
  18.1 1.5 %collective-permute-done.6 = f32[32,128]{1,0:T(8,128)S(1)} collective-permute-done((f32[32,128]{1,0:T(8,128)S(1)}, f32[32,128]{1,0:T(8,128)S(1)}, u32[]{:S(2)}, u32[]{:S(2)}) %collective-permute-start.6) | collective-permute-done | bytes 16416 | tf_op jit(solution)/shard_map/ppermute | solution.py:29
  19.7 3.2 %factor_apply.1 = (f32[80,48,128]{2,1,0:T(8,128)}, f32[80,80]{1,0:T(8,128)}) custom-call(f32[32,128]{1,0:T(8,128)S(1)} %add.25.packed, f32[80,1]{1,0:T(8,128)S(1)} %copy.6.scale, bf16[128,6144]{1,0:T(8,128)(2,1)S(1)} %get-tuple-element.12.modes_panel, bf16[32,6144]{1,0:T(8,128)(2,1)S(1)} %get-tuple-element.15.snaps_panel), custom_call_target="tpu_custom_call" | custom-call | tf_op jit(solution)/shard_map/factor_apply/pallas_call | solution.py:313
  (5 shorter events, 0.0 us)
Async XLA Ops:
  0.6 1.7 %copy-start = (f32[64,2,3072]{2,1,0:T(2,128)S(1)}, f32[64,2,3072]{2,1,0:T(2,128)}, u32[]{:S(2)}) copy-start(f32[64,2,3072]{2,1,0:T(2,128)} %param.3) | copy-start | bytes 4718596
  1.8 1.6 %collective-permute-start = (f32[384,128]{1,0:T(8,128)S(1)}, f32[384,128]{1,0:T(8,128)S(1)}, u32[]{:S(2)}, u32[]{:S(2)}) collective-permute-start(f32[384,128]{1,0:T(8,128)S(1)} %get-tuple-element.11), channel_id=1, source_target_pairs={{0,1},{1,0},{2,3},{3,2},{4,5},{5,4},{6,7},{7,6},{8,9},{9,8},{10,11... | collective-permute-start | bytes 589832 | tf_op jit(solution)/shard_map/ppermute | solution.py:284
  2.4 15.7 %copy-start.1 = (f32[64]{0:T(128)S(1)}, f32[64]{0:T(128)}, u32[]{:S(2)}) copy-start(f32[64]{0:T(128)} %param.4) | copy-start | bytes 772
  4.0 1.2 %collective-permute-start.1 = (f32[32,128]{1,0:T(8,128)S(1)}, f32[32,128]{1,0:T(8,128)S(1)}, u32[]{:S(2)}, u32[]{:S(2)}) collective-permute-start(f32[32,128]{1,0:T(8,128)S(1)} %get-tuple-element.14), channel_id=1, source_target_pairs={{0,1},{1,0},{2,3},{3,2},{4,5},{5,4},{6,7},{7,6},{8,9},{9,8},{10,11... | collective-permute-start | bytes 49160 | tf_op jit(solution)/shard_map/ppermute | solution.py:29
  5.3 5.0 %collective-permute-start.4 = (f32[32,128]{1,0:T(8,128)S(1)}, f32[32,128]{1,0:T(8,128)S(1)}, u32[]{:S(2)}, u32[]{:S(2)}) collective-permute-start(f32[32,128]{1,0:T(8,128)S(1)} %add.20), channel_id=1, source_target_pairs={{0,7},{1,6},{2,5},{3,4},{4,3},{5,2},{6,1},{7,0},{8,15},{9,14},{10,... | collective-permute-start | bytes 49160 | tf_op jit(solution)/shard_map/ppermute | solution.py:29
  8.8 3.2 %collective-permute-start.3 = (f32[32,128]{1,0:T(8,128)S(1)}, f32[32,128]{1,0:T(8,128)S(1)}, u32[]{:S(2)}, u32[]{:S(2)}) collective-permute-start(f32[32,128]{1,0:T(8,128)S(1)} %add.20), channel_id=1, source_target_pairs={{0,5},{1,4},{2,7},{3,6},{4,1},{5,0},{6,3},{7,2},{8,13},{9,12},{10,... | collective-permute-start | bytes 49160 | tf_op jit(solution)/shard_map/ppermute | solution.py:29
  9.3 3.2 %collective-permute-start.2 = (f32[32,128]{1,0:T(8,128)S(1)}, f32[32,128]{1,0:T(8,128)S(1)}, u32[]{:S(2)}, u32[]{:S(2)}) collective-permute-start(f32[32,128]{1,0:T(8,128)S(1)} %add.20), channel_id=1, source_target_pairs={{0,3},{1,2},{2,1},{3,0},{4,7},{5,6},{6,5},{7,4},{8,11},{9,10},{10,... | collective-permute-start | bytes 49160 | tf_op jit(solution)/shard_map/ppermute | solution.py:29
  12.5 3.2 %collective-permute-start.5 = (f32[32,128]{1,0:T(8,128)S(1)}, f32[32,128]{1,0:T(8,128)S(1)}, u32[]{:S(2)}, u32[]{:S(2)}) collective-permute-start(f32[32,128]{1,0:T(8,128)S(1)} %add_add_fusion), channel_id=1, source_target_pairs={{0,9},{1,8},{2,11},{3,10},{4,13},{5,12},{6,15},{7,14},{8,1},{9,0},... | collective-permute-start | bytes 49160 | tf_op jit(solution)/shard_map/ppermute | solution.py:29
  15.6 4.1 %collective-permute-start.6 = (f32[32,128]{1,0:T(8,128)S(1)}, f32[32,128]{1,0:T(8,128)S(1)}, u32[]{:S(2)}, u32[]{:S(2)}) collective-permute-start(f32[32,128]{1,0:T(8,128)S(1)} %add.24), channel_id=1, source_target_pairs={{0,17},{1,16},{2,19},{3,18},{4,21},{5,20},{6,23},{7,22},{8,25},{9,... | collective-permute-start | bytes 49160 | tf_op jit(solution)/shard_map/ppermute | solution.py:29

commit v9 on v8

--- a/solution.py
+++ b/solution.py
@@ -11,6 +11,7 @@
 LANES = 128
 TILE = 8
 BLOCK = 16
+PIECES = 2
 F32, BF16 = jnp.float32, jnp.bfloat16
 VMEM = pl.BlockSpec(memory_space=pltpu.VMEM)
 ANY = pl.BlockSpec(memory_space=pl.ANY)
@@ -53,38 +54,39 @@
     return lax.dot_general(a, b, (((1,), (1,)), ((), ())), preferred_element_type=F32)
 
 
-def modes_kernel(modes, panel, gram):
-    count = gram.shape[1]
-    slabs = modes.shape[0] // count
-    for i in range(slabs):
-        high, low = split(modes[pl.ds(i, count, stride=slabs), :])
-        panel[:count, i * LANES:(i + 1) * LANES] = high
-        panel[count:, i * LANES:(i + 1) * LANES] = low
-    gram[...] = rows_times_rows(panel[...], panel[:count])
-
-
-def pick_kernel(rows, source, keep, send, snaps, sem):
-    copy = pltpu.make_async_copy(source, snaps, sem)
-    copy.start()
-    copy.wait()
-    core = lax.axis_index("grp")
-    count = keep.shape[0] // rows
-    stride = snaps.shape[0] // count
-    for r in range(rows):
-        at = slice(r * count, (r + 1) * count)
-        keep[at] = snaps[pl.ds(core * rows + r, count, stride=stride), :]
-        send[at] = snaps[pl.ds((1 - core) * rows + r, count, stride=stride), :]
+def modes_kernel(source, panel, gram, buf, sems):
+    count, slabs, _ = source.shape
+    flat = buf.reshape(count * slabs, LANES)
+    pieces = sems.shape[0]
+    step = slabs // pieces
+    copies = []
+    for p in range(pieces):
+        part = (slice(None), pl.ds(p * step, step))
+        copies.append(pltpu.make_async_copy(source.at[part], buf.at[part], sems.at[p]))
+        copies[-1].start()
+    terms = []
+    for p in range(pieces):
+        copies[p].wait()
+        for i in range(p * step, (p + 1) * step):
+            high, low = split(flat[pl.ds(i, count, stride=slabs), :])
+            panel[:count, i * LANES:(i + 1) * LANES] = high
+            panel[count:, i * LANES:(i + 1) * LANES] = low
+        cols = slice(p * step * LANES, (p + 1) * step * LANES)
+        terms.append(rows_times_rows(panel[:, cols], panel[:count, cols]))
+    gram[...] = total_of(terms)
 
 
 def snaps_kernel(rows, keep, got, modes_panel, modes_gram, panel, packed):
     snaps, modes = panel.shape[0] // 2, modes_gram.shape[1]
-    tiles = keep.shape[0] // (snaps * rows)
-    kept = [lax.axis_index("grp") == h for h in (0, 1)]
+    core = lax.axis_index("grp")
+    stride = keep.shape[0] // snaps
+    here = stride // 2
     for h in (0, 1):
-        for i in range(tiles * rows):
-            place = pl.ds((i % rows) * snaps * tiles + i // rows, snaps, stride=tiles)
-            high, low = split(jnp.where(kept[h], keep[place, :], got[place, :]))
-            at = (h * tiles * rows + i) * LANES
+        for i in range(here):
+            start = i // rows * 2 * rows + core * rows + i % rows
+            place = pl.ds(start, snaps, stride=stride)
+            high, low = split(jnp.where(core == h, keep[place, :], got[place, :]))
+            at = (h * here + i) * LANES
             panel[:snaps, at:at + LANES] = high
             panel[snaps:, at:at + LANES] = low
     high = jnp.concatenate([modes_panel[:modes], panel[:snaps]], axis=0)
@@ -265,23 +267,11 @@
     cores = lax.axis_size("grp")
     cells = rows * cols * lax.axis_size("srv") * cores
     fields = basis_modes.reshape(modes, rows, tiles, LANES).transpose(0, 2, 1, 3)
-    fields = fields.reshape(modes * slabs, LANES)
+    fields = pltpu.with_memory_space_constraint(fields.reshape(modes, slabs, LANES), pltpu.HBM)
     own = snapshots.reshape(snaps, cores * rows, tiles // cores, LANES)
     own = with_layout_constraint(own, Layout((0, 2, 1, 3))).transpose(0, 2, 1, 3)
     own = own.reshape(snaps * tiles * rows, LANES)
-    own = pltpu.with_memory_space_constraint(own, pltpu.HBM)
-    part = jax.ShapeDtypeStruct((own.shape[0] // cores, LANES), F32)
-    keep, send = pl.pallas_call(
-        functools.partial(pick_kernel, rows),
-        out_shape=(part, part),
-        in_specs=[HBM],
-        out_specs=(VMEM, VMEM),
-        scratch_shapes=[pltpu.VMEM(own.shape, F32), pltpu.SemaphoreType.DMA],
-        compiler_params=PARAMS,
-        cost_estimate=pl.CostEstimate(flops=10**9, bytes_accessed=own.size * 8, transcendentals=0),
-        name="pick_rows",
-    )(own)
-    got = lax.ppermute(send, "grp", [(0, 1), (1, 0)])
+    got = lax.ppermute(own, "grp", [(0, 1), (1, 0)])
 
     chunk = 6
     modes_panel, modes_gram = pl.pallas_call(
@@ -290,8 +280,9 @@
             jax.ShapeDtypeStruct((2 * modes, slabs * LANES), BF16),
             jax.ShapeDtypeStruct((2 * modes, modes), F32),
         ),
-        in_specs=[VMEM],
+        in_specs=[HBM],
         out_specs=(VMEM, VMEM),
+        scratch_shapes=[pltpu.VMEM(fields.shape, F32), pltpu.SemaphoreType.DMA((PIECES,))],
         cost_estimate=pl.CostEstimate(flops=10**8, bytes_accessed=fields.size * 4, transcendentals=0),
         compiler_params=PARAMS,
         name="modes_gram",
@@ -307,7 +298,7 @@
         compiler_params=PARAMS,
         cost_estimate=pl.CostEstimate(flops=10**8, bytes_accessed=10**6, transcendentals=0),
         name="snaps_gram",
-    )(keep, got, modes_panel, modes_gram)
+    )(own, got, modes_panel, modes_gram)
     packed = total(packed)
     scale = jnp.concatenate([weights, jnp.ones((snaps,), F32)])
     new_modes, factor = pl.pallas_call(

time: 23.1 us -> 22.8 us (0.987)
  starting transfers between devices: 8.89 us -> 8.63 us
    pallas_call x1 -> x0, Pallas kernels: 1.15 us -> none  [per_device(): pl.pallas_call(functools.partial(pick_kernel, rows), out_shape=(part, par...]
    pallas_call x1, Pallas kernels: 0.94 us -> 2.08 us  [per_device(): pl.pallas_call(modes_kernel, out_shape=(jax.ShapeDtypeStruct((2 * modes,...]
    ppermute x6, starting transfers between devices: 8.33 us -> 8.07 us  [total(): lax.ppermute(value, AXES, [(i, i ^ m) for i in range(count)])]
  transfers between devices with their start and end apart: 7 -> 7, of which waited for: 7 -> 6; matrix products, arithmetic and copies ran while one was open for 0% -> 0% of each run, Pallas kernels for 4% -> 9%
where the time goes in v9:
time: 22.8 us; the launch traced here: 22.6 us
  starting transfers between devices  8.63 us (38%)
  waiting for transfers between devices  7.25 us (32%)
  Pallas kernels  5.95 us (26%)
  between operations  0.68 us (3%)
    ppermute x6, starting transfers between devices, total(): lax.ppermute(value, AXES, [(i, i ^ m) for i in range(count)])  8.07 us
    ppermute x6, waiting for transfers between devices, total(): lax.ppermute(value, AXES, [(i, i ^ m) for i in range(count)])  7.25 us
    pallas_call x1, Pallas kernels, per_device(): pl.pallas_call(functools.partial(apply_kernel, cells), out_shape=(jax.Sha...  3.24 us
    pallas_call x1, Pallas kernels, per_device(): pl.pallas_call(modes_kernel, out_shape=(jax.ShapeDtypeStruct((2 * modes,...  2.08 us
    pallas_call x1, Pallas kernels, per_device(): pl.pallas_call(functools.partial(snaps_kernel, rows), out_shape=(jax.Shap...  0.63 us
    ppermute x1, starting transfers between devices, per_device(): got = lax.ppermute(own, 'grp', [(0, 1), (1, 0)])  0.56 us
  transfers between devices with their start and end apart: 7, of which 6 were waited for; matrix products, arithmetic and copies ran while one was open for 0% of the time, Pallas kernels for 9%

profile of v9, /device:TPU:0, one launch (start us, length us, event | category | flops | bytes accessed | tf_op | source)
XLA Modules:
  0.0 22.6 jit_solution(1284152040057714186)
XLA Ops:
  0.6 0.0 copy-start
  0.6 0.6 %collective-permute-start = (f32[768,128]{1,0:T(8,128)}, f32[768,128]{1,0:T(8,128)S(1)}, u32[]{:S(2)}, u32[]{:S(2)}) collective-permute-start(f32[768,128]{1,0:T(8,128)} %bitcast.17), channel_id=1, source_target_pairs={{0,1},{1,0},{2,3},{3,2},{4,5},{5,4},{6,7},{7,6},{8,9},{9,8},{10,11... | collective-permute-start | bytes 1179656 | tf_op jit(solution)/shard_map/ppermute | solution.py:274
  1.2 2.1 %modes_gram.1 = (bf16[128,6144]{1,0:T(8,128)(2,1)S(1)}, f32[128,64]{1,0:T(8,128)S(1)}) custom-call(f32[64,48,128]{2,1,0:T(8,128)} %bitcast.19), custom_call_target="tpu_custom_call" | custom-call | flops 100000000 | bytes 1572864 | tf_op jit(solution)/shard_map/modes_gram/pallas_call | solution.py:277
  3.3 0.0 copy-start.1
  3.3 0.0 collective-permute-done.got
  3.3 0.0 copy-done
  3.3 0.6 %snaps_gram.1 = (bf16[32,6144]{1,0:T(8,128)(2,1)S(1)}, f32[32,128]{1,0:T(8,128)S(1)}) custom-call(f32[768,128]{1,0:T(8,128)S(1)} %bitcast.18, f32[768,128]{1,0:T(8,128)S(1)} %collective-permute-done.got, bf16[128,6144]{1,0:T(8,128)(2,1)S(1)} %get-tuple-element.8.modes_panel, f32[128,64]{1,0:T(8,128)S(1)} %get-tuple-element.9.modes_gram), custom_call_target="tpu_custom_call" | custom-call | flops 100000000 | bytes 1000000 | tf_op jit(solution)/shard_map/snaps_gram/pallas_call | solution.py:290
  4.0 0.1 collective-permute-start.1
  4.0 1.1 %collective-permute-done.1 = f32[32,128]{1,0:T(8,128)S(1)} collective-permute-done((f32[32,128]{1,0:T(8,128)S(1)}, f32[32,128]{1,0:T(8,128)S(1)}, u32[]{:S(2)}, u32[]{:S(2)}) %collective-permute-start.1) | collective-permute-done | bytes 16416 | tf_op jit(solution)/shard_map/ppermute | solution.py:30
  5.2 3.5 %collective-permute-start.4 = (f32[32,128]{1,0:T(8,128)S(1)}, f32[32,128]{1,0:T(8,128)S(1)}, u32[]{:S(2)}, u32[]{:S(2)}) collective-permute-start(f32[32,128]{1,0:T(8,128)S(1)} %add.20), channel_id=1, source_target_pairs={{0,7},{1,6},{2,5},{3,4},{4,3},{5,2},{6,1},{7,0},{8,15},{9,14},{10,... | collective-permute-start | bytes 49160 | tf_op jit(solution)/shard_map/ppermute | solution.py:30
  8.7 0.3 %collective-permute-start.3 = (f32[32,128]{1,0:T(8,128)S(1)}, f32[32,128]{1,0:T(8,128)S(1)}, u32[]{:S(2)}, u32[]{:S(2)}) collective-permute-start(f32[32,128]{1,0:T(8,128)S(1)} %add.20), channel_id=1, source_target_pairs={{0,5},{1,4},{2,7},{3,6},{4,1},{5,0},{6,3},{7,2},{8,13},{9,12},{10,... | collective-permute-start | bytes 49160 | tf_op jit(solution)/shard_map/ppermute | solution.py:30
  9.0 0.1 collective-permute-start.2
  9.1 1.1 %collective-permute-done.4 = f32[32,128]{1,0:T(8,128)S(1)} collective-permute-done((f32[32,128]{1,0:T(8,128)S(1)}, f32[32,128]{1,0:T(8,128)S(1)}, u32[]{:S(2)}, u32[]{:S(2)}) %collective-permute-start.4) | collective-permute-done | bytes 16416 | tf_op jit(solution)/shard_map/ppermute | solution.py:30
  10.2 1.7 %collective-permute-done.3 = f32[32,128]{1,0:T(8,128)S(1)} collective-permute-done((f32[32,128]{1,0:T(8,128)S(1)}, f32[32,128]{1,0:T(8,128)S(1)}, u32[]{:S(2)}, u32[]{:S(2)}) %collective-permute-start.3) | collective-permute-done | bytes 16416 | tf_op jit(solution)/shard_map/ppermute | solution.py:30
  11.9 0.3 %collective-permute-done.2 = f32[32,128]{1,0:T(8,128)S(1)} collective-permute-done((f32[32,128]{1,0:T(8,128)S(1)}, f32[32,128]{1,0:T(8,128)S(1)}, u32[]{:S(2)}, u32[]{:S(2)}) %collective-permute-start.2) | collective-permute-done | bytes 16416 | tf_op jit(solution)/shard_map/ppermute | solution.py:30
  12.2 1.5 %collective-permute-start.5 = (f32[32,128]{1,0:T(8,128)S(1)}, f32[32,128]{1,0:T(8,128)S(1)}, u32[]{:S(2)}, u32[]{:S(2)}) collective-permute-start(f32[32,128]{1,0:T(8,128)S(1)} %add_add_fusion), channel_id=1, source_target_pairs={{0,9},{1,8},{2,11},{3,10},{4,13},{5,12},{6,15},{7,14},{8,1},{9,0},... | collective-permute-start | bytes 49160 | tf_op jit(solution)/shard_map/ppermute | solution.py:30
  13.7 1.6 %collective-permute-done.5 = f32[32,128]{1,0:T(8,128)S(1)} collective-permute-done((f32[32,128]{1,0:T(8,128)S(1)}, f32[32,128]{1,0:T(8,128)S(1)}, u32[]{:S(2)}, u32[]{:S(2)}) %collective-permute-start.5) | collective-permute-done | bytes 16416 | tf_op jit(solution)/shard_map/ppermute | solution.py:30
  15.3 2.5 %collective-permute-start.6 = (f32[32,128]{1,0:T(8,128)S(1)}, f32[32,128]{1,0:T(8,128)S(1)}, u32[]{:S(2)}, u32[]{:S(2)}) collective-permute-start(f32[32,128]{1,0:T(8,128)S(1)} %add.24), channel_id=1, source_target_pairs={{0,17},{1,16},{2,19},{3,18},{4,21},{5,20},{6,23},{7,22},{8,25},{9,... | collective-permute-start | bytes 49160 | tf_op jit(solution)/shard_map/ppermute | solution.py:30
  17.9 0.0 copy-done.1
  17.9 0.1 copy.6.scale
  18.0 1.4 %collective-permute-done.6 = f32[32,128]{1,0:T(8,128)S(1)} collective-permute-done((f32[32,128]{1,0:T(8,128)S(1)}, f32[32,128]{1,0:T(8,128)S(1)}, u32[]{:S(2)}, u32[]{:S(2)}) %collective-permute-start.6) | collective-permute-done | bytes 16416 | tf_op jit(solution)/shard_map/ppermute | solution.py:30
  19.4 3.2 %factor_apply.1 = (f32[80,48,128]{2,1,0:T(8,128)}, f32[80,80]{1,0:T(8,128)}) custom-call(f32[32,128]{1,0:T(8,128)S(1)} %add.25.packed, f32[80,1]{1,0:T(8,128)S(1)} %copy.6.scale, bf16[128,6144]{1,0:T(8,128)(2,1)S(1)} %get-tuple-element.8.modes_panel, bf16[32,6144]{1,0:T(8,128)(2,1)S(1)} %get-tuple-element.11.snaps_panel), custom_call_target="tpu_custom_call" | custom-call | tf_op jit(solution)/shard_map/factor_apply/pallas_call | solution.py:304
  (5 shorter events, 0.0 us)
Async XLA Ops:
  0.6 2.7 %copy-start = (f32[16,4,1536]{2,1,0:T(4,128)S(1)}, f32[16,4,1536]{2,1,0:T(4,128)}, u32[]{:S(2)}) copy-start(f32[16,4,1536]{2,1,0:T(4,128)} %param.5) | copy-start | bytes 1179652
  0.6 2.7 %collective-permute-start = (f32[768,128]{1,0:T(8,128)}, f32[768,128]{1,0:T(8,128)S(1)}, u32[]{:S(2)}, u32[]{:S(2)}) collective-permute-start(f32[768,128]{1,0:T(8,128)} %bitcast.17), channel_id=1, source_target_pairs={{0,1},{1,0},{2,3},{3,2},{4,5},{5,4},{6,7},{7,6},{8,9},{9,8},{10,11... | collective-permute-start | bytes 1179656 | tf_op jit(solution)/shard_map/ppermute | solution.py:274
  3.3 14.6 %copy-start.1 = (f32[64]{0:T(128)S(1)}, f32[64]{0:T(128)}, u32[]{:S(2)}) copy-start(f32[64]{0:T(128)} %param.4) | copy-start | bytes 772
  4.0 1.2 %collective-permute-start.1 = (f32[32,128]{1,0:T(8,128)S(1)}, f32[32,128]{1,0:T(8,128)S(1)}, u32[]{:S(2)}, u32[]{:S(2)}) collective-permute-start(f32[32,128]{1,0:T(8,128)S(1)} %get-tuple-element.10), channel_id=1, source_target_pairs={{0,1},{1,0},{2,3},{3,2},{4,5},{5,4},{6,7},{7,6},{8,9},{9,8},{10,11... | collective-permute-start | bytes 49160 | tf_op jit(solution)/shard_map/ppermute | solution.py:30
  5.2 5.0 %collective-permute-start.4 = (f32[32,128]{1,0:T(8,128)S(1)}, f32[32,128]{1,0:T(8,128)S(1)}, u32[]{:S(2)}, u32[]{:S(2)}) collective-permute-start(f32[32,128]{1,0:T(8,128)S(1)} %add.20), channel_id=1, source_target_pairs={{0,7},{1,6},{2,5},{3,4},{4,3},{5,2},{6,1},{7,0},{8,15},{9,14},{10,... | collective-permute-start | bytes 49160 | tf_op jit(solution)/shard_map/ppermute | solution.py:30
  8.7 3.2 %collective-permute-start.3 = (f32[32,128]{1,0:T(8,128)S(1)}, f32[32,128]{1,0:T(8,128)S(1)}, u32[]{:S(2)}, u32[]{:S(2)}) collective-permute-start(f32[32,128]{1,0:T(8,128)S(1)} %add.20), channel_id=1, source_target_pairs={{0,5},{1,4},{2,7},{3,6},{4,1},{5,0},{6,3},{7,2},{8,13},{9,12},{10,... | collective-permute-start | bytes 49160 | tf_op jit(solution)/shard_map/ppermute | solution.py:30
  9.0 3.2 %collective-permute-start.2 = (f32[32,128]{1,0:T(8,128)S(1)}, f32[32,128]{1,0:T(8,128)S(1)}, u32[]{:S(2)}, u32[]{:S(2)}) collective-permute-start(f32[32,128]{1,0:T(8,128)S(1)} %add.20), channel_id=1, source_target_pairs={{0,3},{1,2},{2,1},{3,0},{4,7},{5,6},{6,5},{7,4},{8,11},{9,10},{10,... | collective-permute-start | bytes 49160 | tf_op jit(solution)/shard_map/ppermute | solution.py:30
  12.2 3.2 %collective-permute-start.5 = (f32[32,128]{1,0:T(8,128)S(1)}, f32[32,128]{1,0:T(8,128)S(1)}, u32[]{:S(2)}, u32[]{:S(2)}) collective-permute-start(f32[32,128]{1,0:T(8,128)S(1)} %add_add_fusion), channel_id=1, source_target_pairs={{0,9},{1,8},{2,11},{3,10},{4,13},{5,12},{6,15},{7,14},{8,1},{9,0},... | collective-permute-start | bytes 49160 | tf_op jit(solution)/shard_map/ppermute | solution.py:30
  15.3 4.1 %collective-permute-start.6 = (f32[32,128]{1,0:T(8,128)S(1)}, f32[32,128]{1,0:T(8,128)S(1)}, u32[]{:S(2)}, u32[]{:S(2)}) collective-permute-start(f32[32,128]{1,0:T(8,128)S(1)} %add.24), channel_id=1, source_target_pairs={{0,17},{1,16},{2,19},{3,18},{4,21},{5,20},{6,23},{7,22},{8,25},{9,... | collective-permute-start | bytes 49160 | tf_op jit(solution)/shard_map/ppermute | solution.py:30

commit v10 on v9

--- a/solution.py
+++ b/solution.py
@@ -11,7 +11,7 @@
 LANES = 128
 TILE = 8
 BLOCK = 16
-PIECES = 2
+COST = 10**9
 F32, BF16 = jnp.float32, jnp.bfloat16
 VMEM = pl.BlockSpec(memory_space=pltpu.VMEM)
 ANY = pl.BlockSpec(memory_space=pl.ANY)
@@ -54,26 +54,18 @@
     return lax.dot_general(a, b, (((1,), (1,)), ((), ())), preferred_element_type=F32)
 
 
-def modes_kernel(source, panel, gram, buf, sems):
-    count, slabs, _ = source.shape
-    flat = buf.reshape(count * slabs, LANES)
-    pieces = sems.shape[0]
-    step = slabs // pieces
-    copies = []
-    for p in range(pieces):
-        part = (slice(None), pl.ds(p * step, step))
-        copies.append(pltpu.make_async_copy(source.at[part], buf.at[part], sems.at[p]))
-        copies[-1].start()
-    terms = []
-    for p in range(pieces):
-        copies[p].wait()
-        for i in range(p * step, (p + 1) * step):
-            high, low = split(flat[pl.ds(i, count, stride=slabs), :])
-            panel[:count, i * LANES:(i + 1) * LANES] = high
-            panel[count:, i * LANES:(i + 1) * LANES] = low
-        cols = slice(p * step * LANES, (p + 1) * step * LANES)
-        terms.append(rows_times_rows(panel[:, cols], panel[:count, cols]))
-    gram[...] = total_of(terms)
+def ones_kernel(out):
+    out[...] = jnp.ones(out.shape, F32)
+
+
+def modes_kernel(modes, panel, gram):
+    count = gram.shape[1]
+    slabs = modes.shape[0] // count
+    for i in range(slabs):
+        high, low = split(modes[pl.ds(i, count, stride=slabs), :])
+        panel[:count, i * LANES:(i + 1) * LANES] = high
+        panel[count:, i * LANES:(i + 1) * LANES] = low
+    gram[...] = rows_times_rows(panel[...], panel[:count])
 
 
 def snaps_kernel(rows, keep, got, modes_panel, modes_gram, panel, packed):
@@ -267,10 +259,19 @@
     cores = lax.axis_size("grp")
     cells = rows * cols * lax.axis_size("srv") * cores
     fields = basis_modes.reshape(modes, rows, tiles, LANES).transpose(0, 2, 1, 3)
-    fields = pltpu.with_memory_space_constraint(fields.reshape(modes, slabs, LANES), pltpu.HBM)
+    fields = fields.reshape(modes * slabs, LANES)
     own = snapshots.reshape(snaps, cores * rows, tiles // cores, LANES)
     own = with_layout_constraint(own, Layout((0, 2, 1, 3))).transpose(0, 2, 1, 3)
     own = own.reshape(snaps * tiles * rows, LANES)
+    ones = pl.pallas_call(
+        ones_kernel,
+        out_shape=jax.ShapeDtypeStruct((1, snaps), F32),
+        out_specs=VMEM,
+        compiler_params=PARAMS,
+        cost_estimate=pl.CostEstimate(flops=COST, bytes_accessed=10**6, transcendentals=0),
+        name="ones_row",
+    )()
+    fields, ones = lax.optimization_barrier((fields, ones))
     got = lax.ppermute(own, "grp", [(0, 1), (1, 0)])
 
     chunk = 6
@@ -280,9 +281,8 @@
             jax.ShapeDtypeStruct((2 * modes, slabs * LANES), BF16),
             jax.ShapeDtypeStruct((2 * modes, modes), F32),
         ),
-        in_specs=[HBM],
+        in_specs=[VMEM],
         out_specs=(VMEM, VMEM),
-        scratch_shapes=[pltpu.VMEM(fields.shape, F32), pltpu.SemaphoreType.DMA((PIECES,))],
         cost_estimate=pl.CostEstimate(flops=10**8, bytes_accessed=fields.size * 4, transcendentals=0),
         compiler_params=PARAMS,
         name="modes_gram",
@@ -300,7 +300,7 @@
         name="snaps_gram",
     )(own, got, modes_panel, modes_gram)
     packed = total(packed)
-    scale = jnp.concatenate([weights, jnp.ones((snaps,), F32)])
+    scale = jnp.concatenate([weights, ones[0]])
     new_modes, factor = pl.pallas_call(
         functools.partial(apply_kernel, cells),
         out_shape=(

time: 22.8 us -> 22.9 us (level)
  Pallas kernels: 5.95 us -> 4.92 us
  local copies, waits for them, and re-layouts: 0.12 us -> 0.95 us
  starting transfers between devices: 8.63 us -> 9.02 us
    pallas_call x1, Pallas kernels: 2.08 us -> 1.05 us  [per_device(): pl.pallas_call(modes_kernel, out_shape=(jax.ShapeDtypeStruct((2 * modes,...]
    unnamed x4 -> x6, local copies, waits for them, and re-layouts: 0.01 us -> 0.85 us
    ppermute x6, starting transfers between devices: 8.07 us -> 8.46 us  [total(): lax.ppermute(value, AXES, [(i, i ^ m) for i in range(count)])]
  transfers between devices with their start and end apart: 7 -> 7, of which waited for: 6 -> 6; matrix products, arithmetic and copies ran while one was open for 0% -> 1% of each run, Pallas kernels for 9% -> 5%
where the time goes in v10:
time: 22.9 us; the launch traced here: 22.8 us
  starting transfers between devices  9.02 us (39%)
  waiting for transfers between devices  7.11 us (31%)
  Pallas kernels  4.92 us (21%)
  local copies, waits for them, and re-layouts  0.95 us (4%)
  between operations  0.68 us (3%)
    ppermute x6, starting transfers between devices, total(): lax.ppermute(value, AXES, [(i, i ^ m) for i in range(count)])  8.46 us
    ppermute x6, waiting for transfers between devices, total(): lax.ppermute(value, AXES, [(i, i ^ m) for i in range(count)])  7.11 us
    pallas_call x1, Pallas kernels, per_device(): pl.pallas_call(functools.partial(apply_kernel, cells), out_shape=(jax.Sha...  3.23 us
    pallas_call x1, Pallas kernels, per_device(): pl.pallas_call(modes_kernel, out_shape=(jax.ShapeDtypeStruct((2 * modes,...  1.05 us
    unnamed x6, local copies, waits for them, and re-layouts  0.85 us
    pallas_call x1, Pallas kernels, per_device(): pl.pallas_call(functools.partial(snaps_kernel, rows), out_shape=(jax.Shap...  0.63 us
    ppermute x1, starting transfers between devices, per_device(): got = lax.ppermute(own, 'grp', [(0, 1), (1, 0)])  0.56 us
  transfers between devices with their start and end apart: 7, of which 6 were waited for; matrix products, arithmetic and copies ran while one was open for 1% of the time, Pallas kernels for 5%

profile of v10, /device:TPU:0, one launch (start us, length us, event | category | flops | bytes accessed | tf_op | source)
XLA Modules:
  0.0 22.8 jit_solution(9828974101728725749)
XLA Ops:
  0.6 0.0 copy-start
  0.6 0.6 %collective-permute-start = (f32[768,128]{1,0:T(8,128)}, f32[768,128]{1,0:T(8,128)S(1)}, u32[]{:S(2)}, u32[]{:S(2)}) collective-permute-start(f32[768,128]{1,0:T(8,128)} %bitcast.19), channel_id=1, source_target_pairs={{0,1},{1,0},{2,3},{3,2},{4,5},{5,4},{6,7},{7,6},{8,9},{9,8},{10,11... | collective-permute-start | bytes 1179656 | tf_op jit(solution)/shard_map/ppermute | solution.py:275
  1.2 0.0 copy-start.1
  1.2 0.8 %copy-done = f32[64,2,3072]{2,1,0:T(2,128)S(1)} copy-done((f32[64,2,3072]{2,1,0:T(2,128)S(1)}, f32[64,2,3072]{2,1,0:T(2,128)}, u32[]{:S(2)}) %copy-start) | copy-done | bytes 1572888
  2.0 1.1 %modes_gram.1 = (bf16[128,6144]{1,0:T(8,128)(2,1)S(1)}, f32[128,64]{1,0:T(8,128)S(1)}) custom-call(f32[3072,128]{1,0:T(8,128)S(1)} %bitcast.18), custom_call_target="tpu_custom_call" | custom-call | flops 100000000 | bytes 1572864 | tf_op jit(solution)/shard_map/modes_gram/pallas_call | solution.py:278
  3.1 0.0 copy-start.2
  3.1 0.0 collective-permute-done.got
  3.1 0.0 copy-done.1
  3.1 0.6 %snaps_gram.1 = (bf16[32,6144]{1,0:T(8,128)(2,1)S(1)}, f32[32,128]{1,0:T(8,128)S(1)}) custom-call(f32[768,128]{1,0:T(8,128)S(1)} %bitcast.20, f32[768,128]{1,0:T(8,128)S(1)} %collective-permute-done.got, bf16[128,6144]{1,0:T(8,128)(2,1)S(1)} %get-tuple-element.11.modes_panel, f32[128,64]{1,0:T(8,128)S(1)} %get-tuple-element.12.modes_gram), custom_call_target="tpu_custom_call" | custom-call | flops 100000000 | bytes 1000000 | tf_op jit(solution)/shard_map/snaps_gram/pallas_call | solution.py:290
  3.8 0.5 %collective-permute-start.1 = (f32[32,128]{1,0:T(8,128)S(1)}, f32[32,128]{1,0:T(8,128)S(1)}, u32[]{:S(2)}, u32[]{:S(2)}) collective-permute-start(f32[32,128]{1,0:T(8,128)S(1)} %get-tuple-element.13), channel_id=1, source_target_pairs={{0,1},{1,0},{2,3},{3,2},{4,5},{5,4},{6,7},{7,6},{8,9},{9,8},{10,11... | collective-permute-start | bytes 49160 | tf_op jit(solution)/shard_map/ppermute | solution.py:30
  4.3 0.8 %collective-permute-done.1 = f32[32,128]{1,0:T(8,128)S(1)} collective-permute-done((f32[32,128]{1,0:T(8,128)S(1)}, f32[32,128]{1,0:T(8,128)S(1)}, u32[]{:S(2)}, u32[]{:S(2)}) %collective-permute-start.1) | collective-permute-done | bytes 16416 | tf_op jit(solution)/shard_map/ppermute | solution.py:30
  5.1 3.5 %collective-permute-start.4 = (f32[32,128]{1,0:T(8,128)S(1)}, f32[32,128]{1,0:T(8,128)S(1)}, u32[]{:S(2)}, u32[]{:S(2)}) collective-permute-start(f32[32,128]{1,0:T(8,128)S(1)} %add.18), channel_id=1, source_target_pairs={{0,7},{1,6},{2,5},{3,4},{4,3},{5,2},{6,1},{7,0},{8,15},{9,14},{10,... | collective-permute-start | bytes 49160 | tf_op jit(solution)/shard_map/ppermute | solution.py:30
  8.7 0.5 %collective-permute-start.3 = (f32[32,128]{1,0:T(8,128)S(1)}, f32[32,128]{1,0:T(8,128)S(1)}, u32[]{:S(2)}, u32[]{:S(2)}) collective-permute-start(f32[32,128]{1,0:T(8,128)S(1)} %add.18), channel_id=1, source_target_pairs={{0,5},{1,4},{2,7},{3,6},{4,1},{5,0},{6,3},{7,2},{8,13},{9,12},{10,... | collective-permute-start | bytes 49160 | tf_op jit(solution)/shard_map/ppermute | solution.py:30
  9.1 0.1 collective-permute-start.2
  9.3 0.9 %collective-permute-done.4 = f32[32,128]{1,0:T(8,128)S(1)} collective-permute-done((f32[32,128]{1,0:T(8,128)S(1)}, f32[32,128]{1,0:T(8,128)S(1)}, u32[]{:S(2)}, u32[]{:S(2)}) %collective-permute-start.4) | collective-permute-done | bytes 16416 | tf_op jit(solution)/shard_map/ppermute | solution.py:30
  10.1 1.7 %collective-permute-done.3 = f32[32,128]{1,0:T(8,128)S(1)} collective-permute-done((f32[32,128]{1,0:T(8,128)S(1)}, f32[32,128]{1,0:T(8,128)S(1)}, u32[]{:S(2)}, u32[]{:S(2)}) %collective-permute-start.3) | collective-permute-done | bytes 16416 | tf_op jit(solution)/shard_map/ppermute | solution.py:30
  11.8 0.5 %collective-permute-done.2 = f32[32,128]{1,0:T(8,128)S(1)} collective-permute-done((f32[32,128]{1,0:T(8,128)S(1)}, f32[32,128]{1,0:T(8,128)S(1)}, u32[]{:S(2)}, u32[]{:S(2)}) %collective-permute-start.2) | collective-permute-done | bytes 16416 | tf_op jit(solution)/shard_map/ppermute | solution.py:30
  12.3 1.4 %collective-permute-start.5 = (f32[32,128]{1,0:T(8,128)S(1)}, f32[32,128]{1,0:T(8,128)S(1)}, u32[]{:S(2)}, u32[]{:S(2)}) collective-permute-start(f32[32,128]{1,0:T(8,128)S(1)} %add_add_fusion), channel_id=1, source_target_pairs={{0,9},{1,8},{2,11},{3,10},{4,13},{5,12},{6,15},{7,14},{8,1},{9,0},... | collective-permute-start | bytes 49160 | tf_op jit(solution)/shard_map/ppermute | solution.py:30
  13.7 1.8 %collective-permute-done.5 = f32[32,128]{1,0:T(8,128)S(1)} collective-permute-done((f32[32,128]{1,0:T(8,128)S(1)}, f32[32,128]{1,0:T(8,128)S(1)}, u32[]{:S(2)}, u32[]{:S(2)}) %collective-permute-start.5) | collective-permute-done | bytes 16416 | tf_op jit(solution)/shard_map/ppermute | solution.py:30
  15.5 2.4 %collective-permute-start.6 = (f32[32,128]{1,0:T(8,128)S(1)}, f32[32,128]{1,0:T(8,128)S(1)}, u32[]{:S(2)}, u32[]{:S(2)}) collective-permute-start(f32[32,128]{1,0:T(8,128)S(1)} %add.22), channel_id=1, source_target_pairs={{0,17},{1,16},{2,19},{3,18},{4,21},{5,20},{6,23},{7,22},{8,25},{9,... | collective-permute-start | bytes 49160 | tf_op jit(solution)/shard_map/ppermute | solution.py:30
  17.9 0.0 copy-done.2
  17.9 0.1 maximum_bitcast_fusion
  18.0 0.1 copy.6.scale
  18.1 1.5 %collective-permute-done.6 = f32[32,128]{1,0:T(8,128)S(1)} collective-permute-done((f32[32,128]{1,0:T(8,128)S(1)}, f32[32,128]{1,0:T(8,128)S(1)}, u32[]{:S(2)}, u32[]{:S(2)}) %collective-permute-start.6) | collective-permute-done | bytes 16416 | tf_op jit(solution)/shard_map/ppermute | solution.py:30
  19.5 3.2 %factor_apply.1 = (f32[80,48,128]{2,1,0:T(8,128)}, f32[80,80]{1,0:T(8,128)}) custom-call(f32[32,128]{1,0:T(8,128)S(1)} %add.23.packed, f32[80,1]{1,0:T(8,128)S(1)} %copy.6.scale, bf16[128,6144]{1,0:T(8,128)(2,1)S(1)} %get-tuple-element.11.modes_panel, bf16[32,6144]{1,0:T(8,128)(2,1)S(1)} %get-tuple-element.15.snaps_panel), custom_call_target="tpu_custom_call" | custom-call | tf_op jit(solution)/shard_map/factor_apply/pallas_call | solution.py:304
  (5 shorter events, 0.0 us)
Async XLA Ops:
  0.6 1.4 %copy-start = (f32[64,2,3072]{2,1,0:T(2,128)S(1)}, f32[64,2,3072]{2,1,0:T(2,128)}, u32[]{:S(2)}) copy-start(f32[64,2,3072]{2,1,0:T(2,128)} %param.3) | copy-start | bytes 4718596
  0.6 2.5 %collective-permute-start = (f32[768,128]{1,0:T(8,128)}, f32[768,128]{1,0:T(8,128)S(1)}, u32[]{:S(2)}, u32[]{:S(2)}) collective-permute-start(f32[768,128]{1,0:T(8,128)} %bitcast.19), channel_id=1, source_target_pairs={{0,1},{1,0},{2,3},{3,2},{4,5},{5,4},{6,7},{7,6},{8,9},{9,8},{10,11... | collective-permute-start | bytes 1179656 | tf_op jit(solution)/shard_map/ppermute | solution.py:275
  1.2 1.9 %copy-start.1 = (f32[16,4,1536]{2,1,0:T(4,128)S(1)}, f32[16,4,1536]{2,1,0:T(4,128)}, u32[]{:S(2)}) copy-start(f32[16,4,1536]{2,1,0:T(4,128)} %param.5) | copy-start | bytes 1179652
  3.1 14.8 %copy-start.2 = (f32[64]{0:T(128)S(1)}, f32[64]{0:T(128)}, u32[]{:S(2)}) copy-start(f32[64]{0:T(128)} %param.4) | copy-start | bytes 772
  3.8 1.4 %collective-permute-start.1 = (f32[32,128]{1,0:T(8,128)S(1)}, f32[32,128]{1,0:T(8,128)S(1)}, u32[]{:S(2)}, u32[]{:S(2)}) collective-permute-start(f32[32,128]{1,0:T(8,128)S(1)} %get-tuple-element.13), channel_id=1, source_target_pairs={{0,1},{1,0},{2,3},{3,2},{4,5},{5,4},{6,7},{7,6},{8,9},{9,8},{10,11... | collective-permute-start | bytes 49160 | tf_op jit(solution)/shard_map/ppermute | solution.py:30
  5.1 5.0 %collective-permute-start.4 = (f32[32,128]{1,0:T(8,128)S(1)}, f32[32,128]{1,0:T(8,128)S(1)}, u32[]{:S(2)}, u32[]{:S(2)}) collective-permute-start(f32[32,128]{1,0:T(8,128)S(1)} %add.18), channel_id=1, source_target_pairs={{0,7},{1,6},{2,5},{3,4},{4,3},{5,2},{6,1},{7,0},{8,15},{9,14},{10,... | collective-permute-start | bytes 49160 | tf_op jit(solution)/shard_map/ppermute | solution.py:30
  8.7 3.2 %collective-permute-start.3 = (f32[32,128]{1,0:T(8,128)S(1)}, f32[32,128]{1,0:T(8,128)S(1)}, u32[]{:S(2)}, u32[]{:S(2)}) collective-permute-start(f32[32,128]{1,0:T(8,128)S(1)} %add.18), channel_id=1, source_target_pairs={{0,5},{1,4},{2,7},{3,6},{4,1},{5,0},{6,3},{7,2},{8,13},{9,12},{10,... | collective-permute-start | bytes 49160 | tf_op jit(solution)/shard_map/ppermute | solution.py:30
  9.1 3.2 %collective-permute-start.2 = (f32[32,128]{1,0:T(8,128)S(1)}, f32[32,128]{1,0:T(8,128)S(1)}, u32[]{:S(2)}, u32[]{:S(2)}) collective-permute-start(f32[32,128]{1,0:T(8,128)S(1)} %add.18), channel_id=1, source_target_pairs={{0,3},{1,2},{2,1},{3,0},{4,7},{5,6},{6,5},{7,4},{8,11},{9,10},{10,... | collective-permute-start | bytes 49160 | tf_op jit(solution)/shard_map/ppermute | solution.py:30
  12.3 3.2 %collective-permute-start.5 = (f32[32,128]{1,0:T(8,128)S(1)}, f32[32,128]{1,0:T(8,128)S(1)}, u32[]{:S(2)}, u32[]{:S(2)}) collective-permute-start(f32[32,128]{1,0:T(8,128)S(1)} %add_add_fusion), channel_id=1, source_target_pairs={{0,9},{1,8},{2,11},{3,10},{4,13},{5,12},{6,15},{7,14},{8,1},{9,0},... | collective-permute-start | bytes 49160 | tf_op jit(solution)/shard_map/ppermute | solution.py:30
  15.5 4.1 %collective-permute-start.6 = (f32[32,128]{1,0:T(8,128)S(1)}, f32[32,128]{1,0:T(8,128)S(1)}, u32[]{:S(2)}, u32[]{:S(2)}) collective-permute-start(f32[32,128]{1,0:T(8,128)S(1)} %add.22), channel_id=1, source_target_pairs={{0,17},{1,16},{2,19},{3,18},{4,21},{5,20},{6,23},{7,22},{8,25},{9,... | collective-permute-start | bytes 49160 | tf_op jit(solution)/shard_map/ppermute | solution.py:30

commit v11 on v9

--- a/solution.py
+++ b/solution.py
@@ -25,7 +25,7 @@
         return lax.psum(value, AXES)
     count = servers * cores
     masks = [2 << p | 1 for p in range(servers.bit_length() - 1)]
-    rounds = [[1], [masks[0], masks[1], masks[0] | masks[1]]] + [[mask] for mask in masks[2:]]
+    rounds = [[1]] + [[mask] for mask in masks[3:]] + [[masks[0], masks[1], masks[0] | masks[1]]] + [[mask] for mask in masks[2:3]]
     for masks in rounds:
         parts = [lax.ppermute(value, AXES, [(i, i ^ m) for i in range(count)]) for m in masks]
         for part in parts:
@@ -244,11 +244,18 @@
     slabs = buf.shape[1]
     flat = buf.reshape(width * slabs, LANES)
     step = slabs // chunks
-    for k in range(chunks):
+
+    def product(k):
         cols = slice(k * step * LANES, (k + 1) * step * LANES)
         right = jnp.concatenate([modes_panel[:, cols], snaps_panel[:, cols]], axis=0)
         res = jnp.dot(both_w, right, preferred_element_type=F32)
-        res = res[:width] + res[width:]
+        return res[:width] + res[width:]
+
+    following = product(0)
+    for k in range(chunks):
+        res = following
+        if k + 1 < chunks:
+            following = product(k + 1)
         for i in range(step):
             flat[pl.ds(k * step + i, width, stride=slabs), :] = res[:, i * LANES:(i + 1) * LANES]
         part = (slice(None), pl.ds(k * step, step))
@@ -273,7 +280,7 @@
     own = own.reshape(snaps * tiles * rows, LANES)
     got = lax.ppermute(own, "grp", [(0, 1), (1, 0)])
 
-    chunk = 6
+    chunk = 12
     modes_panel, modes_gram = pl.pallas_call(
         modes_kernel,
         out_shape=(

time: 22.8 us -> 22.8 us (level)
  no operation moved by 1% of the time
where the time goes in v11:
time: 22.8 us; the launch traced here: 22.6 us
  starting transfers between devices  8.81 us (39%)
  waiting for transfers between devices  7.06 us (31%)
  Pallas kernels  5.94 us (26%)
  between operations  0.68 us (3%)
    ppermute x6, starting transfers between devices, total(): lax.ppermute(value, AXES, [(i, i ^ m) for i in range(count)])  8.26 us
    ppermute x6, waiting for transfers between devices, total(): lax.ppermute(value, AXES, [(i, i ^ m) for i in range(count)])  7.06 us
    pallas_call x1, Pallas kernels, per_device(): pl.pallas_call(functools.partial(apply_kernel, cells), out_shape=(jax.Sha...  3.23 us
    pallas_call x1, Pallas kernels, per_device(): pl.pallas_call(modes_kernel, out_shape=(jax.ShapeDtypeStruct((2 * modes,...  2.08 us
    pallas_call x1, Pallas kernels, per_device(): pl.pallas_call(functools.partial(snaps_kernel, rows), out_shape=(jax.Shap...  0.63 us
    ppermute x1, starting transfers between devices, per_device(): got = lax.ppermute(own, 'grp', [(0, 1), (1, 0)])  0.56 us
  transfers between devices with their start and end apart: 7, of which 6 were waited for; matrix products, arithmetic and copies ran while one was open for 0% of the time, Pallas kernels for 9%

profile of v11, /device:TPU:0, one launch (start us, length us, event | category | flops | bytes accessed | tf_op | source)
XLA Modules:
  0.0 22.6 jit_solution(1762642484912473933)
XLA Ops:
  0.6 0.0 copy-start
  0.6 0.6 %collective-permute-start = (f32[768,128]{1,0:T(8,128)}, f32[768,128]{1,0:T(8,128)S(1)}, u32[]{:S(2)}, u32[]{:S(2)}) collective-permute-start(f32[768,128]{1,0:T(8,128)} %bitcast.17), channel_id=1, source_target_pairs={{0,1},{1,0},{2,3},{3,2},{4,5},{5,4},{6,7},{7,6},{8,9},{9,8},{10,11... | collective-permute-start | bytes 1179656 | tf_op jit(solution)/shard_map/ppermute | solution.py:281
  1.2 2.1 %modes_gram.1 = (bf16[128,6144]{1,0:T(8,128)(2,1)S(1)}, f32[128,64]{1,0:T(8,128)S(1)}) custom-call(f32[64,48,128]{2,1,0:T(8,128)} %bitcast.19), custom_call_target="tpu_custom_call" | custom-call | flops 100000000 | bytes 1572864 | tf_op jit(solution)/shard_map/modes_gram/pallas_call | solution.py:284
  3.3 0.0 copy-start.1
  3.3 0.0 collective-permute-done.got
  3.3 0.0 copy-done
  3.3 0.6 %snaps_gram.1 = (bf16[32,6144]{1,0:T(8,128)(2,1)S(1)}, f32[32,128]{1,0:T(8,128)S(1)}) custom-call(f32[768,128]{1,0:T(8,128)S(1)} %bitcast.18, f32[768,128]{1,0:T(8,128)S(1)} %collective-permute-done.got, bf16[128,6144]{1,0:T(8,128)(2,1)S(1)} %get-tuple-element.8.modes_panel, f32[128,64]{1,0:T(8,128)S(1)} %get-tuple-element.9.modes_gram), custom_call_target="tpu_custom_call" | custom-call | flops 100000000 | bytes 1000000 | tf_op jit(solution)/shard_map/snaps_gram/pallas_call | solution.py:297
  4.0 0.1 collective-permute-start.1
  4.0 1.1 %collective-permute-done.1 = f32[32,128]{1,0:T(8,128)S(1)} collective-permute-done((f32[32,128]{1,0:T(8,128)S(1)}, f32[32,128]{1,0:T(8,128)S(1)}, u32[]{:S(2)}, u32[]{:S(2)}) %collective-permute-start.1) | collective-permute-done | bytes 16416 | tf_op jit(solution)/shard_map/ppermute | solution.py:30
  5.2 3.7 %collective-permute-start.2 = (f32[32,128]{1,0:T(8,128)S(1)}, f32[32,128]{1,0:T(8,128)S(1)}, u32[]{:S(2)}, u32[]{:S(2)}) collective-permute-start(f32[32,128]{1,0:T(8,128)S(1)} %add.20), channel_id=1, source_target_pairs={{0,17},{1,16},{2,19},{3,18},{4,21},{5,20},{6,23},{7,22},{8,25},{9,... | collective-permute-start | bytes 49160 | tf_op jit(solution)/shard_map/ppermute | solution.py:30
  8.9 1.4 %collective-permute-done.2 = f32[32,128]{1,0:T(8,128)S(1)} collective-permute-done((f32[32,128]{1,0:T(8,128)S(1)}, f32[32,128]{1,0:T(8,128)S(1)}, u32[]{:S(2)}, u32[]{:S(2)}) %collective-permute-start.2) | collective-permute-done | bytes 16416 | tf_op jit(solution)/shard_map/ppermute | solution.py:30
  10.3 2.5 %collective-permute-start.5 = (f32[32,128]{1,0:T(8,128)S(1)}, f32[32,128]{1,0:T(8,128)S(1)}, u32[]{:S(2)}, u32[]{:S(2)}) collective-permute-start(f32[32,128]{1,0:T(8,128)S(1)} %add.21), channel_id=1, source_target_pairs={{0,7},{1,6},{2,5},{3,4},{4,3},{5,2},{6,1},{7,0},{8,15},{9,14},{10,... | collective-permute-start | bytes 49160 | tf_op jit(solution)/shard_map/ppermute | solution.py:30
  12.8 0.3 %collective-permute-start.4 = (f32[32,128]{1,0:T(8,128)S(1)}, f32[32,128]{1,0:T(8,128)S(1)}, u32[]{:S(2)}, u32[]{:S(2)}) collective-permute-start(f32[32,128]{1,0:T(8,128)S(1)} %add.21), channel_id=1, source_target_pairs={{0,5},{1,4},{2,7},{3,6},{4,1},{5,0},{6,3},{7,2},{8,13},{9,12},{10,... | collective-permute-start | bytes 49160 | tf_op jit(solution)/shard_map/ppermute | solution.py:30
  13.1 0.2 collective-permute-start.3
  13.3 1.1 %collective-permute-done.5 = f32[32,128]{1,0:T(8,128)S(1)} collective-permute-done((f32[32,128]{1,0:T(8,128)S(1)}, f32[32,128]{1,0:T(8,128)S(1)}, u32[]{:S(2)}, u32[]{:S(2)}) %collective-permute-start.5) | collective-permute-done | bytes 16416 | tf_op jit(solution)/shard_map/ppermute | solution.py:30
  14.4 1.6 %collective-permute-done.4 = f32[32,128]{1,0:T(8,128)S(1)} collective-permute-done((f32[32,128]{1,0:T(8,128)S(1)}, f32[32,128]{1,0:T(8,128)S(1)}, u32[]{:S(2)}, u32[]{:S(2)}) %collective-permute-start.4) | collective-permute-done | bytes 16416 | tf_op jit(solution)/shard_map/ppermute | solution.py:30
  16.0 0.3 %collective-permute-done.3 = f32[32,128]{1,0:T(8,128)S(1)} collective-permute-done((f32[32,128]{1,0:T(8,128)S(1)}, f32[32,128]{1,0:T(8,128)S(1)}, u32[]{:S(2)}, u32[]{:S(2)}) %collective-permute-start.3) | collective-permute-done | bytes 16416 | tf_op jit(solution)/shard_map/ppermute | solution.py:30
  16.2 1.5 %collective-permute-start.6 = (f32[32,128]{1,0:T(8,128)S(1)}, f32[32,128]{1,0:T(8,128)S(1)}, u32[]{:S(2)}, u32[]{:S(2)}) collective-permute-start(f32[32,128]{1,0:T(8,128)S(1)} %add_add_fusion), channel_id=1, source_target_pairs={{0,9},{1,8},{2,11},{3,10},{4,13},{5,12},{6,15},{7,14},{8,1},{9,0},... | collective-permute-start | bytes 49160 | tf_op jit(solution)/shard_map/ppermute | solution.py:30
  17.8 0.0 copy-done.1
  17.8 0.1 copy.6.scale
  17.9 1.5 %collective-permute-done.6 = f32[32,128]{1,0:T(8,128)S(1)} collective-permute-done((f32[32,128]{1,0:T(8,128)S(1)}, f32[32,128]{1,0:T(8,128)S(1)}, u32[]{:S(2)}, u32[]{:S(2)}) %collective-permute-start.6) | collective-permute-done | bytes 16416 | tf_op jit(solution)/shard_map/ppermute | solution.py:30
  19.4 3.2 %factor_apply.1 = (f32[80,48,128]{2,1,0:T(8,128)}, f32[80,80]{1,0:T(8,128)}) custom-call(f32[32,128]{1,0:T(8,128)S(1)} %add.25.packed, f32[80,1]{1,0:T(8,128)S(1)} %copy.6.scale, bf16[128,6144]{1,0:T(8,128)(2,1)S(1)} %get-tuple-element.8.modes_panel, bf16[32,6144]{1,0:T(8,128)(2,1)S(1)} %get-tuple-element.11.snaps_panel), custom_call_target="tpu_custom_call" | custom-call | tf_op jit(solution)/shard_map/factor_apply/pallas_call | solution.py:311
  (5 shorter events, 0.0 us)
Async XLA Ops:
  0.6 2.7 %copy-start = (f32[16,4,1536]{2,1,0:T(4,128)S(1)}, f32[16,4,1536]{2,1,0:T(4,128)}, u32[]{:S(2)}) copy-start(f32[16,4,1536]{2,1,0:T(4,128)} %param.5) | copy-start | bytes 1179652
  0.6 2.7 %collective-permute-start = (f32[768,128]{1,0:T(8,128)}, f32[768,128]{1,0:T(8,128)S(1)}, u32[]{:S(2)}, u32[]{:S(2)}) collective-permute-start(f32[768,128]{1,0:T(8,128)} %bitcast.17), channel_id=1, source_target_pairs={{0,1},{1,0},{2,3},{3,2},{4,5},{5,4},{6,7},{7,6},{8,9},{9,8},{10,11... | collective-permute-start | bytes 1179656 | tf_op jit(solution)/shard_map/ppermute | solution.py:281
  3.3 14.5 %copy-start.1 = (f32[64]{0:T(128)S(1)}, f32[64]{0:T(128)}, u32[]{:S(2)}) copy-start(f32[64]{0:T(128)} %param.4) | copy-start | bytes 772
  4.0 1.2 %collective-permute-start.1 = (f32[32,128]{1,0:T(8,128)S(1)}, f32[32,128]{1,0:T(8,128)S(1)}, u32[]{:S(2)}, u32[]{:S(2)}) collective-permute-start(f32[32,128]{1,0:T(8,128)S(1)} %get-tuple-element.10), channel_id=1, source_target_pairs={{0,1},{1,0},{2,3},{3,2},{4,5},{5,4},{6,7},{7,6},{8,9},{9,8},{10,11... | collective-permute-start | bytes 49160 | tf_op jit(solution)/shard_map/ppermute | solution.py:30
  5.2 5.1 %collective-permute-start.2 = (f32[32,128]{1,0:T(8,128)S(1)}, f32[32,128]{1,0:T(8,128)S(1)}, u32[]{:S(2)}, u32[]{:S(2)}) collective-permute-start(f32[32,128]{1,0:T(8,128)S(1)} %add.20), channel_id=1, source_target_pairs={{0,17},{1,16},{2,19},{3,18},{4,21},{5,20},{6,23},{7,22},{8,25},{9,... | collective-permute-start | bytes 49160 | tf_op jit(solution)/shard_map/ppermute | solution.py:30
  10.3 4.1 %collective-permute-start.5 = (f32[32,128]{1,0:T(8,128)S(1)}, f32[32,128]{1,0:T(8,128)S(1)}, u32[]{:S(2)}, u32[]{:S(2)}) collective-permute-start(f32[32,128]{1,0:T(8,128)S(1)} %add.21), channel_id=1, source_target_pairs={{0,7},{1,6},{2,5},{3,4},{4,3},{5,2},{6,1},{7,0},{8,15},{9,14},{10,... | collective-permute-start | bytes 49160 | tf_op jit(solution)/shard_map/ppermute | solution.py:30
  12.8 3.2 %collective-permute-start.4 = (f32[32,128]{1,0:T(8,128)S(1)}, f32[32,128]{1,0:T(8,128)S(1)}, u32[]{:S(2)}, u32[]{:S(2)}) collective-permute-start(f32[32,128]{1,0:T(8,128)S(1)} %add.21), channel_id=1, source_target_pairs={{0,5},{1,4},{2,7},{3,6},{4,1},{5,0},{6,3},{7,2},{8,13},{9,12},{10,... | collective-permute-start | bytes 49160 | tf_op jit(solution)/shard_map/ppermute | solution.py:30
  13.1 3.2 %collective-permute-start.3 = (f32[32,128]{1,0:T(8,128)S(1)}, f32[32,128]{1,0:T(8,128)S(1)}, u32[]{:S(2)}, u32[]{:S(2)}) collective-permute-start(f32[32,128]{1,0:T(8,128)S(1)} %add.21), channel_id=1, source_target_pairs={{0,3},{1,2},{2,1},{3,0},{4,7},{5,6},{6,5},{7,4},{8,11},{9,10},{10,... | collective-permute-start | bytes 49160 | tf_op jit(solution)/shard_map/ppermute | solution.py:30
  16.2 3.2 %collective-permute-start.6 = (f32[32,128]{1,0:T(8,128)S(1)}, f32[32,128]{1,0:T(8,128)S(1)}, u32[]{:S(2)}, u32[]{:S(2)}) collective-permute-start(f32[32,128]{1,0:T(8,128)S(1)} %add_add_fusion), channel_id=1, source_target_pairs={{0,9},{1,8},{2,11},{3,10},{4,13},{5,12},{6,15},{7,14},{8,1},{9,0},... | collective-permute-start | bytes 49160 | tf_op jit(solution)/shard_map/ppermute | solution.py:30

commit v12 on v11

--- a/solution.py
+++ b/solution.py
@@ -280,7 +280,7 @@
     own = own.reshape(snaps * tiles * rows, LANES)
     got = lax.ppermute(own, "grp", [(0, 1), (1, 0)])
 
-    chunk = 12
+    chunk = 6
     modes_panel, modes_gram = pl.pallas_call(
         modes_kernel,
         out_shape=(

time: 22.8 us -> 22.8 us (level)
  no operation moved by 1% of the time
where the time goes in v12:
time: 22.8 us; the launch traced here: 22.6 us
  starting transfers between devices  8.81 us (39%)
  waiting for transfers between devices  7.06 us (31%)
  Pallas kernels  5.95 us (26%)
  between operations  0.68 us (3%)
    ppermute x6, starting transfers between devices, total(): lax.ppermute(value, AXES, [(i, i ^ m) for i in range(count)])  8.26 us
    ppermute x6, waiting for transfers between devices, total(): lax.ppermute(value, AXES, [(i, i ^ m) for i in range(count)])  7.06 us
    pallas_call x1, Pallas kernels, per_device(): pl.pallas_call(functools.partial(apply_kernel, cells), out_shape=(jax.Sha...  3.23 us
    pallas_call x1, Pallas kernels, per_device(): pl.pallas_call(modes_kernel, out_shape=(jax.ShapeDtypeStruct((2 * modes,...  2.08 us
    pallas_call x1, Pallas kernels, per_device(): pl.pallas_call(functools.partial(snaps_kernel, rows), out_shape=(jax.Shap...  0.63 us
    ppermute x1, starting transfers between devices, per_device(): got = lax.ppermute(own, 'grp', [(0, 1), (1, 0)])  0.56 us
  transfers between devices with their start and end apart: 7, of which 6 were waited for; matrix products, arithmetic and copies ran while one was open for 0% of the time, Pallas kernels for 9%

profile of v12, /device:TPU:0, one launch (start us, length us, event | category | flops | bytes accessed | tf_op | source)
XLA Modules:
  0.0 22.6 jit_solution(591145269150950458)
XLA Ops:
  0.6 0.0 copy-start
  0.6 0.6 %collective-permute-start = (f32[768,128]{1,0:T(8,128)}, f32[768,128]{1,0:T(8,128)S(1)}, u32[]{:S(2)}, u32[]{:S(2)}) collective-permute-start(f32[768,128]{1,0:T(8,128)} %bitcast.17), channel_id=1, source_target_pairs={{0,1},{1,0},{2,3},{3,2},{4,5},{5,4},{6,7},{7,6},{8,9},{9,8},{10,11... | collective-permute-start | bytes 1179656 | tf_op jit(solution)/shard_map/ppermute | solution.py:281
  1.2 2.1 %modes_gram.1 = (bf16[128,6144]{1,0:T(8,128)(2,1)S(1)}, f32[128,64]{1,0:T(8,128)S(1)}) custom-call(f32[64,48,128]{2,1,0:T(8,128)} %bitcast.19), custom_call_target="tpu_custom_call" | custom-call | flops 100000000 | bytes 1572864 | tf_op jit(solution)/shard_map/modes_gram/pallas_call | solution.py:284
  3.3 0.0 copy-start.1
  3.3 0.0 collective-permute-done.got
  3.3 0.0 copy-done
  3.3 0.6 %snaps_gram.1 = (bf16[32,6144]{1,0:T(8,128)(2,1)S(1)}, f32[32,128]{1,0:T(8,128)S(1)}) custom-call(f32[768,128]{1,0:T(8,128)S(1)} %bitcast.18, f32[768,128]{1,0:T(8,128)S(1)} %collective-permute-done.got, bf16[128,6144]{1,0:T(8,128)(2,1)S(1)} %get-tuple-element.8.modes_panel, f32[128,64]{1,0:T(8,128)S(1)} %get-tuple-element.9.modes_gram), custom_call_target="tpu_custom_call" | custom-call | flops 100000000 | bytes 1000000 | tf_op jit(solution)/shard_map/snaps_gram/pallas_call | solution.py:297
  4.0 0.1 collective-permute-start.1
  4.0 1.1 %collective-permute-done.1 = f32[32,128]{1,0:T(8,128)S(1)} collective-permute-done((f32[32,128]{1,0:T(8,128)S(1)}, f32[32,128]{1,0:T(8,128)S(1)}, u32[]{:S(2)}, u32[]{:S(2)}) %collective-permute-start.1) | collective-permute-done | bytes 16416 | tf_op jit(solution)/shard_map/ppermute | solution.py:30
  5.2 3.7 %collective-permute-start.2 = (f32[32,128]{1,0:T(8,128)S(1)}, f32[32,128]{1,0:T(8,128)S(1)}, u32[]{:S(2)}, u32[]{:S(2)}) collective-permute-start(f32[32,128]{1,0:T(8,128)S(1)} %add.20), channel_id=1, source_target_pairs={{0,17},{1,16},{2,19},{3,18},{4,21},{5,20},{6,23},{7,22},{8,25},{9,... | collective-permute-start | bytes 49160 | tf_op jit(solution)/shard_map/ppermute | solution.py:30
  8.9 1.4 %collective-permute-done.2 = f32[32,128]{1,0:T(8,128)S(1)} collective-permute-done((f32[32,128]{1,0:T(8,128)S(1)}, f32[32,128]{1,0:T(8,128)S(1)}, u32[]{:S(2)}, u32[]{:S(2)}) %collective-permute-start.2) | collective-permute-done | bytes 16416 | tf_op jit(solution)/shard_map/ppermute | solution.py:30
  10.3 2.5 %collective-permute-start.5 = (f32[32,128]{1,0:T(8,128)S(1)}, f32[32,128]{1,0:T(8,128)S(1)}, u32[]{:S(2)}, u32[]{:S(2)}) collective-permute-start(f32[32,128]{1,0:T(8,128)S(1)} %add.21), channel_id=1, source_target_pairs={{0,7},{1,6},{2,5},{3,4},{4,3},{5,2},{6,1},{7,0},{8,15},{9,14},{10,... | collective-permute-start | bytes 49160 | tf_op jit(solution)/shard_map/ppermute | solution.py:30
  12.8 0.3 %collective-permute-start.4 = (f32[32,128]{1,0:T(8,128)S(1)}, f32[32,128]{1,0:T(8,128)S(1)}, u32[]{:S(2)}, u32[]{:S(2)}) collective-permute-start(f32[32,128]{1,0:T(8,128)S(1)} %add.21), channel_id=1, source_target_pairs={{0,5},{1,4},{2,7},{3,6},{4,1},{5,0},{6,3},{7,2},{8,13},{9,12},{10,... | collective-permute-start | bytes 49160 | tf_op jit(solution)/shard_map/ppermute | solution.py:30
  13.1 0.2 collective-permute-start.3
  13.3 1.1 %collective-permute-done.5 = f32[32,128]{1,0:T(8,128)S(1)} collective-permute-done((f32[32,128]{1,0:T(8,128)S(1)}, f32[32,128]{1,0:T(8,128)S(1)}, u32[]{:S(2)}, u32[]{:S(2)}) %collective-permute-start.5) | collective-permute-done | bytes 16416 | tf_op jit(solution)/shard_map/ppermute | solution.py:30
  14.4 1.6 %collective-permute-done.4 = f32[32,128]{1,0:T(8,128)S(1)} collective-permute-done((f32[32,128]{1,0:T(8,128)S(1)}, f32[32,128]{1,0:T(8,128)S(1)}, u32[]{:S(2)}, u32[]{:S(2)}) %collective-permute-start.4) | collective-permute-done | bytes 16416 | tf_op jit(solution)/shard_map/ppermute | solution.py:30
  16.0 0.3 %collective-permute-done.3 = f32[32,128]{1,0:T(8,128)S(1)} collective-permute-done((f32[32,128]{1,0:T(8,128)S(1)}, f32[32,128]{1,0:T(8,128)S(1)}, u32[]{:S(2)}, u32[]{:S(2)}) %collective-permute-start.3) | collective-permute-done | bytes 16416 | tf_op jit(solution)/shard_map/ppermute | solution.py:30
  16.2 1.5 %collective-permute-start.6 = (f32[32,128]{1,0:T(8,128)S(1)}, f32[32,128]{1,0:T(8,128)S(1)}, u32[]{:S(2)}, u32[]{:S(2)}) collective-permute-start(f32[32,128]{1,0:T(8,128)S(1)} %add_add_fusion), channel_id=1, source_target_pairs={{0,9},{1,8},{2,11},{3,10},{4,13},{5,12},{6,15},{7,14},{8,1},{9,0},... | collective-permute-start | bytes 49160 | tf_op jit(solution)/shard_map/ppermute | solution.py:30
  17.8 0.0 copy-done.1
  17.8 0.1 copy.6.scale
  17.9 1.5 %collective-permute-done.6 = f32[32,128]{1,0:T(8,128)S(1)} collective-permute-done((f32[32,128]{1,0:T(8,128)S(1)}, f32[32,128]{1,0:T(8,128)S(1)}, u32[]{:S(2)}, u32[]{:S(2)}) %collective-permute-start.6) | collective-permute-done | bytes 16416 | tf_op jit(solution)/shard_map/ppermute | solution.py:30
  19.4 3.2 %factor_apply.1 = (f32[80,48,128]{2,1,0:T(8,128)}, f32[80,80]{1,0:T(8,128)}) custom-call(f32[32,128]{1,0:T(8,128)S(1)} %add.25.packed, f32[80,1]{1,0:T(8,128)S(1)} %copy.6.scale, bf16[128,6144]{1,0:T(8,128)(2,1)S(1)} %get-tuple-element.8.modes_panel, bf16[32,6144]{1,0:T(8,128)(2,1)S(1)} %get-tuple-element.11.snaps_panel), custom_call_target="tpu_custom_call" | custom-call | tf_op jit(solution)/shard_map/factor_apply/pallas_call | solution.py:311
  (5 shorter events, 0.0 us)
Async XLA Ops:
  0.6 2.7 %copy-start = (f32[16,4,1536]{2,1,0:T(4,128)S(1)}, f32[16,4,1536]{2,1,0:T(4,128)}, u32[]{:S(2)}) copy-start(f32[16,4,1536]{2,1,0:T(4,128)} %param.5) | copy-start | bytes 1179652
  0.6 2.7 %collective-permute-start = (f32[768,128]{1,0:T(8,128)}, f32[768,128]{1,0:T(8,128)S(1)}, u32[]{:S(2)}, u32[]{:S(2)}) collective-permute-start(f32[768,128]{1,0:T(8,128)} %bitcast.17), channel_id=1, source_target_pairs={{0,1},{1,0},{2,3},{3,2},{4,5},{5,4},{6,7},{7,6},{8,9},{9,8},{10,11... | collective-permute-start | bytes 1179656 | tf_op jit(solution)/shard_map/ppermute | solution.py:281
  3.3 14.5 %copy-start.1 = (f32[64]{0:T(128)S(1)}, f32[64]{0:T(128)}, u32[]{:S(2)}) copy-start(f32[64]{0:T(128)} %param.4) | copy-start | bytes 772
  4.0 1.2 %collective-permute-start.1 = (f32[32,128]{1,0:T(8,128)S(1)}, f32[32,128]{1,0:T(8,128)S(1)}, u32[]{:S(2)}, u32[]{:S(2)}) collective-permute-start(f32[32,128]{1,0:T(8,128)S(1)} %get-tuple-element.10), channel_id=1, source_target_pairs={{0,1},{1,0},{2,3},{3,2},{4,5},{5,4},{6,7},{7,6},{8,9},{9,8},{10,11... | collective-permute-start | bytes 49160 | tf_op jit(solution)/shard_map/ppermute | solution.py:30
  5.2 5.1 %collective-permute-start.2 = (f32[32,128]{1,0:T(8,128)S(1)}, f32[32,128]{1,0:T(8,128)S(1)}, u32[]{:S(2)}, u32[]{:S(2)}) collective-permute-start(f32[32,128]{1,0:T(8,128)S(1)} %add.20), channel_id=1, source_target_pairs={{0,17},{1,16},{2,19},{3,18},{4,21},{5,20},{6,23},{7,22},{8,25},{9,... | collective-permute-start | bytes 49160 | tf_op jit(solution)/shard_map/ppermute | solution.py:30
  10.3 4.1 %collective-permute-start.5 = (f32[32,128]{1,0:T(8,128)S(1)}, f32[32,128]{1,0:T(8,128)S(1)}, u32[]{:S(2)}, u32[]{:S(2)}) collective-permute-start(f32[32,128]{1,0:T(8,128)S(1)} %add.21), channel_id=1, source_target_pairs={{0,7},{1,6},{2,5},{3,4},{4,3},{5,2},{6,1},{7,0},{8,15},{9,14},{10,... | collective-permute-start | bytes 49160 | tf_op jit(solution)/shard_map/ppermute | solution.py:30
  12.8 3.2 %collective-permute-start.4 = (f32[32,128]{1,0:T(8,128)S(1)}, f32[32,128]{1,0:T(8,128)S(1)}, u32[]{:S(2)}, u32[]{:S(2)}) collective-permute-start(f32[32,128]{1,0:T(8,128)S(1)} %add.21), channel_id=1, source_target_pairs={{0,5},{1,4},{2,7},{3,6},{4,1},{5,0},{6,3},{7,2},{8,13},{9,12},{10,... | collective-permute-start | bytes 49160 | tf_op jit(solution)/shard_map/ppermute | solution.py:30
  13.1 3.2 %collective-permute-start.3 = (f32[32,128]{1,0:T(8,128)S(1)}, f32[32,128]{1,0:T(8,128)S(1)}, u32[]{:S(2)}, u32[]{:S(2)}) collective-permute-start(f32[32,128]{1,0:T(8,128)S(1)} %add.21), channel_id=1, source_target_pairs={{0,3},{1,2},{2,1},{3,0},{4,7},{5,6},{6,5},{7,4},{8,11},{9,10},{10,... | collective-permute-start | bytes 49160 | tf_op jit(solution)/shard_map/ppermute | solution.py:30
  16.2 3.2 %collective-permute-start.6 = (f32[32,128]{1,0:T(8,128)S(1)}, f32[32,128]{1,0:T(8,128)S(1)}, u32[]{:S(2)}, u32[]{:S(2)}) collective-permute-start(f32[32,128]{1,0:T(8,128)S(1)} %add_add_fusion), channel_id=1, source_target_pairs={{0,9},{1,8},{2,11},{3,10},{4,13},{5,12},{6,15},{7,14},{8,1},{9,0},... | collective-permute-start | bytes 49160 | tf_op jit(solution)/shard_map/ppermute | solution.py:30
